TPU v7x, 32 devices: a whole 2x2x4 slice. The times are simulated.
32 devices in a mesh: ga: 8 (over z, x), band: 4 (over y, core).
Axes of the slice: x: 2, y: 2, z: 4, core: 2. Of those that a mesh axis runs over, the one named last changes fastest.
Arguments:
- waves: float32 [2, 8192, 1024], P(None, 'ga', 'band'), may hold values from -6 to 6
- miller: int32 [3, 8192], P(None, 'ga'), may hold values from -8 to 8
- positions: float32 [64, 3], replicated, may hold values from 0 to 1
- form_factors: float32 [4, 18, 8192], P(None, None, 'ga'), may hold values from -0.0625 to 0.0625
- coupling: float32 [4, 18, 18], replicated, may hold values from -1.6970563 to 5.656854
- species: int32 [64], replicated, may hold values from 0 to 3
- block_sizes: int32 [64], replicated, may hold values from 1 to 18, 512 in all
- occupation: float32 [1024], P('band'), may hold values from 0.05 to 2
Outputs:
- residual: float32 [2, 8192, 1024], P(None, 'ga', 'band')
- estimate: float32 [1024], P('band')
- energy: float32 [], replicated
All inputs are finite; a program needn't handle non-finite values.
Results may differ from a plain program's by a relative error of at most 0.00007.
Values sent between devices are 32-bit elements; how exact they have to be, the bound alone decides.
No kernel may reach another device: no remote copies, remote signals or barrier semaphores. Data moves between devices by JAX's collectives and lax.ppermute only.
A program may use at most 64 MiB of HBM per device.

v0:
```python
import functools
import math

import jax
import jax.numpy as jnp
from jax import lax
from jax.experimental import pallas as pl
from jax.experimental.pallas import tpu as pltpu
from jax.sharding import PartitionSpec as P

PROJ = 512
KINETIC_SCALE = 0.005
EPSILON = 1e-06
LANES = 128
F32 = jnp.float32
BF16 = jnp.bfloat16


def iota(shape, dim):
    return lax.broadcasted_iota(jnp.int32, shape, dim)


def split(x):
    hi = x.astype(BF16)
    return hi, (x - hi.astype(F32)).astype(BF16)


def dot(a, b, contract=((1,), (0,))):
    return lax.dot_general(a, b, (contract, ((), ())), preferred_element_type=F32)


def pick(mask, values, axis):
    return jnp.sum(jnp.where(mask, values, 0.0), axis=axis, keepdims=True)


def depth_of(kmax, nspec):
    return -(-kmax * nspec // 16) * 16


def columns_of(sizes, species):
    atoms = sizes.shape[1]
    here, there = iota((atoms, atoms), 0), iota((atoms, atoms), 1)
    start = pick(there < here, sizes, 1)
    size = pick(there == here, sizes, 1)
    spec = pick(there == here, species, 1)
    return start, size, spec


def rows_by_projector(sizes, species, nspec):
    atoms = sizes.shape[1]
    _, size, spec = columns_of(sizes, species)
    atom = lax.rem(iota((atoms, 2 * atoms), 1), atoms)
    here = iota((atoms, 2 * atoms), 0)
    start = pick(here < atom, size, 0)
    end = start + pick(here == atom, size, 0)
    spec = pick(here == atom, spec, 0)
    place = iota((PROJ, 2 * atoms), 0).astype(F32)
    hot = (place >= start) & (place < end)
    lane = iota((PROJ, 2 * atoms), 1)
    first = hot & (lane < atoms)
    row = pick(first, spec - nspec * start, 1) + nspec * iota((PROJ, 1), 0).astype(F32)
    owner = pick(first, lane.astype(F32), 1)
    return row, jnp.where(hot, 1.0, 0.0).astype(BF16), owner


def rows_by_lane(sizes, species, nspec):
    atoms = sizes.shape[1]
    start, size, spec = columns_of(sizes, species)
    place = iota((atoms, PROJ), 1).astype(F32)
    hot = (place >= start) & (place < start + size)
    lane = iota((1, PROJ), 1).astype(F32)
    channel = lane - pick(hot, start, 0)
    row = nspec * channel + pick(hot, spec, 0)
    owner = pick(hot, iota((atoms, PROJ), 0).astype(F32), 0)
    ones = jnp.where(hot, 1.0, 0.0)
    return row, jnp.concatenate([ones, ones], axis=0).astype(BF16), owner, channel


def column(rows, n):
    size = rows.shape[1]
    return pick(iota((size, size), 0) == iota((size, size), 1), rows[n : n + 1], 1)


def trig(positions, miller):
    cycles = (
        column(positions, 0) * miller[0:1] + column(positions, 1) * miller[1:2] + column(positions, 2) * miller[2:3]
    )
    half = (cycles - jnp.round(cycles)) * math.pi
    sq = half * half
    sine = 1.0 / 6227020800.0
    for n in (39916800.0, 362880.0, 5040.0, 120.0, 6.0, 1.0):
        sine = 1.0 / n - sq * sine
    sine = half * sine
    cosine = 1.0 / 479001600.0
    for n in (3628800.0, 40320.0, 720.0, 24.0, 2.0, 1.0):
        cosine = 1.0 / n - sq * cosine
    return 1.0 - 2.0 * sine * sine, 2.0 * sine * cosine


def stacked(x):
    hi, lo = split(x)
    return jnp.concatenate([hi, lo], axis=0)


def fill_rows(scratch, table):
    kmax, nspec, width = table.shape
    scratch[...] = jnp.zeros(scratch.shape, F32)
    for k in range(kmax):
        scratch[k * nspec : (k + 1) * nspec, 0:width] = table[k]


def hot_rows(row, depth):
    j = lax.rem(iota((PROJ, 2 * depth), 1), depth).astype(F32)
    return jnp.where(row == j, 1.0, 0.0).astype(BF16)


def hot_rows_t(row, depth):
    j = lax.rem(iota((2 * depth, PROJ), 0), depth).astype(F32)
    return jnp.where(row == j, 1.0, 0.0).astype(BF16)


def squares(miller):
    total = miller[0:1] * miller[0:1] + miller[1:2] * miller[1:2] + miller[2:3] * miller[2:3]
    return total


def bit(device, b):
    return lax.rem(lax.shift_right_logical(device, b), 2)


def block_row(device, order, rel, rows):
    index = 2 * lax.bitwise_xor(bit(device, order[0]), rel[0]) + lax.bitwise_xor(bit(device, order[1]), rel[1])
    return pl.multiple_of(index * rows, rows)


def project_half(order, re, im, miller, hi_ref, lo_ref, outs, rhs_hi, rhs_lo, full):
    planes, half = re.shape
    rows = PROJ // 4
    device = lax.axis_index("ga")
    weight = jnp.where(iota((8, planes), 0) == 0, squares(miller), 1.0).astype(BF16)
    scale = jnp.where(iota((8, half), 0) == 0, 0.5 * KINETIC_SCALE, 1.0)
    dens_hi, dens_lo = split(re * re + im * im)
    sums = scale * (dot(weight, dens_hi) + dot(weight, dens_lo))
    re_hi, re_lo = split(re)
    im_hi, im_lo = split(im)
    for ref, a, b in ((rhs_hi, re_hi, im_hi), (rhs_lo, re_lo, im_lo)):
        ref[0:planes, 0:half] = a
        ref[0:planes, half:] = b
        ref[planes:, 0:half] = b
        ref[planes:, half:] = -a
    full[...] = dot(hi_ref[...], rhs_hi[...]) + dot(hi_ref[...], rhs_lo[...]) + dot(lo_ref[...], rhs_hi[...])
    tail = jnp.concatenate([sums, jnp.zeros_like(sums)], axis=1)
    for first, out in ((1, outs[0]), (0, outs[1])):
        for second in (0, 1):
            out[second * rows : (second + 1) * rows] = full[pl.ds(block_row(device, order, (first, second), rows), rows)]
        out[2 * rows :] = tail


def project_first(order, waves_in, miller_in, positions_in, form_in, species_in, sizes_in, *refs):
    outs, (hi_ref, lo_ref) = refs[:2], refs[2:4]
    waves, miller, positions, form, species, sizes, table, rhs_hi, rhs_lo, full, sems = refs[4:]
    planes = miller.shape[1]
    half = waves.shape[2]
    pairs = (
        (sizes_in, sizes),
        (species_in, species),
        (miller_in, miller),
        (positions_in, positions),
        (form_in, form),
        (waves_in.at[:, :, pl.ds(0, half)], waves),
    )
    copies = [pltpu.make_async_copy(a, b, sems.at[n]) for n, (a, b) in enumerate(pairs)]
    for copy in copies:
        copy.start()
    for copy in copies[:5]:
        copy.wait()
    fill_rows(table, form)
    depth = table.shape[0]
    m = miller[...].astype(F32)
    cosine, sine = trig(positions[...], m)
    cosine, sine = stacked(cosine), stacked(sine)
    radial = stacked(table[...])
    row, owners, _ = rows_by_projector(sizes[...].astype(F32), species[...].astype(F32), form.shape[1])
    picks = hot_rows(row, depth)
    rows = PROJ // 4
    for r in range(4):
        part = slice(r * rows, (r + 1) * rows)
        size = dot(picks[part], radial)
        hi, lo = split(size * dot(owners[part], cosine))
        hi_ref[part, 0:planes] = hi
        lo_ref[part, 0:planes] = lo
        hi, lo = split(-(size * dot(owners[part], sine)))
        hi_ref[part, planes : 2 * planes] = hi
        lo_ref[part, planes : 2 * planes] = lo
    copies[5].wait()
    project_half(order, waves[0], waves[1], m, hi_ref, lo_ref, outs, rhs_hi, rhs_lo, full)


def project_second(order, waves, miller, hi_ref, lo_ref, *refs):
    outs, (rhs_hi, rhs_lo, full) = refs[:2], refs[2:]
    half = waves.shape[2] // 2
    re, im = waves[0, :, half:], waves[1, :, half:]
    project_half(order, re, im, miller[...].astype(F32), hi_ref, lo_ref, outs, rhs_hi, rhs_lo, full)


def apply_tables_kernel(miller, positions, form, coupling, species, sizes, hi_ref, lo_ref, dense_hi, dense_lo, table, ctable):
    planes = miller.shape[1]
    nspec = form.shape[1]
    fill_rows(table, form)
    fill_rows(ctable, coupling)
    depth = table.shape[0]
    m = miller[...].astype(F32)
    cosine, sine = trig(positions[...], m)
    cosine, sine = stacked(cosine), stacked(sine)
    radial = stacked(table[...])
    lengths, kinds = sizes[...].astype(F32), species[...].astype(F32)
    row, owners, owner_row, channel = rows_by_lane(lengths, kinds, nspec)
    picks = hot_rows_t(row, depth)
    step = planes // 4
    over = ((0,), (0,))
    for r in range(4):
        part = slice(r * step, (r + 1) * step)
        size = dot(radial[:, part], picks, over)
        hi, lo = split(size * dot(cosine[:, part], owners, over))
        hi_ref[part, 0:PROJ] = hi
        lo_ref[part, 0:PROJ] = lo
        hi, lo = split(-(size * dot(sine[:, part], owners, over)))
        hi_ref[part, PROJ : 2 * PROJ] = hi
        lo_ref[part, PROJ : 2 * PROJ] = lo
    row, _, owner_col = rows_by_projector(lengths, kinds, nspec)
    lines = dot(hot_rows(row, depth), stacked(ctable[...]))
    lines_hi, lines_lo = split(lines)
    spread = jnp.where(iota((ctable.shape[1], PROJ), 0).astype(F32) == channel, 1.0, 0.0).astype(BF16)
    dense = dot(lines_hi, spread) + dot(lines_lo, spread)
    hi, lo = split(jnp.where(owner_col == owner_row, dense, 0.0))
    dense_hi[...] = hi
    dense_lo[...] = lo


def stats_kernel(order, own, near, far, sums, occupation, dense_hi, dense_lo, *refs):
    share_in, levels_in = refs[:-5] or (None, None)
    rhs_hi, rhs_lo, level_out, share_out, full = refs[-5:]
    rows = PROJ // 4
    half = occupation.shape[1]
    device = lax.axis_index("ga")
    for rel, ref, at in (((0, 0), own, 0), ((0, 1), near, 0), ((1, 0), far, 0), ((1, 1), far, rows)):
        full[pl.ds(block_row(device, order, rel, rows), rows)] = ref[at : at + rows]
    proj = full[...]
    p_hi, p_lo = split(proj)
    mixed = dot(dense_hi[...], p_hi) + dot(dense_hi[...], p_lo) + dot(dense_lo[...], p_hi)
    pairs = jnp.sum(proj * mixed, axis=0, keepdims=True)
    nonlocal_sum = pairs[:, 0:half] + pairs[:, half:]
    kin, norm = sums[0:1, 0:half], sums[1:2, 0:half]
    level = (kin + nonlocal_sum) / (norm + EPSILON)
    share = jnp.sum(occupation[...] * (nonlocal_sum / (norm + EPSILON)), axis=1, keepdims=True)
    if share_in is None:
        level_out[...] = level
        share_out[...] = share
    else:
        level_out[0:1] = levels_in[...]
        level_out[1:2] = level
        share_out[...] = share_in[...] + share
    m_hi, m_lo = split(mixed)
    for ref, m in ((rhs_hi, m_hi), (rhs_lo, m_lo)):
        ref[0:PROJ] = m
        ref[PROJ:, 0:half] = -m[:, half:]
        ref[PROJ:, half:] = m[:, 0:half]


def apply_kernel(q, rhs_hi, rhs_lo, levels, waves, miller, hi_ref, lo_ref, *refs):
    residual, staged, sem = refs[-3:]
    planes = miller.shape[1]
    half = staged.shape[2]
    bands = slice(q * half, (q + 1) * half)
    level = levels[q : q + 1]
    unit = jnp.where(iota((8, half), 0) == 0, 1.0, 0.0).astype(BF16)
    applied = dot(hi_ref[...], rhs_hi[...]) + dot(hi_ref[...], rhs_lo[...]) + dot(lo_ref[...], rhs_hi[...])
    line = jnp.broadcast_to(squares(miller[...].astype(F32)), (8, planes)).astype(BF16)
    shifted = (0.5 * KINETIC_SCALE) * dot(line, unit, ((0,), (0,))) - level
    staged[0] = shifted * waves[0, :, bands] + applied[:, 0:half]
    staged[1] = shifted * waves[1, :, bands] + applied[:, half:]
    copy = pltpu.make_async_copy(staged, residual.at[:, :, pl.ds(q * half, half)], sem)
    copy.start()
    copy.wait()


def swap(x, axis, size, mask):
    return lax.ppermute(x, axis, [(i, i ^ mask) for i in range(size)])


def tree(parts):
    while len(parts) > 1:
        parts = [a + b for a, b in zip(parts[::2], parts[1::2])]
    return parts[0]


def on_device(ga, band, waves, miller, positions, form_factors, coupling, species, block_sizes, occupation):
    _, planes, bands = waves.shape
    half = bands // 2
    nspec, kmax, _ = form_factors.shape
    atoms = species.shape[0]
    rows = PROJ // 4
    depth = depth_of(kmax, nspec)
    positions = positions.T
    form = form_factors.transpose(1, 0, 2)
    coupling = coupling.transpose(1, 0, 2)
    species = species.reshape(1, -1)
    sizes = block_sizes.reshape(1, -1)
    bits = ga.bit_length() - 1
    orders = ((0, 1), (1, 0))
    params = pltpu.CompilerParams(vmem_limit_bytes=32 * 1024 * 1024)
    hbm = pl.BlockSpec(memory_space=pltpu.HBM)
    vmem = pl.BlockSpec(memory_space=pltpu.VMEM)
    shape = jax.ShapeDtypeStruct
    pieces = [shape((2 * rows + 8, bands), F32)] * 2
    beta = [shape((PROJ, 2 * planes), BF16)] * 2
    work = [
        pltpu.VMEM((2 * planes, bands), BF16),
        pltpu.VMEM((2 * planes, bands), BF16),
        pltpu.VMEM((PROJ, bands), F32),
    ]
    out = pl.pallas_call(
        functools.partial(project_first, orders[0]),
        name="project_first",
        in_specs=[hbm] * 6,
        out_shape=pieces + beta,
        scratch_shapes=[
            pltpu.VMEM((2, planes, half), F32),
            pltpu.VMEM(miller.shape, jnp.int32),
            pltpu.VMEM(positions.shape, F32),
            pltpu.VMEM(form.shape, F32),
            pltpu.VMEM((1, atoms), jnp.int32),
            pltpu.VMEM((1, atoms), jnp.int32),
            pltpu.VMEM((depth, planes), F32),
            *work,
            pltpu.SemaphoreType.DMA((6,)),
        ],
        compiler_params=params,
    )(*(pltpu.with_memory_space_constraint(x, pltpu.HBM) for x in (waves, miller, positions, form, species, sizes)))
    parts = [out[:2]]
    parts.append(
        pl.pallas_call(
            functools.partial(project_second, orders[1]),
            name="project_second",
            out_shape=pieces,
            scratch_shapes=work,
            compiler_params=params,
        )(waves, miller, out[2], out[3])
    )
    tables = pl.pallas_call(
        apply_tables_kernel,
        name="apply_tables",
        out_shape=[shape((planes, 2 * PROJ), BF16)] * 2 + [shape((PROJ, PROJ), BF16)] * 2,
        scratch_shapes=[pltpu.VMEM((depth, planes), F32), pltpu.VMEM((depth, LANES), F32)],
        compiler_params=params,
    )(miller, positions, form, coupling, species, sizes)
    kept, mine, own, near, far = {}, {}, {}, {}, {}
    for q, order in enumerate(orders):
        kept[q] = parts[q][1] + swap(parts[q][0], "ga", ga, 1 << order[0])
    for q, order in enumerate(orders):
        k = kept[q]
        got = swap(k[rows:], "ga", ga, 1 << order[1])
        mine[q] = jnp.concatenate([k[:rows] + got[:rows], k[2 * rows :] + got[rows:]], axis=0)
    for b in range(2, bits):
        for q in range(2):
            mine[q] = mine[q] + swap(mine[q], "ga", ga, 1 << b)
    for q, order in enumerate(orders):
        own[q] = mine[q][:rows]
        near[q] = swap(own[q], "ga", ga, 1 << order[1])
    for q, order in enumerate(orders):
        far[q] = swap(jnp.concatenate([own[q], near[q]], axis=0), "ga", ga, 1 << order[0])
    occ = occupation.reshape(2, half)
    residual = levels = share = None
    for q in range(2):
        operands = [own[q], near[q], far[q], mine[q][rows:], occ[q : q + 1], tables[2], tables[3]]
        if q == 1:
            operands += [share, levels]
        rhs_hi, rhs_lo, levels, share = pl.pallas_call(
            functools.partial(stats_kernel, orders[q]),
            out_shape=[
                shape((2 * PROJ, bands), BF16),
                shape((2 * PROJ, bands), BF16),
                shape((q + 1, half), F32),
                shape((1, 1), F32),
            ],
            scratch_shapes=[pltpu.VMEM((PROJ, bands), F32)],
            compiler_params=params,
        )(*operands)
        if q == 1:
            energy = tree([share] + [swap(share, "band", band, d) for d in range(1, band)])
        operands = [rhs_hi, rhs_lo, levels, waves, miller, tables[0], tables[1]]
        specs = [vmem] * len(operands)
        alias = {}
        if q == 1:
            alias = {len(operands): 0}
            operands.append(residual)
            specs.append(hbm)
        residual = pl.pallas_call(
            functools.partial(apply_kernel, q),
            in_specs=specs,
            out_specs=hbm,
            out_shape=shape(waves.shape, F32),
            scratch_shapes=[pltpu.VMEM((2, planes, half), F32), pltpu.SemaphoreType.DMA],
            input_output_aliases=alias,
            compiler_params=params,
        )(*operands)
    return residual, levels.reshape(bands), energy.reshape(())


def solution(mesh):
    in_specs = (
        P(None, "ga", "band"),
        P(None, "ga"),
        P(),
        P(None, None, "ga"),
        P(),
        P(),
        P(),
        P("band"),
    )
    out_specs = (P(None, "ga", "band"), P("band"), P())

    def body(*args):
        return on_device(mesh.shape["ga"], mesh.shape["band"], *args)

    return jax.shard_map(body, mesh=mesh, in_specs=in_specs, out_specs=out_specs, check_vma=False)
```

profile of v0, /device:TPU:0, one launch (start us, length us, event | category | flops | bytes accessed | tf_op | source)
XLA Modules:
  0.0 62.6 jit_solution(6921415550132204286)
XLA Ops:
  0.6 0.0 copy-start.2
  0.6 0.0 copy-start
  0.6 5.1 %project_first.1 = (f32[264,256]{1,0:T(8,128)S(1)}, f32[264,256]{1,0:T(8,128)S(1)}, bf16[512,2048]{1,0:T(8,128)(2,1)S(1)}, bf16[512,2048]{1,0:T(8,128)(2,1)S(1)}) custom-call(f32[2,1024,256]{2,1,0:T(8,128)} %waves.5, s32[3,1024]{1,0:T(4,128)} %miller.7, f32[3,64]{1,0:T(4,128)} %bitcast.14, f32[18,4,1024]{2,1,0:T(4,128)} %bitcast.11, s32[1,64]{1,0:T(1,128)} %bitcast.16, ...), custom_call_target="tpu_custom_call" | custom-call | tf_op jit(solution)/shard_map/project_first/pallas_call | solution.py:322
  5.8 3.0 %collective-permute-start.5 = (f32[264,256]{1,0:T(8,128)S(1)}, f32[264,256]{1,0:T(8,128)S(1)}, u32[]{:S(2)}, u32[]{:S(2)}) collective-permute-start(f32[264,256]{1,0:T(8,128)S(1)} %get-tuple-element.28), channel_id=1, source_target_pairs={{0,4},{4,0},{8,12},{12,8},{16,20},{20,16},{24,28},{28,24},{1,5},{5... | collective-permute-start | bytes 811016 | tf_op jit(solution)/shard_map/ppermute | solution.py:288
  8.8 0.0 copy-done.2
  8.8 0.0 copy-done
  8.8 2.2 %project_second.1 = (f32[264,256]{1,0:T(8,128)S(1)}, f32[264,256]{1,0:T(8,128)S(1)}) custom-call(f32[2,1024,256]{2,1,0:T(8,128)S(1)} %copy-done, s32[3,1024]{1,0:T(4,128)S(1)} %copy-done.2, bf16[512,2048]{1,0:T(8,128)(2,1)S(1)} %get-tuple-element.21.hi_ref, bf16[512,2048]{1,0:T(8,128)(2,1)S(1)} %get-tuple-element.22.lo_ref), custom_call_target="tpu_custom_call" | custom-call | tf_op jit(solution)/shard_map/project_second/pallas_call | solution.py:342
  11.1 1.7 %collective-permute-start = (f32[264,256]{1,0:T(8,128)S(1)}, f32[264,256]{1,0:T(8,128)S(1)}, u32[]{:S(2)}, u32[]{:S(2)}) collective-permute-start(f32[264,256]{1,0:T(8,128)S(1)} %get-tuple-element.24), channel_id=1, source_target_pairs={{0,8},{4,12},{8,0},{12,4},{16,24},{20,28},{24,16},{28,20},{1,9},{5... | collective-permute-start | bytes 811016 | tf_op jit(solution)/shard_map/ppermute | solution.py:288
  12.7 2.6 %collective-permute-done.5 = f32[264,256]{1,0:T(8,128)S(1)} collective-permute-done((f32[264,256]{1,0:T(8,128)S(1)}, f32[264,256]{1,0:T(8,128)S(1)}, u32[]{:S(2)}, u32[]{:S(2)}) %collective-permute-start.5) | collective-permute-done | bytes 270368 | tf_op jit(solution)/shard_map/ppermute | solution.py:288
  15.4 1.9 %collective-permute-start.6 = (f32[136,256]{1,0:T(8,128)S(1)}, f32[136,256]{1,0:T(8,128)S(1)}, u32[]{:S(2)}, u32[]{:S(2)}) collective-permute-start(f32[136,256]{1,0:T(8,128)S(1)} %slice.80), channel_id=1, source_target_pairs={{0,8},{4,12},{8,0},{12,4},{16,24},{20,28},{24,16},{28,20},{1,9},{5... | collective-permute-start | bytes 417800 | tf_op jit(solution)/shard_map/ppermute | solution.py:288
  17.3 3.2 %collective-permute-done = f32[264,256]{1,0:T(8,128)S(1)} collective-permute-done((f32[264,256]{1,0:T(8,128)S(1)}, f32[264,256]{1,0:T(8,128)S(1)}, u32[]{:S(2)}, u32[]{:S(2)}) %collective-permute-start) | collective-permute-done | bytes 270368 | tf_op jit(solution)/shard_map/ppermute | solution.py:288
  20.5 0.0 copy-start.1
  20.5 0.0 copy-start.3
  20.5 0.0 copy-start.4
  20.6 0.0 copy-start.5
  20.6 0.0 copy-start.6
  20.6 0.0 copy-start.8
  20.6 0.1 collective-permute-start.1
  20.7 1.4 %collective-permute-done.6 = f32[136,256]{1,0:T(8,128)S(1)} collective-permute-done((f32[136,256]{1,0:T(8,128)S(1)}, f32[136,256]{1,0:T(8,128)S(1)}, u32[]{:S(2)}, u32[]{:S(2)}) %collective-permute-start.6) | collective-permute-done | bytes 139296 | tf_op jit(solution)/shard_map/ppermute | solution.py:288
  22.1 2.6 %collective-permute-start.7 = (f32[136,256]{1,0:T(8,128)S(1)}, f32[136,256]{1,0:T(8,128)S(1)}, u32[]{:S(2)}, u32[]{:S(2)}) collective-permute-start(f32[136,256]{1,0:T(8,128)S(1)} %pad_maximum_fusion.3), channel_id=1, source_target_pairs={{0,16},{4,20},{8,24},{12,28},{16,0},{20,4},{24,8},{28,12},{1,17},{... | collective-permute-start | bytes 417800 | tf_op jit(solution)/shard_map/ppermute | solution.py:288
  24.8 1.0 %collective-permute-done.1 = f32[136,256]{1,0:T(8,128)S(1)} collective-permute-done((f32[136,256]{1,0:T(8,128)S(1)}, f32[136,256]{1,0:T(8,128)S(1)}, u32[]{:S(2)}, u32[]{:S(2)}) %collective-permute-start.1) | collective-permute-done | bytes 139296 | tf_op jit(solution)/shard_map/ppermute | solution.py:288
  25.8 2.7 %collective-permute-start.2 = (f32[136,256]{1,0:T(8,128)S(1)}, f32[136,256]{1,0:T(8,128)S(1)}, u32[]{:S(2)}, u32[]{:S(2)}) collective-permute-start(f32[136,256]{1,0:T(8,128)S(1)} %pad_maximum_fusion.2), channel_id=1, source_target_pairs={{0,16},{4,20},{8,24},{12,28},{16,0},{20,4},{24,8},{28,12},{1,17},{... | collective-permute-start | bytes 417800 | tf_op jit(solution)/shard_map/ppermute | solution.py:288
  28.4 6.0 %collective-permute-done.7 = f32[136,256]{1,0:T(8,128)S(1)} collective-permute-done((f32[136,256]{1,0:T(8,128)S(1)}, f32[136,256]{1,0:T(8,128)S(1)}, u32[]{:S(2)}, u32[]{:S(2)}) %collective-permute-start.7) | collective-permute-done | bytes 139296 | tf_op jit(solution)/shard_map/ppermute | solution.py:288
  34.5 0.1 collective-permute-start.8
  34.6 1.9 %collective-permute-done.2 = f32[136,256]{1,0:T(8,128)S(1)} collective-permute-done((f32[136,256]{1,0:T(8,128)S(1)}, f32[136,256]{1,0:T(8,128)S(1)}, u32[]{:S(2)}, u32[]{:S(2)}) %collective-permute-start.2) | collective-permute-done | bytes 139296 | tf_op jit(solution)/shard_map/ppermute | solution.py:288
  36.4 0.8 %collective-permute-start.3 = (f32[128,256]{1,0:T(8,128)S(1)}, f32[128,256]{1,0:T(8,128)S(1)}, u32[]{:S(2)}, u32[]{:S(2)}) collective-permute-start(f32[128,256]{1,0:T(8,128)S(1)} %slice.77.own), channel_id=1, source_target_pairs={{0,4},{4,0},{8,12},{12,8},{16,20},{20,16},{24,28},{28,24},{1,5},{5... | collective-permute-start | bytes 393224 | tf_op jit(solution)/shard_map/ppermute | solution.py:288
  37.3 2.2 %collective-permute-done.8.near = f32[128,256]{1,0:T(8,128)S(1)} collective-permute-done((f32[128,256]{1,0:T(8,128)S(1)}, f32[128,256]{1,0:T(8,128)S(1)}, u32[]{:S(2)}, u32[]{:S(2)}) %collective-permute-start.8) | collective-permute-done | bytes 131104 | tf_op jit(solution)/shard_map/ppermute | solution.py:288
  39.5 0.9 %collective-permute-start.9 = (f32[256,256]{1,0:T(8,128)S(1)}, f32[256,256]{1,0:T(8,128)S(1)}, u32[]{:S(2)}, u32[]{:S(2)}) collective-permute-start(f32[256,256]{1,0:T(8,128)S(1)} %pad_maximum_fusion.1), channel_id=1, source_target_pairs={{0,4},{4,0},{8,12},{12,8},{16,20},{20,16},{24,28},{28,24},{1,5},{5... | collective-permute-start | bytes 786440 | tf_op jit(solution)/shard_map/ppermute | solution.py:288
  40.4 2.3 %collective-permute-done.3.near = f32[128,256]{1,0:T(8,128)S(1)} collective-permute-done((f32[128,256]{1,0:T(8,128)S(1)}, f32[128,256]{1,0:T(8,128)S(1)}, u32[]{:S(2)}, u32[]{:S(2)}) %collective-permute-start.3) | collective-permute-done | bytes 131104 | tf_op jit(solution)/shard_map/ppermute | solution.py:288
  42.8 0.8 %collective-permute-start.4 = (f32[256,256]{1,0:T(8,128)S(1)}, f32[256,256]{1,0:T(8,128)S(1)}, u32[]{:S(2)}, u32[]{:S(2)}) collective-permute-start(f32[256,256]{1,0:T(8,128)S(1)} %pad_maximum_fusion), channel_id=1, source_target_pairs={{0,8},{4,12},{8,0},{12,4},{16,24},{20,28},{24,16},{28,20},{1,9},{5... | collective-permute-start | bytes 786440 | tf_op jit(solution)/shard_map/ppermute | solution.py:288
  43.5 0.0 copy-done.1
  43.5 0.0 copy-done.3
  43.5 0.0 copy-done.4
  43.5 0.0 copy-done.5
  43.5 0.0 copy-done.6
  43.5 2.0 %apply_tables.1 = (bf16[1024,1024]{1,0:T(8,128)(2,1)S(1)}, bf16[1024,1024]{1,0:T(8,128)(2,1)S(1)}, bf16[512,512]{1,0:T(8,128)(2,1)S(1)}, bf16[512,512]{1,0:T(8,128)(2,1)S(1)}) custom-call(s32[3,1024]{1,0:T(4,128)S(1)} %copy-done.2, f32[3,64]{1,0:T(4,128)S(1)} %bitcast.15, f32[18,4,1024]{2,1,0:T(4,128)S(1)} %bitcast.12, f32[18,4,18]{2,1,0:T(4,128)S(1)} %bitcast.13, ...), custom_call_target="tpu_custom_call" | custom-call | tf_op jit(solution)/shard_map/apply_tables/pallas_call | solution.py:350
  45.6 0.0 copy-done.8
  45.6 1.5 %collective-permute-done.9.far = f32[256,256]{1,0:T(8,128)S(1)} collective-permute-done((f32[256,256]{1,0:T(8,128)S(1)}, f32[256,256]{1,0:T(8,128)S(1)}, u32[]{:S(2)}, u32[]{:S(2)}) %collective-permute-start.9) | collective-permute-done | bytes 262176 | tf_op jit(solution)/shard_map/ppermute | solution.py:288
  47.1 1.3 %shard_map.103 = (bf16[1024,256]{1,0:T(8,128)(2,1)S(1)}, bf16[1024,256]{1,0:T(8,128)(2,1)S(1)}, f32[1,128]{1,0:T(1,128)S(1)}, f32[1,1]{1,0:T(1,128)}) custom-call(f32[128,256]{1,0:T(8,128)S(1)} %slice.84.own, f32[128,256]{1,0:T(8,128)S(1)} %collective-permute-done.8.near, f32[256,256]{1,0:T(8,128)S(1)} %collective-permute-done.9.far, ...), custom_call_target="tpu_custom_call" | custom-call | tf_op jit(solution)/shard_map/pallas_call | solution.py:378
  48.4 0.9 %collective-permute-done.4.far = f32[256,256]{1,0:T(8,128)S(1)} collective-permute-done((f32[256,256]{1,0:T(8,128)S(1)}, f32[256,256]{1,0:T(8,128)S(1)}, u32[]{:S(2)}, u32[]{:S(2)}) %collective-permute-start.4) | collective-permute-done | bytes 262176 | tf_op jit(solution)/shard_map/ppermute | solution.py:288
  49.2 2.0 %shard_map.104 = (bf16[1024,256]{1,0:T(8,128)(2,1)S(1)}, bf16[1024,256]{1,0:T(8,128)(2,1)S(1)}, f32[2,128]{1,0:T(2,128)}, f32[1,1]{1,0:T(1,128)}) custom-call(f32[128,256]{1,0:T(8,128)S(1)} %slice.77.own, f32[128,256]{1,0:T(8,128)S(1)} %collective-permute-done.3.near, f32[256,256]{1,0:T(8,128)S(1)} %collective-permute-done.4.far, f32[8,256]{1,0:T(8,128)S(1)} %slice.78.sums, ...), custom_call_target="tpu_custom_call" | custom-call | tf_op jit(solution)/shard_map/pallas_call | solution.py:378
  51.2 0.0 collective-permute-start.12
  51.2 1.5 %collective-permute-start.11 = (f32[1,1]{1,0:T(1,128)}, f32[1,1]{1,0:T(1,128)}, u32[]{:S(2)}, u32[]{:S(2)}) collective-permute-start(f32[1,1]{1,0:T(1,128)} %get-tuple-element.38), channel_id=1, source_target_pairs={{0,2},{1,3},{2,0},{3,1},{4,6},{5,7},{6,4},{7,5},{8,10},{9,11},{10,... | collective-permute-start | bytes 20 | tf_op jit(solution)/shard_map/ppermute | solution.py:288
  52.7 0.3 collective-permute-start.10
  53.0 0.0 copy-start.7
  53.0 2.9 %shard_map.105.refs_0_ = f32[2,1024,256]{2,1,0:T(8,128)} custom-call(bf16[1024,256]{1,0:T(8,128)(2,1)S(1)} %get-tuple-element.36.rhs_hi, bf16[1024,256]{1,0:T(8,128)(2,1)S(1)} %get-tuple-element.37.rhs_lo, f32[1,128]{1,0:T(1,128)S(1)} %get-tuple-element.30.refs_1_.levels, f32[2,1024,256]{2,1,0:T(8,128)S(1)} %copy-done, s32[3,1024]{1,0:T(4,128)S(1)} %copy-done.2, ...), custom_call_target="tpu_custom_call" | custom-call | tf_op jit(solution)/shard_map/pallas_call | solution.py:398
  55.9 0.0 copy-done.7
  55.9 2.9 %shard_map.106 = f32[2,1024,256]{2,1,0:T(8,128)} custom-call(bf16[1024,256]{1,0:T(8,128)(2,1)S(1)} %get-tuple-element.31.rhs_hi, bf16[1024,256]{1,0:T(8,128)(2,1)S(1)} %get-tuple-element.32.rhs_lo, f32[2,128]{1,0:T(2,128)S(1)} %copy-done.7, f32[2,1024,256]{2,1,0:T(8,128)S(1)} %copy-done, s32[3,1024]{1,0:T(4,128)S(1)} %copy-done.2, ...), custom_call_target="tpu_custom_call", output_to_operand_aliasing={{}: (7, {})} | custom-call | tf_op jit(solution)/shard_map/pallas_call | solution.py:398
  58.8 0.0 collective-permute-done.10
  60.1 0.0 collective-permute-done.12
  60.2 0.0 collective-permute-done.11
  (19 shorter events, 0.3 us)
Async XLA Ops:
  0.6 8.2 %copy-start.2 = (s32[3,1024]{1,0:T(4,128)S(1)}, s32[3,1024]{1,0:T(4,128)}, u32[]{:S(2)}) copy-start(s32[3,1024]{1,0:T(4,128)} %miller.7) | copy-start | bytes 36868
  0.6 8.2 %copy-start = (f32[2,1024,256]{2,1,0:T(8,128)S(1)}, f32[2,1024,256]{2,1,0:T(8,128)}, u32[]{:S(2)}) copy-start(f32[2,1024,256]{2,1,0:T(8,128)} %waves.5) | copy-start | bytes 6291460
  5.8 9.5 %collective-permute-start.5 = (f32[264,256]{1,0:T(8,128)S(1)}, f32[264,256]{1,0:T(8,128)S(1)}, u32[]{:S(2)}, u32[]{:S(2)}) collective-permute-start(f32[264,256]{1,0:T(8,128)S(1)} %get-tuple-element.28), channel_id=1, source_target_pairs={{0,4},{4,0},{8,12},{12,8},{16,20},{20,16},{24,28},{28,24},{1,5},{5... | collective-permute-start | bytes 811016 | tf_op jit(solution)/shard_map/ppermute | solution.py:288
  11.1 9.4 %collective-permute-start = (f32[264,256]{1,0:T(8,128)S(1)}, f32[264,256]{1,0:T(8,128)S(1)}, u32[]{:S(2)}, u32[]{:S(2)}) collective-permute-start(f32[264,256]{1,0:T(8,128)S(1)} %get-tuple-element.24), channel_id=1, source_target_pairs={{0,8},{4,12},{8,0},{12,4},{16,24},{20,28},{24,16},{28,20},{1,9},{5... | collective-permute-start | bytes 811016 | tf_op jit(solution)/shard_map/ppermute | solution.py:288
  15.4 6.7 %collective-permute-start.6 = (f32[136,256]{1,0:T(8,128)S(1)}, f32[136,256]{1,0:T(8,128)S(1)}, u32[]{:S(2)}, u32[]{:S(2)}) collective-permute-start(f32[136,256]{1,0:T(8,128)S(1)} %slice.80), channel_id=1, source_target_pairs={{0,8},{4,12},{8,0},{12,4},{16,24},{20,28},{24,16},{28,20},{1,9},{5... | collective-permute-start | bytes 417800 | tf_op jit(solution)/shard_map/ppermute | solution.py:288
  20.5 23.0 %copy-start.1 = (f32[4,18,1024]{2,0,1:T(4,128)S(1)}, f32[4,18,1024]{2,0,1:T(4,128)}, u32[]{:S(2)}) copy-start(f32[4,18,1024]{2,0,1:T(4,128)} %param.11) | copy-start | bytes 884740
  20.5 23.0 %copy-start.3 = (f32[4,18,18]{2,0,1:T(4,128)S(1)}, f32[4,18,18]{2,0,1:T(4,128)}, u32[]{:S(2)}) copy-start(f32[4,18,18]{2,0,1:T(4,128)} %param.12) | copy-start | bytes 15556
  20.5 23.0 %copy-start.4 = (f32[64,3]{0,1:T(4,128)S(1)}, f32[64,3]{0,1:T(4,128)}, u32[]{:S(2)}) copy-start(f32[64,3]{0,1:T(4,128)} %param.10) | copy-start | bytes 2308
  20.6 23.0 %copy-start.5 = (s32[64]{0:T(128)S(1)}, s32[64]{0:T(128)}, u32[]{:S(2)}) copy-start(s32[64]{0:T(128)} %param.13) | copy-start | bytes 772
  20.6 23.0 %copy-start.6 = (s32[64]{0:T(128)S(1)}, s32[64]{0:T(128)}, u32[]{:S(2)}) copy-start(s32[64]{0:T(128)} %param.14) | copy-start | bytes 772
  20.6 25.0 %copy-start.8 = (f32[256]{0:T(256)S(1)}, f32[256]{0:T(256)}, u32[]{:S(2)}) copy-start(f32[256]{0:T(256)} %param.15) | copy-start | bytes 3076
  20.6 5.1 %collective-permute-start.1 = (f32[136,256]{1,0:T(8,128)S(1)}, f32[136,256]{1,0:T(8,128)S(1)}, u32[]{:S(2)}, u32[]{:S(2)}) collective-permute-start(f32[136,256]{1,0:T(8,128)S(1)} %slice.73), channel_id=1, source_target_pairs={{0,4},{4,0},{8,12},{12,8},{16,20},{20,16},{24,28},{28,24},{1,5},{5... | collective-permute-start | bytes 417800 | tf_op jit(solution)/shard_map/ppermute | solution.py:288
  22.1 12.3 %collective-permute-start.7 = (f32[136,256]{1,0:T(8,128)S(1)}, f32[136,256]{1,0:T(8,128)S(1)}, u32[]{:S(2)}, u32[]{:S(2)}) collective-permute-start(f32[136,256]{1,0:T(8,128)S(1)} %pad_maximum_fusion.3), channel_id=1, source_target_pairs={{0,16},{4,20},{8,24},{12,28},{16,0},{20,4},{24,8},{28,12},{1,17},{... | collective-permute-start | bytes 417800 | tf_op jit(solution)/shard_map/ppermute | solution.py:288
  25.8 10.6 %collective-permute-start.2 = (f32[136,256]{1,0:T(8,128)S(1)}, f32[136,256]{1,0:T(8,128)S(1)}, u32[]{:S(2)}, u32[]{:S(2)}) collective-permute-start(f32[136,256]{1,0:T(8,128)S(1)} %pad_maximum_fusion.2), channel_id=1, source_target_pairs={{0,16},{4,20},{8,24},{12,28},{16,0},{20,4},{24,8},{28,12},{1,17},{... | collective-permute-start | bytes 417800 | tf_op jit(solution)/shard_map/ppermute | solution.py:288
  34.5 5.0 %collective-permute-start.8 = (f32[128,256]{1,0:T(8,128)S(1)}, f32[128,256]{1,0:T(8,128)S(1)}, u32[]{:S(2)}, u32[]{:S(2)}) collective-permute-start(f32[128,256]{1,0:T(8,128)S(1)} %slice.84.own), channel_id=1, source_target_pairs={{0,8},{4,12},{8,0},{12,4},{16,24},{20,28},{24,16},{28,20},{1,9},{5... | collective-permute-start | bytes 393224 | tf_op jit(solution)/shard_map/ppermute | solution.py:288
  36.4 6.3 %collective-permute-start.3 = (f32[128,256]{1,0:T(8,128)S(1)}, f32[128,256]{1,0:T(8,128)S(1)}, u32[]{:S(2)}, u32[]{:S(2)}) collective-permute-start(f32[128,256]{1,0:T(8,128)S(1)} %slice.77.own), channel_id=1, source_target_pairs={{0,4},{4,0},{8,12},{12,8},{16,20},{20,16},{24,28},{28,24},{1,5},{5... | collective-permute-start | bytes 393224 | tf_op jit(solution)/shard_map/ppermute | solution.py:288
  39.5 7.6 %collective-permute-start.9 = (f32[256,256]{1,0:T(8,128)S(1)}, f32[256,256]{1,0:T(8,128)S(1)}, u32[]{:S(2)}, u32[]{:S(2)}) collective-permute-start(f32[256,256]{1,0:T(8,128)S(1)} %pad_maximum_fusion.1), channel_id=1, source_target_pairs={{0,4},{4,0},{8,12},{12,8},{16,20},{20,16},{24,28},{28,24},{1,5},{5... | collective-permute-start | bytes 786440 | tf_op jit(solution)/shard_map/ppermute | solution.py:288
  42.8 6.4 %collective-permute-start.4 = (f32[256,256]{1,0:T(8,128)S(1)}, f32[256,256]{1,0:T(8,128)S(1)}, u32[]{:S(2)}, u32[]{:S(2)}) collective-permute-start(f32[256,256]{1,0:T(8,128)S(1)} %pad_maximum_fusion), channel_id=1, source_target_pairs={{0,8},{4,12},{8,0},{12,4},{16,24},{20,28},{24,16},{28,20},{1,9},{5... | collective-permute-start | bytes 786440 | tf_op jit(solution)/shard_map/ppermute | solution.py:288
  51.2 9.0 %collective-permute-start.12 = (f32[1,1]{1,0:T(1,128)}, f32[1,1]{1,0:T(1,128)}, u32[]{:S(2)}, u32[]{:S(2)}) collective-permute-start(f32[1,1]{1,0:T(1,128)} %get-tuple-element.38), channel_id=1, source_target_pairs={{0,3},{1,2},{2,1},{3,0},{4,7},{5,6},{6,5},{7,4},{8,11},{9,10},{10,... | collective-permute-start | bytes 20 | tf_op jit(solution)/shard_map/ppermute | solution.py:288
  51.2 9.0 %collective-permute-start.11 = (f32[1,1]{1,0:T(1,128)}, f32[1,1]{1,0:T(1,128)}, u32[]{:S(2)}, u32[]{:S(2)}) collective-permute-start(f32[1,1]{1,0:T(1,128)} %get-tuple-element.38), channel_id=1, source_target_pairs={{0,2},{1,3},{2,0},{3,1},{4,6},{5,7},{6,4},{7,5},{8,10},{9,11},{10,... | collective-permute-start | bytes 20 | tf_op jit(solution)/shard_map/ppermute | solution.py:288
  52.7 6.2 %collective-permute-start.10 = (f32[1,1]{1,0:T(1,128)}, f32[1,1]{1,0:T(1,128)}, u32[]{:S(2)}, u32[]{:S(2)}) collective-permute-start(f32[1,1]{1,0:T(1,128)} %get-tuple-element.38), channel_id=1, source_target_pairs={{0,1},{1,0},{2,3},{3,2},{4,5},{5,4},{6,7},{7,6},{8,9},{9,8},{10,11... | collective-permute-start | bytes 20 | tf_op jit(solution)/shard_map/ppermute | solution.py:288
  53.0 2.9 %copy-start.7 = (f32[2,128]{1,0:T(2,128)S(1)}, f32[2,128]{1,0:T(2,128)}, u32[]{:S(2)}) copy-start(f32[2,128]{1,0:T(2,128)} %get-tuple-element.33.levels) | copy-start | bytes 3076
where the time goes:
time: 62.8 us; the launch traced here: 62.6 us
  waiting for transfers between devices  22.9 us (36%)
  Pallas kernels  18.4 us (29%)
  starting transfers between devices  16.4 us (26%)
  between operations  4.65 us (7%)
    ppermute x13, waiting for transfers between devices, swap(): return lax.ppermute(x, axis, [(i, i ^ mask) for i in range(size)])  22.9 us
    ppermute x13, starting transfers between devices, swap(): return lax.ppermute(x, axis, [(i, i ^ mask) for i in range(size)])  16.4 us
    pallas_call x2, Pallas kernels, on_device(): pl.pallas_call(functools.partial(apply_kernel, q), in_specs=specs, out_sp...  5.79 us
    pallas_call x1, Pallas kernels, on_device(): pl.pallas_call(functools.partial(project_first, orders[0]), name='project...  5.14 us
    pallas_call x2, Pallas kernels, on_device(): pl.pallas_call(functools.partial(stats_kernel, orders[q]), out_shape=[sha...  3.22 us
    pallas_call x1, Pallas kernels, on_device(): pl.pallas_call(functools.partial(project_second, orders[1]), name='projec...  2.22 us
    pallas_call x1, Pallas kernels, on_device(): pl.pallas_call(apply_tables_kernel, name='apply_tables', out_shape=[shape...  2.02 us
  transfers between devices with their start and end apart: 13, of which 10 were waited for; matrix products, arithmetic and copies ran while one was open for 0% of the time, Pallas kernels for 18%

commit v1 on v0

--- a/solution.py
+++ b/solution.py
@@ -133,14 +133,12 @@
     return pl.multiple_of(index * rows, rows)
 
 
-def project_half(order, re, im, miller, hi_ref, lo_ref, outs, rhs_hi, rhs_lo, full):
+def half_row(device, order, rel, rows):
+    return pl.multiple_of(lax.bitwise_xor(bit(device, order[0]), rel) * 2 * rows, rows)
+
+
+def load_bands(re, im, rhs_hi, rhs_lo):
     planes, half = re.shape
-    rows = PROJ // 4
-    device = lax.axis_index("ga")
-    weight = jnp.where(iota((8, planes), 0) == 0, squares(miller), 1.0).astype(BF16)
-    scale = jnp.where(iota((8, half), 0) == 0, 0.5 * KINETIC_SCALE, 1.0)
-    dens_hi, dens_lo = split(re * re + im * im)
-    sums = scale * (dot(weight, dens_hi) + dot(weight, dens_lo))
     re_hi, re_lo = split(re)
     im_hi, im_lo = split(im)
     for ref, a, b in ((rhs_hi, re_hi, im_hi), (rhs_lo, re_lo, im_lo)):
@@ -148,18 +146,46 @@
         ref[0:planes, half:] = b
         ref[planes:, 0:half] = b
         ref[planes:, half:] = -a
-    full[...] = dot(hi_ref[...], rhs_hi[...]) + dot(hi_ref[...], rhs_lo[...]) + dot(lo_ref[...], rhs_hi[...])
-    tail = jnp.concatenate([sums, jnp.zeros_like(sums)], axis=1)
-    for first, out in ((1, outs[0]), (0, outs[1])):
-        for second in (0, 1):
-            out[second * rows : (second + 1) * rows] = full[pl.ds(block_row(device, order, (first, second), rows), rows)]
-        out[2 * rows :] = tail
-
-
-def project_first(order, waves_in, miller_in, positions_in, form_in, species_in, sizes_in, *refs):
-    outs, (hi_ref, lo_ref) = refs[:2], refs[2:4]
-    waves, miller, positions, form, species, sizes, table, rhs_hi, rhs_lo, full, sems = refs[4:]
-    planes = miller.shape[1]
+
+
+def band_sums(re, im, miller):
+    planes, half = re.shape
+    weight = jnp.where(iota((8, planes), 0) == 0, squares(miller), 1.0).astype(BF16)
+    scale = jnp.where(iota((8, half), 0) == 0, 0.5 * KINETIC_SCALE, 1.0)
+    hi, lo = split(re * re + im * im)
+    return scale * (dot(weight, hi) + dot(weight, lo))
+
+
+def beta_rows(at, count, picks, owners, cosine, sine, radial, hi_ref, lo_ref):
+    planes = cosine.shape[1]
+    step = count // 2
+    for r in range(2):
+        source = pl.ds(pl.multiple_of(at + r * step, step), step)
+        part = slice(r * step, (r + 1) * step)
+        owner = owners[source]
+        size = dot(picks[source], radial[...])
+        hi, lo = split(size * dot(owner, cosine[...]))
+        hi_ref[part, 0:planes] = hi
+        lo_ref[part, 0:planes] = lo
+        hi, lo = split(-(size * dot(owner, sine[...])))
+        hi_ref[part, planes : 2 * planes] = hi
+        lo_ref[part, planes : 2 * planes] = lo
+
+
+def project(hi_ref, lo_ref, rhs_hi, rhs_lo):
+    return dot(hi_ref[...], rhs_hi[...]) + dot(hi_ref[...], rhs_lo[...]) + dot(lo_ref[...], rhs_hi[...])
+
+
+def ordered(device, order, full, out):
+    rows = full.shape[0] // 2
+    for second in (0, 1):
+        at = pl.multiple_of(lax.bitwise_xor(bit(device, order[1]), second) * rows, rows)
+        out[second * rows : (second + 1) * rows] = full[pl.ds(at, rows)]
+
+
+def project_send(order, waves_in, miller_in, positions_in, form_in, species_in, sizes_in, *refs):
+    out, hi_ref, lo_ref, rhs_hi, rhs_lo, cosine, sine, radial, picks, owners = refs[:10]
+    waves, miller, positions, form, species, sizes, table, full, sems = refs[10:]
     half = waves.shape[2]
     pairs = (
         (sizes_in, sizes),
@@ -172,35 +198,41 @@
     copies = [pltpu.make_async_copy(a, b, sems.at[n]) for n, (a, b) in enumerate(pairs)]
     for copy in copies:
         copy.start()
+    device = lax.axis_index("ga")
     for copy in copies[:5]:
         copy.wait()
     fill_rows(table, form)
-    depth = table.shape[0]
+    cos, sin = trig(positions[...], miller[...].astype(F32))
+    cosine[...] = stacked(cos)
+    sine[...] = stacked(sin)
+    radial[...] = stacked(table[...])
+    row, owner, _ = rows_by_projector(sizes[...].astype(F32), species[...].astype(F32), form.shape[1])
+    picks[...] = hot_rows(row, table.shape[0])
+    owners[...] = owner
+    rows = PROJ // 4
+    beta_rows(half_row(device, order, 1, rows), 2 * rows, picks, owners, cosine, sine, radial, hi_ref, lo_ref)
+    copies[5].wait()
+    load_bands(waves[0], waves[1], rhs_hi, rhs_lo)
+    full[...] = project(hi_ref, lo_ref, rhs_hi, rhs_lo)
+    ordered(device, order, full, out)
+
+
+def project_rest(order, waves, miller, hi_ref, lo_ref, rhs_hi, rhs_lo, cosine, sine, radial, picks, owners, *refs):
+    keep_first, send_second, keep_second, hi_keep, lo_keep, rhs_hi2, rhs_lo2, full = refs
+    half = waves.shape[2] // 2
+    rows = PROJ // 4
+    device = lax.axis_index("ga")
+    beta_rows(half_row(device, order, 0, rows), 2 * rows, picks, owners, cosine, sine, radial, hi_keep, lo_keep)
+    full[...] = project(hi_keep, lo_keep, rhs_hi, rhs_lo)
+    ordered(device, order, full, keep_first)
+    load_bands(waves[0, :, half:], waves[1, :, half:], rhs_hi2, rhs_lo2)
     m = miller[...].astype(F32)
-    cosine, sine = trig(positions[...], m)
-    cosine, sine = stacked(cosine), stacked(sine)
-    radial = stacked(table[...])
-    row, owners, _ = rows_by_projector(sizes[...].astype(F32), species[...].astype(F32), form.shape[1])
-    picks = hot_rows(row, depth)
-    rows = PROJ // 4
-    for r in range(4):
-        part = slice(r * rows, (r + 1) * rows)
-        size = dot(picks[part], radial)
-        hi, lo = split(size * dot(owners[part], cosine))
-        hi_ref[part, 0:planes] = hi
-        lo_ref[part, 0:planes] = lo
-        hi, lo = split(-(size * dot(owners[part], sine)))
-        hi_ref[part, planes : 2 * planes] = hi
-        lo_ref[part, planes : 2 * planes] = lo
-    copies[5].wait()
-    project_half(order, waves[0], waves[1], m, hi_ref, lo_ref, outs, rhs_hi, rhs_lo, full)
-
-
-def project_second(order, waves, miller, hi_ref, lo_ref, *refs):
-    outs, (rhs_hi, rhs_lo, full) = refs[:2], refs[2:]
-    half = waves.shape[2] // 2
-    re, im = waves[0, :, half:], waves[1, :, half:]
-    project_half(order, re, im, miller[...].astype(F32), hi_ref, lo_ref, outs, rhs_hi, rhs_lo, full)
+    sums = [band_sums(waves[0, :, part], waves[1, :, part], m) for part in (slice(0, half), slice(half, 2 * half))]
+    tail = jnp.concatenate(sums, axis=1)
+    for hi, lo, out in ((hi_ref, lo_ref, send_second), (hi_keep, lo_keep, keep_second)):
+        full[...] = project(hi, lo, rhs_hi2, rhs_lo2)
+        ordered(device, order, full, out)
+        out[2 * rows :] = tail
 
 
 def apply_tables_kernel(miller, positions, form, coupling, species, sizes, hi_ref, lo_ref, dense_hi, dense_lo, table, ctable):
@@ -237,11 +269,11 @@
     dense_lo[...] = lo
 
 
-def stats_kernel(order, own, near, far, sums, occupation, dense_hi, dense_lo, *refs):
-    share_in, levels_in = refs[:-5] or (None, None)
+def stats_kernel(order, q, own, near, far, sums, occupation, dense_hi, dense_lo, *refs):
     rhs_hi, rhs_lo, level_out, share_out, full = refs[-5:]
     rows = PROJ // 4
     half = occupation.shape[1]
+    bands = slice(q * half, (q + 1) * half)
     device = lax.axis_index("ga")
     for rel, ref, at in (((0, 0), own, 0), ((0, 1), near, 0), ((1, 0), far, 0), ((1, 1), far, rows)):
         full[pl.ds(block_row(device, order, rel, rows), rows)] = ref[at : at + rows]
@@ -250,16 +282,13 @@
     mixed = dot(dense_hi[...], p_hi) + dot(dense_hi[...], p_lo) + dot(dense_lo[...], p_hi)
     pairs = jnp.sum(proj * mixed, axis=0, keepdims=True)
     nonlocal_sum = pairs[:, 0:half] + pairs[:, half:]
-    kin, norm = sums[0:1, 0:half], sums[1:2, 0:half]
-    level = (kin + nonlocal_sum) / (norm + EPSILON)
+    kin, norm = sums[0:1, bands], sums[1:2, bands]
+    level_out[...] = (kin + nonlocal_sum) / (norm + EPSILON)
     share = jnp.sum(occupation[...] * (nonlocal_sum / (norm + EPSILON)), axis=1, keepdims=True)
-    if share_in is None:
-        level_out[...] = level
-        share_out[...] = share
-    else:
-        level_out[0:1] = levels_in[...]
-        level_out[1:2] = level
-        share_out[...] = share_in[...] + share
+    share = jnp.broadcast_to(share, share_out.shape)
+    for other in refs[:-5]:
+        share = other[...] + share
+    share_out[...] = share
     m_hi, m_lo = split(mixed)
     for ref, m in ((rhs_hi, m_hi), (rhs_lo, m_lo)):
         ref[0:PROJ] = m
@@ -267,21 +296,29 @@
         ref[PROJ:, half:] = m[:, 0:half]
 
 
-def apply_kernel(q, rhs_hi, rhs_lo, levels, waves, miller, hi_ref, lo_ref, *refs):
-    residual, staged, sem = refs[-3:]
+def apply_kernel(q, rhs_hi, rhs_lo, waves, miller, hi_ref, lo_ref, level, *refs):
     planes = miller.shape[1]
-    half = staged.shape[2]
+    half = level.shape[1]
     bands = slice(q * half, (q + 1) * half)
-    level = levels[q : q + 1]
     unit = jnp.where(iota((8, half), 0) == 0, 1.0, 0.0).astype(BF16)
     applied = dot(hi_ref[...], rhs_hi[...]) + dot(hi_ref[...], rhs_lo[...]) + dot(lo_ref[...], rhs_hi[...])
     line = jnp.broadcast_to(squares(miller[...].astype(F32)), (8, planes)).astype(BF16)
-    shifted = (0.5 * KINETIC_SCALE) * dot(line, unit, ((0,), (0,))) - level
+    shifted = (0.5 * KINETIC_SCALE) * dot(line, unit, ((0,), (0,))) - level[...]
+    if q == 0:
+        residual, staged, sems = refs
+    else:
+        before, _, residual, estimate, staged, levels, sems = refs
+        levels[0:1] = before[...]
+        levels[1:2] = level[...]
     staged[0] = shifted * waves[0, :, bands] + applied[:, 0:half]
     staged[1] = shifted * waves[1, :, bands] + applied[:, half:]
-    copy = pltpu.make_async_copy(staged, residual.at[:, :, pl.ds(q * half, half)], sem)
-    copy.start()
-    copy.wait()
+    copies = [pltpu.make_async_copy(staged, residual.at[:, :, pl.ds(q * half, half)], sems.at[0])]
+    if q == 1:
+        copies.append(pltpu.make_async_copy(levels, estimate, sems.at[1]))
+    for copy in copies:
+        copy.start()
+    for copy in copies:
+        copy.wait()
 
 
 def swap(x, axis, size, mask):
@@ -307,23 +344,20 @@
     species = species.reshape(1, -1)
     sizes = block_sizes.reshape(1, -1)
     bits = ga.bit_length() - 1
-    orders = ((0, 1), (1, 0))
+    order = (0, 1)
     params = pltpu.CompilerParams(vmem_limit_bytes=32 * 1024 * 1024)
     hbm = pl.BlockSpec(memory_space=pltpu.HBM)
     vmem = pl.BlockSpec(memory_space=pltpu.VMEM)
     shape = jax.ShapeDtypeStruct
-    pieces = [shape((2 * rows + 8, bands), F32)] * 2
-    beta = [shape((PROJ, 2 * planes), BF16)] * 2
-    work = [
-        pltpu.VMEM((2 * planes, bands), BF16),
-        pltpu.VMEM((2 * planes, bands), BF16),
-        pltpu.VMEM((PROJ, bands), F32),
-    ]
-    out = pl.pallas_call(
-        functools.partial(project_first, orders[0]),
-        name="project_first",
+    plain, summed = shape((2 * rows, bands), F32), shape((2 * rows + 8, bands), F32)
+    beta = [((2 * rows, 2 * planes), BF16)] * 2
+    rhs = [((2 * planes, bands), BF16)] * 2
+    tables = [((2 * atoms, planes), BF16)] * 2 + [((2 * depth, planes), BF16), ((PROJ, 2 * depth), BF16), ((PROJ, 2 * atoms), BF16)]
+    send_first, *passed = pl.pallas_call(
+        functools.partial(project_send, order),
+        name="project_send",
         in_specs=[hbm] * 6,
-        out_shape=pieces + beta,
+        out_shape=[plain] + [shape(*x) for x in beta + rhs + tables],
         scratch_shapes=[
             pltpu.VMEM((2, planes, half), F32),
             pltpu.VMEM(miller.shape, jnp.int32),
@@ -332,21 +366,18 @@
             pltpu.VMEM((1, atoms), jnp.int32),
             pltpu.VMEM((1, atoms), jnp.int32),
             pltpu.VMEM((depth, planes), F32),
-            *work,
+            pltpu.VMEM((2 * rows, bands), F32),
             pltpu.SemaphoreType.DMA((6,)),
         ],
         compiler_params=params,
     )(*(pltpu.with_memory_space_constraint(x, pltpu.HBM) for x in (waves, miller, positions, form, species, sizes)))
-    parts = [out[:2]]
-    parts.append(
-        pl.pallas_call(
-            functools.partial(project_second, orders[1]),
-            name="project_second",
-            out_shape=pieces,
-            scratch_shapes=work,
-            compiler_params=params,
-        )(waves, miller, out[2], out[3])
-    )
+    keep_first, send_second, keep_second = pl.pallas_call(
+        functools.partial(project_rest, order),
+        name="project_rest",
+        out_shape=[plain, summed, summed],
+        scratch_shapes=[pltpu.VMEM(*x) for x in beta + rhs] + [pltpu.VMEM((2 * rows, bands), F32)],
+        compiler_params=params,
+    )(waves, miller, *passed)
     tables = pl.pallas_call(
         apply_tables_kernel,
         name="apply_tables",
@@ -354,57 +385,50 @@
         scratch_shapes=[pltpu.VMEM((depth, planes), F32), pltpu.VMEM((depth, LANES), F32)],
         compiler_params=params,
     )(miller, positions, form, coupling, species, sizes)
-    kept, mine, own, near, far = {}, {}, {}, {}, {}
-    for q, order in enumerate(orders):
-        kept[q] = parts[q][1] + swap(parts[q][0], "ga", ga, 1 << order[0])
-    for q, order in enumerate(orders):
-        k = kept[q]
+    mine, own, near, far = {}, {}, {}, {}
+    kept = [
+        keep_first + swap(send_first, "ga", ga, 1 << order[0]), keep_second + swap(send_second, "ga", ga, 1 << order[0])
+    ]
+    for q, k in enumerate(kept):
         got = swap(k[rows:], "ga", ga, 1 << order[1])
-        mine[q] = jnp.concatenate([k[:rows] + got[:rows], k[2 * rows :] + got[rows:]], axis=0)
+        mine[q] = k[:rows] + got[:rows]
+        if q == 1:
+            mine[q] = jnp.concatenate([mine[q], k[2 * rows :] + got[rows:]], axis=0)
     for b in range(2, bits):
         for q in range(2):
             mine[q] = mine[q] + swap(mine[q], "ga", ga, 1 << b)
-    for q, order in enumerate(orders):
+    for q in range(2):
         own[q] = mine[q][:rows]
         near[q] = swap(own[q], "ga", ga, 1 << order[1])
-    for q, order in enumerate(orders):
+    for q in range(2):
         far[q] = swap(jnp.concatenate([own[q], near[q]], axis=0), "ga", ga, 1 << order[0])
+    sums = mine[1][rows:]
     occ = occupation.reshape(2, half)
-    residual = levels = share = None
+    residual, levels, share = [], [], []
     for q in range(2):
-        operands = [own[q], near[q], far[q], mine[q][rows:], occ[q : q + 1], tables[2], tables[3]]
-        if q == 1:
-            operands += [share, levels]
-        rhs_hi, rhs_lo, levels, share = pl.pallas_call(
-            functools.partial(stats_kernel, orders[q]),
-            out_shape=[
-                shape((2 * PROJ, bands), BF16),
-                shape((2 * PROJ, bands), BF16),
-                shape((q + 1, half), F32),
-                shape((1, 1), F32),
-            ],
+        rhs_hi, rhs_lo, level, total = pl.pallas_call(
+            functools.partial(stats_kernel, order, q),
+            out_shape=[shape((2 * PROJ, bands), BF16)] * 2 + [shape((1, half), F32)] * 2,
             scratch_shapes=[pltpu.VMEM((PROJ, bands), F32)],
             compiler_params=params,
-        )(*operands)
+        )(own[q], near[q], far[q], sums, occ[q : q + 1], tables[2], tables[3], *share)
+        share = [total]
         if q == 1:
-            energy = tree([share] + [swap(share, "band", band, d) for d in range(1, band)])
-        operands = [rhs_hi, rhs_lo, levels, waves, miller, tables[0], tables[1]]
-        specs = [vmem] * len(operands)
-        alias = {}
-        if q == 1:
-            alias = {len(operands): 0}
-            operands.append(residual)
-            specs.append(hbm)
+            energy = tree([total] + [swap(total, "band", band, d) for d in range(1, band)])[0, 0]
+        operands = [rhs_hi, rhs_lo, waves, miller, tables[0], tables[1], level, *levels, *residual]
+        levels.append(level)
         residual = pl.pallas_call(
             functools.partial(apply_kernel, q),
-            in_specs=specs,
-            out_specs=hbm,
-            out_shape=shape(waves.shape, F32),
-            scratch_shapes=[pltpu.VMEM((2, planes, half), F32), pltpu.SemaphoreType.DMA],
-            input_output_aliases=alias,
+            in_specs=[vmem] * (7 + q) + [hbm] * q,
+            out_specs=[hbm] * (1 + q),
+            out_shape=[shape(waves.shape, F32)] + [shape((2, half), F32)] * q,
+            scratch_shapes=[pltpu.VMEM((2, planes, half), F32)]
+            + [pltpu.VMEM((2, half), F32)] * q
+            + [pltpu.SemaphoreType.DMA((2,))],
+            input_output_aliases={8: 0} if q else {},
             compiler_params=params,
         )(*operands)
-    return residual, levels.reshape(bands), energy.reshape(())
+    return residual[0], residual[1].reshape(bands), energy
 
 
 def solution(mesh):

time: 62.8 us -> 64.5 us (1.027)
  waiting for transfers between devices: 22.9 us -> 26.9 us
  between operations: 4.65 us -> 0.89 us
  starting transfers between devices: 16.4 us -> 19.5 us
  Pallas kernels: 18.4 us -> 16.3 us
    ppermute x13, waiting for transfers between devices: 22.9 us -> 26.9 us  [swap(): return lax.ppermute(x, axis, [(i, i ^ mask) for i in range(size)])]
    ppermute x13, starting transfers between devices: 16.4 us -> 19.5 us  [swap(): return lax.ppermute(x, axis, [(i, i ^ mask) for i in range(size)])]
    pallas_call x6, Pallas kernels: 16.4 us -> 14.2 us  [the longest x2 5.76 us: on_device(): pl.pallas_call(functools.partial(apply_kernel, q), in_specs=[vmem] * (7 +...]
  transfers between devices with their start and end apart: 13 -> 13, of which waited for: 10 -> 7; matrix products, arithmetic and copies ran while one was open for 0% -> 0% of each run, Pallas kernels for 18% -> 13%
where the time goes in v1:
time: 64.5 us; the launch traced here: 64.4 us
  waiting for transfers between devices  26.9 us (42%)
  starting transfers between devices  19.5 us (30%)
  Pallas kernels  16.3 us (25%)
  between operations  0.89 us (1%)
  other arithmetic  0.71 us (1%)
    ppermute x13, waiting for transfers between devices, swap(): return lax.ppermute(x, axis, [(i, i ^ mask) for i in range(size)])  26.9 us
    ppermute x13, starting transfers between devices, swap(): return lax.ppermute(x, axis, [(i, i ^ mask) for i in range(size)])  19.5 us
    pallas_call x2, Pallas kernels, on_device(): pl.pallas_call(functools.partial(apply_kernel, q), in_specs=[vmem] * (7 +...  5.76 us
    pallas_call x1, Pallas kernels, on_device(): pl.pallas_call(functools.partial(project_send, order), name='project_send...  3.73 us
    pallas_call x1, Pallas kernels, on_device(): pl.pallas_call(functools.partial(project_rest, order), name='project_rest...  3.28 us
    pallas_call x1, Pallas kernels, on_device(): pl.pallas_call(apply_tables_kernel, name='apply_tables', out_shape=[shape...  2.02 us
    pallas_call x2, Pallas kernels, on_device(): pl.pallas_call(functools.partial(stats_kernel, order, q), out_shape=[shap...  1.48 us
  transfers between devices with their start and end apart: 13, of which 7 were waited for; matrix products, arithmetic and copies ran while one was open for 0% of the time, Pallas kernels for 13%

profile of v1, /device:TPU:0, one launch (start us, length us, event | category | flops | bytes accessed | tf_op | source)
XLA Modules:
  0.0 64.4 jit_solution(1107108252619276398)
XLA Ops:
  0.6 0.0 copy-start
  0.6 0.0 copy-start.2
  0.6 3.7 %project_send.1 = (f32[256,256]{1,0:T(8,128)S(1)}, bf16[256,2048]{1,0:T(8,128)(2,1)S(1)}, bf16[256,2048]{1,0:T(8,128)(2,1)S(1)}, bf16[2048,256]{1,0:T(8,128)(2,1...) custom-call(f32[2,1024,256]{2,1,0:T(8,128)} %waves.5, ...), custom_call_target="tpu_custom_call" | custom-call | tf_op jit(solution)/shard_map/project_send/pallas_call | solution.py:356
  4.4 0.0 copy-done
  4.4 0.0 copy-done.2
  4.4 3.3 %project_rest.1 = (f32[256,256]{1,0:T(8,128)S(1)}, f32[264,256]{1,0:T(8,128)S(1)}, f32[264,256]{1,0:T(8,128)S(1)}) custom-call(f32[2,1024,256]{2,1,0:T(8,128)S(1)} %copy-done, s32[3,1024]{1,0:T(4,128)S(1)} %copy-done.2, bf16[256,2048]{1,0:T(8,128)(2,1)S(1)} %get-tuple-element.30.hi_ref, bf16[256,2048]{1,0:T(8,128)(2,1)S(1)} %get-tuple-element.31.lo_ref, ...), custom_call_target="tpu_custom_call" | custom-call | tf_op jit(solution)/shard_map/project_rest/pallas_call | solution.py:374
  7.7 3.0 %collective-permute-start = (f32[264,256]{1,0:T(8,128)S(1)}, f32[264,256]{1,0:T(8,128)S(1)}, u32[]{:S(2)}, u32[]{:S(2)}) collective-permute-start(f32[264,256]{1,0:T(8,128)S(1)} %get-tuple-element.40), channel_id=1, source_target_pairs={{0,4},{4,0},{8,12},{12,8},{16,20},{20,16},{24,28},{28,24},{1,5},{5... | collective-permute-start | bytes 811016 | tf_op jit(solution)/shard_map/ppermute | solution.py:325
  10.7 0.1 collective-permute-start.5
  10.8 7.3 %collective-permute-done = f32[264,256]{1,0:T(8,128)S(1)} collective-permute-done((f32[264,256]{1,0:T(8,128)S(1)}, f32[264,256]{1,0:T(8,128)S(1)}, u32[]{:S(2)}, u32[]{:S(2)}) %collective-permute-start) | collective-permute-done | bytes 270368 | tf_op jit(solution)/shard_map/ppermute | solution.py:325
  18.1 2.2 %collective-permute-start.1 = (f32[136,256]{1,0:T(8,128)S(1)}, f32[136,256]{1,0:T(8,128)S(1)}, u32[]{:S(2)}, u32[]{:S(2)}) collective-permute-start(f32[136,256]{1,0:T(8,128)S(1)} %slice.57), channel_id=1, source_target_pairs={{0,8},{4,12},{8,0},{12,4},{16,24},{20,28},{24,16},{28,20},{1,9},{5... | collective-permute-start | bytes 417800 | tf_op jit(solution)/shard_map/ppermute | solution.py:325
  20.3 2.5 %collective-permute-done.5 = f32[256,256]{1,0:T(8,128)S(1)} collective-permute-done((f32[256,256]{1,0:T(8,128)S(1)}, f32[256,256]{1,0:T(8,128)S(1)}, u32[]{:S(2)}, u32[]{:S(2)}) %collective-permute-start.5) | collective-permute-done | bytes 262176 | tf_op jit(solution)/shard_map/ppermute | solution.py:325
  22.8 0.0 copy-start.1
  22.8 0.0 copy-start.3
  22.8 0.0 copy-start.4
  22.8 0.0 copy-start.5
  22.8 0.0 copy-start.6
  22.9 0.0 copy-start.7
  22.9 2.0 %collective-permute-start.6 = (f32[128,256]{1,0:T(8,128)S(1)}, f32[128,256]{1,0:T(8,128)S(1)}, u32[]{:S(2)}, u32[]{:S(2)}) collective-permute-start(f32[128,256]{1,0:T(8,128)S(1)} %slice.64), channel_id=1, source_target_pairs={{0,8},{4,12},{8,0},{12,4},{16,24},{20,28},{24,16},{28,20},{1,9},{5... | collective-permute-start | bytes 393224 | tf_op jit(solution)/shard_map/ppermute | solution.py:325
  24.9 0.0 collective-permute-done.1
  24.9 2.7 %collective-permute-start.2 = (f32[136,256]{1,0:T(8,128)S(1)}, f32[136,256]{1,0:T(8,128)S(1)}, u32[]{:S(2)}, u32[]{:S(2)}) collective-permute-start(f32[136,256]{1,0:T(8,128)S(1)} %pad_maximum_fusion.2), channel_id=1, source_target_pairs={{0,16},{4,20},{8,24},{12,28},{16,0},{20,4},{24,8},{28,12},{1,17},{... | collective-permute-start | bytes 417800 | tf_op jit(solution)/shard_map/ppermute | solution.py:325
  27.6 1.5 %collective-permute-done.6 = f32[128,256]{1,0:T(8,128)S(1)} collective-permute-done((f32[128,256]{1,0:T(8,128)S(1)}, f32[128,256]{1,0:T(8,128)S(1)}, u32[]{:S(2)}, u32[]{:S(2)}) %collective-permute-start.6) | collective-permute-done | bytes 131104 | tf_op jit(solution)/shard_map/ppermute | solution.py:325
  29.1 2.7 %collective-permute-start.7 = (f32[128,256]{1,0:T(8,128)S(1)}, f32[128,256]{1,0:T(8,128)S(1)}, u32[]{:S(2)}, u32[]{:S(2)}) collective-permute-start(f32[128,256]{1,0:T(8,128)S(1)} %slice_add_fusion), channel_id=1, source_target_pairs={{0,16},{4,20},{8,24},{12,28},{16,0},{20,4},{24,8},{28,12},{1,17},{... | collective-permute-start | bytes 393224 | tf_op jit(solution)/shard_map/ppermute | solution.py:325
  31.8 7.0 %collective-permute-done.7 = f32[128,256]{1,0:T(8,128)S(1)} collective-permute-done((f32[128,256]{1,0:T(8,128)S(1)}, f32[128,256]{1,0:T(8,128)S(1)}, u32[]{:S(2)}, u32[]{:S(2)}) %collective-permute-start.7) | collective-permute-done | bytes 131104 | tf_op jit(solution)/shard_map/ppermute | solution.py:325
  38.8 0.1 collective-permute-start.8
  38.9 0.0 collective-permute-done.2
  39.0 2.1 %collective-permute-start.3 = (f32[128,256]{1,0:T(8,128)S(1)}, f32[128,256]{1,0:T(8,128)S(1)}, u32[]{:S(2)}, u32[]{:S(2)}) collective-permute-start(f32[128,256]{1,0:T(8,128)S(1)} %slice.61.own), channel_id=1, source_target_pairs={{0,8},{4,12},{8,0},{12,4},{16,24},{20,28},{24,16},{28,20},{1,9},{5... | collective-permute-start | bytes 393224 | tf_op jit(solution)/shard_map/ppermute | solution.py:325
  41.0 3.5 %collective-permute-done.8.near = f32[128,256]{1,0:T(8,128)S(1)} collective-permute-done((f32[128,256]{1,0:T(8,128)S(1)}, f32[128,256]{1,0:T(8,128)S(1)}, u32[]{:S(2)}, u32[]{:S(2)}) %collective-permute-start.8) | collective-permute-done | bytes 131104 | tf_op jit(solution)/shard_map/ppermute | solution.py:325
  44.5 1.5 %collective-permute-start.9 = (f32[256,256]{1,0:T(8,128)S(1)}, f32[256,256]{1,0:T(8,128)S(1)}, u32[]{:S(2)}, u32[]{:S(2)}) collective-permute-start(f32[256,256]{1,0:T(8,128)S(1)} %pad_maximum_fusion.1), channel_id=1, source_target_pairs={{0,4},{4,0},{8,12},{12,8},{16,20},{20,16},{24,28},{28,24},{1,5},{5... | collective-permute-start | bytes 786440 | tf_op jit(solution)/shard_map/ppermute | solution.py:325
  46.1 0.0 collective-permute-done.3.near
  46.1 1.4 %collective-permute-start.4 = (f32[256,256]{1,0:T(8,128)S(1)}, f32[256,256]{1,0:T(8,128)S(1)}, u32[]{:S(2)}, u32[]{:S(2)}) collective-permute-start(f32[256,256]{1,0:T(8,128)S(1)} %pad_maximum_fusion), channel_id=1, source_target_pairs={{0,4},{4,0},{8,12},{12,8},{16,20},{20,16},{24,28},{28,24},{1,5},{5... | collective-permute-start | bytes 786440 | tf_op jit(solution)/shard_map/ppermute | solution.py:325
  47.5 0.0 copy-done.1
  47.5 0.0 copy-done.3
  47.5 0.0 copy-done.4
  47.5 0.0 copy-done.5
  47.5 0.0 copy-done.6
  47.5 2.0 %apply_tables.1 = (bf16[1024,1024]{1,0:T(8,128)(2,1)S(1)}, bf16[1024,1024]{1,0:T(8,128)(2,1)S(1)}, bf16[512,512]{1,0:T(8,128)(2,1)S(1)}, bf16[512,512]{1,0:T(8,128)(2,1)S(1)}) custom-call(s32[3,1024]{1,0:T(4,128)S(1)} %copy-done.2, f32[3,64]{1,0:T(4,128)S(1)} %bitcast.16, f32[18,4,1024]{2,1,0:T(4,128)S(1)} %bitcast.13, f32[18,4,18]{2,1,0:T(4,128)S(1)} %bitcast.14, ...), custom_call_target="tpu_custom_call" | custom-call | tf_op jit(solution)/shard_map/apply_tables/pallas_call | solution.py:381
  49.5 0.0 copy-done.7
  49.6 3.1 %collective-permute-done.9.far = f32[256,256]{1,0:T(8,128)S(1)} collective-permute-done((f32[256,256]{1,0:T(8,128)S(1)}, f32[256,256]{1,0:T(8,128)S(1)}, u32[]{:S(2)}, u32[]{:S(2)}) %collective-permute-start.9) | collective-permute-done | bytes 262176 | tf_op jit(solution)/shard_map/ppermute | solution.py:325
  52.6 0.7 %shard_map.103 = (bf16[1024,256]{1,0:T(8,128)(2,1)S(1)}, bf16[1024,256]{1,0:T(8,128)(2,1)S(1)}, f32[1,128]{1,0:T(1,128)S(1)}, f32[1,128]{1,0:T(1,128)S(1)}) custom-call(f32[128,256]{1,0:T(8,128)S(1)} %add.36.own, f32[128,256]{1,0:T(8,128)S(1)} %collective-permute-done.8.near, f32[256,256]{1,0:T(8,128)S(1)} %collective-permute-done.9.far, ...), custom_call_target="tpu_custom_call" | custom-call | tf_op jit(solution)/shard_map/pallas_call | solution.py:409
  53.4 2.1 %collective-permute-done.4.far = f32[256,256]{1,0:T(8,128)S(1)} collective-permute-done((f32[256,256]{1,0:T(8,128)S(1)}, f32[256,256]{1,0:T(8,128)S(1)}, u32[]{:S(2)}, u32[]{:S(2)}) %collective-permute-start.4) | collective-permute-done | bytes 262176 | tf_op jit(solution)/shard_map/ppermute | solution.py:325
  55.4 0.7 %shard_map.104 = (bf16[1024,256]{1,0:T(8,128)(2,1)S(1)}, bf16[1024,256]{1,0:T(8,128)(2,1)S(1)}, f32[1,128]{1,0:T(1,128)S(1)}, f32[1,128]{1,0:T(1,128)S(1)}) custom-call(f32[128,256]{1,0:T(8,128)S(1)} %slice.61.own, f32[128,256]{1,0:T(8,128)S(1)} %collective-permute-done.3.near, f32[256,256]{1,0:T(8,128)S(1)} %collective-permute-done.4.far, ...), custom_call_target="tpu_custom_call" | custom-call | tf_op jit(solution)/shard_map/pallas_call | solution.py:409
  56.2 0.0 collective-permute-start.10
  56.2 1.6 %collective-permute-start.11 = (f32[1,128]{1,0:T(1,128)S(1)}, f32[1,128]{1,0:T(1,128)S(1)}, u32[]{:S(2)}, u32[]{:S(2)}) collective-permute-start(f32[1,128]{1,0:T(1,128)S(1)} %get-tuple-element.56), channel_id=1, source_target_pairs={{0,2},{1,3},{2,0},{3,1},{4,6},{5,7},{6,4},{7,5},{8,10},{9,11},{10,... | collective-permute-start | bytes 1544 | tf_op jit(solution)/shard_map/ppermute | solution.py:325
  57.8 0.3 collective-permute-start.12
  58.0 2.9 %shard_map.105.refs_1_ = f32[2,1024,256]{2,1,0:T(8,128)} custom-call(bf16[1024,256]{1,0:T(8,128)(2,1)S(1)} %get-tuple-element.52.rhs_hi, bf16[1024,256]{1,0:T(8,128)(2,1)S(1)} %get-tuple-element.53.rhs_lo, f32[2,1024,256]{2,1,0:T(8,128)S(1)} %copy-done, s32[3,1024]{1,0:T(4,128)S(1)} %copy-done.2, bf16[1024,1024]{1,0:T(8,128)(2,1)S(1)} %get-tuple-element.48.hi_ref, ...), custom_call_target="tpu_custom_call" | custom-call | tf_op jit(solution)/shard_map/pallas_call | solution.py:420
  60.9 2.9 %shard_map.106 = (f32[2,1024,256]{2,1,0:T(8,128)}, f32[2,128]{1,0:T(2,128)}) custom-call(bf16[1024,256]{1,0:T(8,128)(2,1)S(1)} %get-tuple-element.46.rhs_hi, bf16[1024,256]{1,0:T(8,128)(2,1)S(1)} %get-tuple-element.47.rhs_lo, f32[2,1024,256]{2,1,0:T(8,128)S(1)} %copy-done, s32[3,1024]{1,0:T(4,128)S(1)} %copy-done.2, ...), custom_call_target="tpu_custom_call", output_to_operand_aliasing={{0}: (8, {})} | custom-call | tf_op jit(solution)/shard_map/pallas_call | solution.py:420
  63.8 0.0 collective-permute-done.10
  63.8 0.0 collective-permute-done.11
  63.8 0.0 collective-permute-done.12
  63.8 0.5 add_add_fusion
  (15 shorter events, 0.2 us)
Async XLA Ops:
  0.6 3.8 %copy-start = (f32[2,1024,256]{2,1,0:T(8,128)S(1)}, f32[2,1024,256]{2,1,0:T(8,128)}, u32[]{:S(2)}) copy-start(f32[2,1024,256]{2,1,0:T(8,128)} %waves.5) | copy-start | bytes 6291460
  0.6 3.8 %copy-start.2 = (s32[3,1024]{1,0:T(4,128)S(1)}, s32[3,1024]{1,0:T(4,128)}, u32[]{:S(2)}) copy-start(s32[3,1024]{1,0:T(4,128)} %miller.7) | copy-start | bytes 36868
  7.7 10.4 %collective-permute-start = (f32[264,256]{1,0:T(8,128)S(1)}, f32[264,256]{1,0:T(8,128)S(1)}, u32[]{:S(2)}, u32[]{:S(2)}) collective-permute-start(f32[264,256]{1,0:T(8,128)S(1)} %get-tuple-element.40), channel_id=1, source_target_pairs={{0,4},{4,0},{8,12},{12,8},{16,20},{20,16},{24,28},{28,24},{1,5},{5... | collective-permute-start | bytes 811016 | tf_op jit(solution)/shard_map/ppermute | solution.py:325
  10.7 12.1 %collective-permute-start.5 = (f32[256,256]{1,0:T(8,128)S(1)}, f32[256,256]{1,0:T(8,128)S(1)}, u32[]{:S(2)}, u32[]{:S(2)}) collective-permute-start(f32[256,256]{1,0:T(8,128)S(1)} %get-tuple-element.44), channel_id=1, source_target_pairs={{0,4},{4,0},{8,12},{12,8},{16,20},{20,16},{24,28},{28,24},{1,5},{5... | collective-permute-start | bytes 786440 | tf_op jit(solution)/shard_map/ppermute | solution.py:325
  18.1 6.8 %collective-permute-start.1 = (f32[136,256]{1,0:T(8,128)S(1)}, f32[136,256]{1,0:T(8,128)S(1)}, u32[]{:S(2)}, u32[]{:S(2)}) collective-permute-start(f32[136,256]{1,0:T(8,128)S(1)} %slice.57), channel_id=1, source_target_pairs={{0,8},{4,12},{8,0},{12,4},{16,24},{20,28},{24,16},{28,20},{1,9},{5... | collective-permute-start | bytes 417800 | tf_op jit(solution)/shard_map/ppermute | solution.py:325
  22.8 24.7 %copy-start.1 = (f32[4,18,1024]{2,0,1:T(4,128)S(1)}, f32[4,18,1024]{2,0,1:T(4,128)}, u32[]{:S(2)}) copy-start(f32[4,18,1024]{2,0,1:T(4,128)} %param.11) | copy-start | bytes 884740
  22.8 24.7 %copy-start.3 = (f32[4,18,18]{2,0,1:T(4,128)S(1)}, f32[4,18,18]{2,0,1:T(4,128)}, u32[]{:S(2)}) copy-start(f32[4,18,18]{2,0,1:T(4,128)} %param.12) | copy-start | bytes 15556
  22.8 24.7 %copy-start.4 = (f32[64,3]{0,1:T(4,128)S(1)}, f32[64,3]{0,1:T(4,128)}, u32[]{:S(2)}) copy-start(f32[64,3]{0,1:T(4,128)} %param.10) | copy-start | bytes 2308
  22.8 24.7 %copy-start.5 = (s32[64]{0:T(128)S(1)}, s32[64]{0:T(128)}, u32[]{:S(2)}) copy-start(s32[64]{0:T(128)} %param.13) | copy-start | bytes 772
  22.8 24.7 %copy-start.6 = (s32[64]{0:T(128)S(1)}, s32[64]{0:T(128)}, u32[]{:S(2)}) copy-start(s32[64]{0:T(128)} %param.14) | copy-start | bytes 772
  22.9 26.6 %copy-start.7 = (f32[256]{0:T(256)S(1)}, f32[256]{0:T(256)}, u32[]{:S(2)}) copy-start(f32[256]{0:T(256)} %param.15) | copy-start | bytes 3076
  22.9 6.2 %collective-permute-start.6 = (f32[128,256]{1,0:T(8,128)S(1)}, f32[128,256]{1,0:T(8,128)S(1)}, u32[]{:S(2)}, u32[]{:S(2)}) collective-permute-start(f32[128,256]{1,0:T(8,128)S(1)} %slice.64), channel_id=1, source_target_pairs={{0,8},{4,12},{8,0},{12,4},{16,24},{20,28},{24,16},{28,20},{1,9},{5... | collective-permute-start | bytes 393224 | tf_op jit(solution)/shard_map/ppermute | solution.py:325
  24.9 14.0 %collective-permute-start.2 = (f32[136,256]{1,0:T(8,128)S(1)}, f32[136,256]{1,0:T(8,128)S(1)}, u32[]{:S(2)}, u32[]{:S(2)}) collective-permute-start(f32[136,256]{1,0:T(8,128)S(1)} %pad_maximum_fusion.2), channel_id=1, source_target_pairs={{0,16},{4,20},{8,24},{12,28},{16,0},{20,4},{24,8},{28,12},{1,17},{... | collective-permute-start | bytes 417800 | tf_op jit(solution)/shard_map/ppermute | solution.py:325
  29.1 9.7 %collective-permute-start.7 = (f32[128,256]{1,0:T(8,128)S(1)}, f32[128,256]{1,0:T(8,128)S(1)}, u32[]{:S(2)}, u32[]{:S(2)}) collective-permute-start(f32[128,256]{1,0:T(8,128)S(1)} %slice_add_fusion), channel_id=1, source_target_pairs={{0,16},{4,20},{8,24},{12,28},{16,0},{20,4},{24,8},{28,12},{1,17},{... | collective-permute-start | bytes 393224 | tf_op jit(solution)/shard_map/ppermute | solution.py:325
  38.8 5.7 %collective-permute-start.8 = (f32[128,256]{1,0:T(8,128)S(1)}, f32[128,256]{1,0:T(8,128)S(1)}, u32[]{:S(2)}, u32[]{:S(2)}) collective-permute-start(f32[128,256]{1,0:T(8,128)S(1)} %add.36.own), channel_id=1, source_target_pairs={{0,8},{4,12},{8,0},{12,4},{16,24},{20,28},{24,16},{28,20},{1,9},{5... | collective-permute-start | bytes 393224 | tf_op jit(solution)/shard_map/ppermute | solution.py:325
  39.0 7.1 %collective-permute-start.3 = (f32[128,256]{1,0:T(8,128)S(1)}, f32[128,256]{1,0:T(8,128)S(1)}, u32[]{:S(2)}, u32[]{:S(2)}) collective-permute-start(f32[128,256]{1,0:T(8,128)S(1)} %slice.61.own), channel_id=1, source_target_pairs={{0,8},{4,12},{8,0},{12,4},{16,24},{20,28},{24,16},{28,20},{1,9},{5... | collective-permute-start | bytes 393224 | tf_op jit(solution)/shard_map/ppermute | solution.py:325
  44.5 8.1 %collective-permute-start.9 = (f32[256,256]{1,0:T(8,128)S(1)}, f32[256,256]{1,0:T(8,128)S(1)}, u32[]{:S(2)}, u32[]{:S(2)}) collective-permute-start(f32[256,256]{1,0:T(8,128)S(1)} %pad_maximum_fusion.1), channel_id=1, source_target_pairs={{0,4},{4,0},{8,12},{12,8},{16,20},{20,16},{24,28},{28,24},{1,5},{5... | collective-permute-start | bytes 786440 | tf_op jit(solution)/shard_map/ppermute | solution.py:325
  46.1 9.3 %collective-permute-start.4 = (f32[256,256]{1,0:T(8,128)S(1)}, f32[256,256]{1,0:T(8,128)S(1)}, u32[]{:S(2)}, u32[]{:S(2)}) collective-permute-start(f32[256,256]{1,0:T(8,128)S(1)} %pad_maximum_fusion), channel_id=1, source_target_pairs={{0,4},{4,0},{8,12},{12,8},{16,20},{20,16},{24,28},{28,24},{1,5},{5... | collective-permute-start | bytes 786440 | tf_op jit(solution)/shard_map/ppermute | solution.py:325
  56.2 7.6 %collective-permute-start.10 = (f32[1,128]{1,0:T(1,128)S(1)}, f32[1,128]{1,0:T(1,128)S(1)}, u32[]{:S(2)}, u32[]{:S(2)}) collective-permute-start(f32[1,128]{1,0:T(1,128)S(1)} %get-tuple-element.56), channel_id=1, source_target_pairs={{0,1},{1,0},{2,3},{3,2},{4,5},{5,4},{6,7},{7,6},{8,9},{9,8},{10,11... | collective-permute-start | bytes 1544 | tf_op jit(solution)/shard_map/ppermute | solution.py:325
  56.2 7.6 %collective-permute-start.11 = (f32[1,128]{1,0:T(1,128)S(1)}, f32[1,128]{1,0:T(1,128)S(1)}, u32[]{:S(2)}, u32[]{:S(2)}) collective-permute-start(f32[1,128]{1,0:T(1,128)S(1)} %get-tuple-element.56), channel_id=1, source_target_pairs={{0,2},{1,3},{2,0},{3,1},{4,6},{5,7},{6,4},{7,5},{8,10},{9,11},{10,... | collective-permute-start | bytes 1544 | tf_op jit(solution)/shard_map/ppermute | solution.py:325
  57.8 6.1 %collective-permute-start.12 = (f32[1,128]{1,0:T(1,128)S(1)}, f32[1,128]{1,0:T(1,128)S(1)}, u32[]{:S(2)}, u32[]{:S(2)}) collective-permute-start(f32[1,128]{1,0:T(1,128)S(1)} %get-tuple-element.56), channel_id=1, source_target_pairs={{0,3},{1,2},{2,1},{3,0},{4,7},{5,6},{6,5},{7,4},{8,11},{9,10},{10,... | collective-permute-start | bytes 1544 | tf_op jit(solution)/shard_map/ppermute | solution.py:325

commit v2 on v1

--- a/solution.py
+++ b/solution.py
@@ -176,16 +176,16 @@
     return dot(hi_ref[...], rhs_hi[...]) + dot(hi_ref[...], rhs_lo[...]) + dot(lo_ref[...], rhs_hi[...])
 
 
-def ordered(device, order, full, out):
+def ordered(device, order, full, outs):
     rows = full.shape[0] // 2
-    for second in (0, 1):
+    for second, out in enumerate(outs):
         at = pl.multiple_of(lax.bitwise_xor(bit(device, order[1]), second) * rows, rows)
-        out[second * rows : (second + 1) * rows] = full[pl.ds(at, rows)]
+        out[0:rows] = full[pl.ds(at, rows)]
 
 
 def project_send(order, waves_in, miller_in, positions_in, form_in, species_in, sizes_in, *refs):
-    out, hi_ref, lo_ref, rhs_hi, rhs_lo, cosine, sine, radial, picks, owners = refs[:10]
-    waves, miller, positions, form, species, sizes, table, full, sems = refs[10:]
+    outs, (hi_ref, lo_ref, rhs_hi, rhs_lo, cosine, sine, radial, picks, owners) = refs[:2], refs[2:11]
+    waves, miller, positions, form, species, sizes, table, full, sems = refs[11:]
     half = waves.shape[2]
     pairs = (
         (sizes_in, sizes),
@@ -214,25 +214,27 @@
     copies[5].wait()
     load_bands(waves[0], waves[1], rhs_hi, rhs_lo)
     full[...] = project(hi_ref, lo_ref, rhs_hi, rhs_lo)
-    ordered(device, order, full, out)
+    ordered(device, order, full, outs)
 
 
 def project_rest(order, waves, miller, hi_ref, lo_ref, rhs_hi, rhs_lo, cosine, sine, radial, picks, owners, *refs):
-    keep_first, send_second, keep_second, hi_keep, lo_keep, rhs_hi2, rhs_lo2, full = refs
+    first, second_send, second_keep = refs[:2], refs[2:4], refs[4:6]
+    hi_keep, lo_keep, rhs_hi2, rhs_lo2, full = refs[6:]
     half = waves.shape[2] // 2
     rows = PROJ // 4
     device = lax.axis_index("ga")
     beta_rows(half_row(device, order, 0, rows), 2 * rows, picks, owners, cosine, sine, radial, hi_keep, lo_keep)
     full[...] = project(hi_keep, lo_keep, rhs_hi, rhs_lo)
-    ordered(device, order, full, keep_first)
+    ordered(device, order, full, first)
     load_bands(waves[0, :, half:], waves[1, :, half:], rhs_hi2, rhs_lo2)
     m = miller[...].astype(F32)
     sums = [band_sums(waves[0, :, part], waves[1, :, part], m) for part in (slice(0, half), slice(half, 2 * half))]
     tail = jnp.concatenate(sums, axis=1)
-    for hi, lo, out in ((hi_ref, lo_ref, send_second), (hi_keep, lo_keep, keep_second)):
+    for hi, lo, outs in ((hi_ref, lo_ref, second_send), (hi_keep, lo_keep, second_keep)):
         full[...] = project(hi, lo, rhs_hi2, rhs_lo2)
-        ordered(device, order, full, out)
-        out[2 * rows :] = tail
+        ordered(device, order, full, outs)
+        for out in outs:
+            out[rows:] = tail
 
 
 def apply_tables_kernel(miller, positions, form, coupling, species, sizes, hi_ref, lo_ref, dense_hi, dense_lo, table, ctable):
@@ -269,14 +271,14 @@
     dense_lo[...] = lo
 
 
-def stats_kernel(order, q, own, near, far, sums, occupation, dense_hi, dense_lo, *refs):
+def stats_kernel(order, q, own, near, far, across, sums, occupation, dense_hi, dense_lo, *refs):
     rhs_hi, rhs_lo, level_out, share_out, full = refs[-5:]
     rows = PROJ // 4
     half = occupation.shape[1]
     bands = slice(q * half, (q + 1) * half)
     device = lax.axis_index("ga")
-    for rel, ref, at in (((0, 0), own, 0), ((0, 1), near, 0), ((1, 0), far, 0), ((1, 1), far, rows)):
-        full[pl.ds(block_row(device, order, rel, rows), rows)] = ref[at : at + rows]
+    for rel, ref in (((0, 0), own), ((0, 1), near), ((1, 0), far), ((1, 1), across)):
+        full[pl.ds(block_row(device, order, rel, rows), rows)] = ref[0:rows]
     proj = full[...]
     p_hi, p_lo = split(proj)
     mixed = dot(dense_hi[...], p_hi) + dot(dense_hi[...], p_lo) + dot(dense_lo[...], p_hi)
@@ -349,15 +351,15 @@
     hbm = pl.BlockSpec(memory_space=pltpu.HBM)
     vmem = pl.BlockSpec(memory_space=pltpu.VMEM)
     shape = jax.ShapeDtypeStruct
-    plain, summed = shape((2 * rows, bands), F32), shape((2 * rows + 8, bands), F32)
+    plain, summed = shape((rows, bands), F32), shape((rows + 8, bands), F32)
     beta = [((2 * rows, 2 * planes), BF16)] * 2
     rhs = [((2 * planes, bands), BF16)] * 2
     tables = [((2 * atoms, planes), BF16)] * 2 + [((2 * depth, planes), BF16), ((PROJ, 2 * depth), BF16), ((PROJ, 2 * atoms), BF16)]
-    send_first, *passed = pl.pallas_call(
+    far_first, across_first, *passed = pl.pallas_call(
         functools.partial(project_send, order),
         name="project_send",
         in_specs=[hbm] * 6,
-        out_shape=[plain] + [shape(*x) for x in beta + rhs + tables],
+        out_shape=[plain] * 2 + [shape(*x) for x in beta + rhs + tables],
         scratch_shapes=[
             pltpu.VMEM((2, planes, half), F32),
             pltpu.VMEM(miller.shape, jnp.int32),
@@ -371,10 +373,10 @@
         ],
         compiler_params=params,
     )(*(pltpu.with_memory_space_constraint(x, pltpu.HBM) for x in (waves, miller, positions, form, species, sizes)))
-    keep_first, send_second, keep_second = pl.pallas_call(
+    keep_first, near_first, far_second, across_second, keep_second, near_second = pl.pallas_call(
         functools.partial(project_rest, order),
         name="project_rest",
-        out_shape=[plain, summed, summed],
+        out_shape=[plain] * 2 + [summed] * 4,
         scratch_shapes=[pltpu.VMEM(*x) for x in beta + rhs] + [pltpu.VMEM((2 * rows, bands), F32)],
         compiler_params=params,
     )(waves, miller, *passed)
@@ -385,23 +387,19 @@
         scratch_shapes=[pltpu.VMEM((depth, planes), F32), pltpu.VMEM((depth, LANES), F32)],
         compiler_params=params,
     )(miller, positions, form, coupling, species, sizes)
-    mine, own, near, far = {}, {}, {}, {}
-    kept = [
-        keep_first + swap(send_first, "ga", ga, 1 << order[0]), keep_second + swap(send_second, "ga", ga, 1 << order[0])
-    ]
-    for q, k in enumerate(kept):
-        got = swap(k[rows:], "ga", ga, 1 << order[1])
-        mine[q] = k[:rows] + got[:rows]
-        if q == 1:
-            mine[q] = jnp.concatenate([mine[q], k[2 * rows :] + got[rows:]], axis=0)
+    far_bit, near_bit = 1 << order[0], 1 << order[1]
+    masks = {"n": near_bit, "f": far_bit, "a": far_bit | near_bit}
+    streams = ((keep_first, near_first, far_first, across_first), (keep_second, near_second, far_second, across_second))
+    mine, own, gathered = {}, {}, {}
+    for q, (keep, *sent) in enumerate(streams):
+        got = [swap(x, "ga", ga, masks[kind]) for kind, x in zip(masks, sent)]
+        mine[q] = tree([keep] + got)
     for b in range(2, bits):
         for q in range(2):
             mine[q] = mine[q] + swap(mine[q], "ga", ga, 1 << b)
     for q in range(2):
         own[q] = mine[q][:rows]
-        near[q] = swap(own[q], "ga", ga, 1 << order[1])
-    for q in range(2):
-        far[q] = swap(jnp.concatenate([own[q], near[q]], axis=0), "ga", ga, 1 << order[0])
+        gathered[q] = [swap(own[q], "ga", ga, mask) for mask in masks.values()]
     sums = mine[1][rows:]
     occ = occupation.reshape(2, half)
     residual, levels, share = [], [], []
@@ -411,7 +409,7 @@
             out_shape=[shape((2 * PROJ, bands), BF16)] * 2 + [shape((1, half), F32)] * 2,
             scratch_shapes=[pltpu.VMEM((PROJ, bands), F32)],
             compiler_params=params,
-        )(own[q], near[q], far[q], sums, occ[q : q + 1], tables[2], tables[3], *share)
+        )(own[q], *gathered[q], sums, occ[q : q + 1], tables[2], tables[3], *share)
         share = [total]
         if q == 1:
             energy = tree([total] + [swap(total, "band", band, d) for d in range(1, band)])[0, 0]

time: 64.5 us -> 55.2 us (0.86)
  waiting for transfers between devices: 26.9 us -> 8.52 us
  starting transfers between devices: 19.5 us -> 28.7 us
    ppermute x13 -> x17, waiting for transfers between devices: 26.9 us -> 8.52 us  [swap(): return lax.ppermute(x, axis, [(i, i ^ mask) for i in range(size)])]
    ppermute x13 -> x17, starting transfers between devices: 19.5 us -> 28.7 us  [swap(): return lax.ppermute(x, axis, [(i, i ^ mask) for i in range(size)])]
  transfers between devices with their start and end apart: 13 -> 17, of which waited for: 7 -> 7; matrix products, arithmetic and copies ran while one was open for 0% -> 0% of each run, Pallas kernels for 13% -> 15%
where the time goes in v2:
time: 55.2 us; the launch traced here: 55.1 us
  starting transfers between devices  28.7 us (52%)
  Pallas kernels  16.3 us (30%)
  waiting for transfers between devices  8.52 us (15%)
  between operations  0.84 us (2%)
  other arithmetic  0.63 us (1%)
    ppermute x17, starting transfers between devices, swap(): return lax.ppermute(x, axis, [(i, i ^ mask) for i in range(size)])  28.7 us
    ppermute x17, waiting for transfers between devices, swap(): return lax.ppermute(x, axis, [(i, i ^ mask) for i in range(size)])  8.52 us
    pallas_call x2, Pallas kernels, on_device(): pl.pallas_call(functools.partial(apply_kernel, q), in_specs=[vmem] * (7 +...  5.75 us
    pallas_call x1, Pallas kernels, on_device(): pl.pallas_call(functools.partial(project_send, order), name='project_send...  3.75 us
    pallas_call x1, Pallas kernels, on_device(): pl.pallas_call(functools.partial(project_rest, order), name='project_rest...  3.3 us
    pallas_call x1, Pallas kernels, on_device(): pl.pallas_call(apply_tables_kernel, name='apply_tables', out_shape=[shape...  2.02 us
    pallas_call x2, Pallas kernels, on_device(): pl.pallas_call(functools.partial(stats_kernel, order, q), out_shape=[shap...  1.48 us
  transfers between devices with their start and end apart: 17, of which 7 were waited for; matrix products, arithmetic and copies ran while one was open for 0% of the time, Pallas kernels for 15%

profile of v2, /device:TPU:0, one launch (start us, length us, event | category | flops | bytes accessed | tf_op | source)
XLA Modules:
  0.0 55.1 jit_solution(10996557253933191575)
XLA Ops:
  0.6 0.0 copy-start
  0.6 0.0 copy-start.2
  0.6 3.8 %project_send.1 = (f32[128,256]{1,0:T(8,128)S(1)}, f32[128,256]{1,0:T(8,128)S(1)}, bf16[256,2048]{1,0:T(8,128)(2,1)S(1)}, bf16[256,2048]{1,0:T(8,128)(2,1)S(1)},...) custom-call(f32[2,1024,256]{2,1,0:T(8,128)} %waves.5, ...), custom_call_target="tpu_custom_call" | custom-call | tf_op jit(solution)/shard_map/project_send/pallas_call | solution.py:358
  4.4 0.0 copy-done
  4.4 0.0 copy-done.2
  4.4 0.0 copy-start.1
  4.4 0.0 copy-start.3
  4.5 0.0 copy-start.4
  4.5 0.0 copy-start.5
  4.5 0.0 copy-start.6
  4.5 3.3 %project_rest.1 = (f32[128,256]{1,0:T(8,128)S(1)}, f32[128,256]{1,0:T(8,128)S(1)}, f32[136,256]{1,0:T(8,128)S(1)}, f32[136,256]{1,0:T(8,128)S(1)}, f32[136,256]{1,0:T(8,128)S(1)}, /*index=5*/f32[136,256]{1,0:T(8,128)S(1)}) custom-call(f32[2,1024,256]{2,1,0:T(8,128)S(1)} %copy-done, s32[3,1024]{1,0:T(4,128)S(1)} %copy-done.2, ...), custom_call_target="tpu_custom_call" | custom-call | tf_op jit(solution)/shard_map/project_rest/pallas_call | solution.py:376
  7.8 0.0 copy-start.7
  7.8 3.2 %collective-permute-start.7 = (f32[128,256]{1,0:T(8,128)S(1)}, f32[128,256]{1,0:T(8,128)S(1)}, u32[]{:S(2)}, u32[]{:S(2)}) collective-permute-start(f32[128,256]{1,0:T(8,128)S(1)} %get-tuple-element.50), channel_id=1, source_target_pairs={{0,8},{4,12},{8,0},{12,4},{16,24},{20,28},{24,16},{28,20},{1,9},{5... | collective-permute-start | bytes 393224 | tf_op jit(solution)/shard_map/ppermute | solution.py:327
  11.0 1.5 %collective-permute-start.8 = (f32[128,256]{1,0:T(8,128)S(1)}, f32[128,256]{1,0:T(8,128)S(1)}, u32[]{:S(2)}, u32[]{:S(2)}) collective-permute-start(f32[128,256]{1,0:T(8,128)S(1)} %get-tuple-element.51), channel_id=1, source_target_pairs={{0,4},{4,0},{8,12},{12,8},{16,20},{20,16},{24,28},{28,24},{1,5},{5... | collective-permute-start | bytes 393224 | tf_op jit(solution)/shard_map/ppermute | solution.py:327
  12.5 0.1 collective-permute-start.9
  12.5 1.9 %collective-permute-start = (f32[136,256]{1,0:T(8,128)S(1)}, f32[136,256]{1,0:T(8,128)S(1)}, u32[]{:S(2)}, u32[]{:S(2)}) collective-permute-start(f32[136,256]{1,0:T(8,128)S(1)} %get-tuple-element.44), channel_id=1, source_target_pairs={{0,8},{4,12},{8,0},{12,4},{16,24},{20,28},{24,16},{28,20},{1,9},{5... | collective-permute-start | bytes 417800 | tf_op jit(solution)/shard_map/ppermute | solution.py:327
  14.5 1.5 %collective-permute-start.1 = (f32[136,256]{1,0:T(8,128)S(1)}, f32[136,256]{1,0:T(8,128)S(1)}, u32[]{:S(2)}, u32[]{:S(2)}) collective-permute-start(f32[136,256]{1,0:T(8,128)S(1)} %get-tuple-element.45), channel_id=1, source_target_pairs={{0,4},{4,0},{8,12},{12,8},{16,20},{20,16},{24,28},{28,24},{1,5},{5... | collective-permute-start | bytes 417800 | tf_op jit(solution)/shard_map/ppermute | solution.py:327
  16.0 0.0 collective-permute-done.7
  16.0 2.3 %collective-permute-start.2 = (f32[136,256]{1,0:T(8,128)S(1)}, f32[136,256]{1,0:T(8,128)S(1)}, u32[]{:S(2)}, u32[]{:S(2)}) collective-permute-start(f32[136,256]{1,0:T(8,128)S(1)} %get-tuple-element.46), channel_id=1, source_target_pairs={{0,12},{4,8},{8,4},{12,0},{16,28},{20,24},{24,20},{28,16},{1,13},{... | collective-permute-start | bytes 417800 | tf_op jit(solution)/shard_map/ppermute | solution.py:327
  18.3 1.5 %collective-permute-done.8 = f32[128,256]{1,0:T(8,128)S(1)} collective-permute-done((f32[128,256]{1,0:T(8,128)S(1)}, f32[128,256]{1,0:T(8,128)S(1)}, u32[]{:S(2)}, u32[]{:S(2)}) %collective-permute-start.8) | collective-permute-done | bytes 131104 | tf_op jit(solution)/shard_map/ppermute | solution.py:327
  19.8 0.0 collective-permute-done.9
  19.8 2.6 %collective-permute-start.10 = (f32[128,256]{1,0:T(8,128)S(1)}, f32[128,256]{1,0:T(8,128)S(1)}, u32[]{:S(2)}, u32[]{:S(2)}) collective-permute-start(f32[128,256]{1,0:T(8,128)S(1)} %add_add_fusion.1), channel_id=1, source_target_pairs={{0,16},{4,20},{8,24},{12,28},{16,0},{20,4},{24,8},{28,12},{1,17},{... | collective-permute-start | bytes 393224 | tf_op jit(solution)/shard_map/ppermute | solution.py:327
  22.4 0.8 %collective-permute-done = f32[136,256]{1,0:T(8,128)S(1)} collective-permute-done((f32[136,256]{1,0:T(8,128)S(1)}, f32[136,256]{1,0:T(8,128)S(1)}, u32[]{:S(2)}, u32[]{:S(2)}) %collective-permute-start) | collective-permute-done | bytes 139296 | tf_op jit(solution)/shard_map/ppermute | solution.py:327
  23.2 0.0 collective-permute-done.1
  23.2 2.5 %collective-permute-done.2 = f32[136,256]{1,0:T(8,128)S(1)} collective-permute-done((f32[136,256]{1,0:T(8,128)S(1)}, f32[136,256]{1,0:T(8,128)S(1)}, u32[]{:S(2)}, u32[]{:S(2)}) %collective-permute-start.2) | collective-permute-done | bytes 139296 | tf_op jit(solution)/shard_map/ppermute | solution.py:327
  25.8 2.6 %collective-permute-start.3 = (f32[136,256]{1,0:T(8,128)S(1)}, f32[136,256]{1,0:T(8,128)S(1)}, u32[]{:S(2)}, u32[]{:S(2)}) collective-permute-start(f32[136,256]{1,0:T(8,128)S(1)} %add_add_fusion), channel_id=1, source_target_pairs={{0,16},{4,20},{8,24},{12,28},{16,0},{20,4},{24,8},{28,12},{1,17},{... | collective-permute-start | bytes 417800 | tf_op jit(solution)/shard_map/ppermute | solution.py:327
  28.4 0.1 collective-permute-done.10
  28.5 3.0 %collective-permute-start.11 = (f32[128,256]{1,0:T(8,128)S(1)}, f32[128,256]{1,0:T(8,128)S(1)}, u32[]{:S(2)}, u32[]{:S(2)}) collective-permute-start(f32[128,256]{1,0:T(8,128)S(1)} %add.40.own), channel_id=1, source_target_pairs={{0,8},{4,12},{8,0},{12,4},{16,24},{20,28},{24,16},{28,20},{1,9},{5... | collective-permute-start | bytes 393224 | tf_op jit(solution)/shard_map/ppermute | solution.py:327
  31.5 0.0 copy-done.1
  31.5 0.0 copy-done.3
  31.5 0.0 copy-done.4
  31.5 0.0 copy-done.5
  31.5 0.0 copy-done.6
  31.5 2.0 %apply_tables.1 = (bf16[1024,1024]{1,0:T(8,128)(2,1)S(1)}, bf16[1024,1024]{1,0:T(8,128)(2,1)S(1)}, bf16[512,512]{1,0:T(8,128)(2,1)S(1)}, bf16[512,512]{1,0:T(8,128)(2,1)S(1)}) custom-call(s32[3,1024]{1,0:T(4,128)S(1)} %copy-done.2, f32[3,64]{1,0:T(4,128)S(1)} %bitcast.16, f32[18,4,1024]{2,1,0:T(4,128)S(1)} %bitcast.13, f32[18,4,18]{2,1,0:T(4,128)S(1)} %bitcast.14, ...), custom_call_target="tpu_custom_call" | custom-call | tf_op jit(solution)/shard_map/apply_tables/pallas_call | solution.py:383
  33.6 3.1 %collective-permute-start.12 = (f32[128,256]{1,0:T(8,128)S(1)}, f32[128,256]{1,0:T(8,128)S(1)}, u32[]{:S(2)}, u32[]{:S(2)}) collective-permute-start(f32[128,256]{1,0:T(8,128)S(1)} %add.40.own), channel_id=1, source_target_pairs={{0,4},{4,0},{8,12},{12,8},{16,20},{20,16},{24,28},{28,24},{1,5},{5... | collective-permute-start | bytes 393224 | tf_op jit(solution)/shard_map/ppermute | solution.py:327
  36.6 1.5 %collective-permute-start.13 = (f32[128,256]{1,0:T(8,128)S(1)}, f32[128,256]{1,0:T(8,128)S(1)}, u32[]{:S(2)}, u32[]{:S(2)}) collective-permute-start(f32[128,256]{1,0:T(8,128)S(1)} %add.40.own), channel_id=1, source_target_pairs={{0,12},{4,8},{8,4},{12,0},{16,28},{20,24},{24,20},{28,16},{1,13},{... | collective-permute-start | bytes 393224 | tf_op jit(solution)/shard_map/ppermute | solution.py:327
  38.1 0.0 collective-permute-done.3
  38.2 0.6 %collective-permute-start.4 = (f32[128,256]{1,0:T(8,128)S(1)}, f32[128,256]{1,0:T(8,128)S(1)}, u32[]{:S(2)}, u32[]{:S(2)}) collective-permute-start(f32[128,256]{1,0:T(8,128)S(1)} %slice.28.own), channel_id=1, source_target_pairs={{0,8},{4,12},{8,0},{12,4},{16,24},{20,28},{24,16},{28,20},{1,9},{5... | collective-permute-start | bytes 393224 | tf_op jit(solution)/shard_map/ppermute | solution.py:327
  38.7 1.5 %collective-permute-start.5 = (f32[128,256]{1,0:T(8,128)S(1)}, f32[128,256]{1,0:T(8,128)S(1)}, u32[]{:S(2)}, u32[]{:S(2)}) collective-permute-start(f32[128,256]{1,0:T(8,128)S(1)} %slice.28.own), channel_id=1, source_target_pairs={{0,4},{4,0},{8,12},{12,8},{16,20},{20,16},{24,28},{28,24},{1,5},{5... | collective-permute-start | bytes 393224 | tf_op jit(solution)/shard_map/ppermute | solution.py:327
  40.3 0.0 collective-permute-done.11.near
  40.3 1.5 %collective-permute-start.6 = (f32[128,256]{1,0:T(8,128)S(1)}, f32[128,256]{1,0:T(8,128)S(1)}, u32[]{:S(2)}, u32[]{:S(2)}) collective-permute-start(f32[128,256]{1,0:T(8,128)S(1)} %slice.28.own), channel_id=1, source_target_pairs={{0,12},{4,8},{8,4},{12,0},{16,28},{20,24},{24,20},{28,16},{1,13},{... | collective-permute-start | bytes 393224 | tf_op jit(solution)/shard_map/ppermute | solution.py:327
  41.7 0.0 copy-done.7
  41.8 0.0 collective-permute-done.12.far
  41.8 1.4 %collective-permute-done.13.across = f32[128,256]{1,0:T(8,128)S(1)} collective-permute-done((f32[128,256]{1,0:T(8,128)S(1)}, f32[128,256]{1,0:T(8,128)S(1)}, u32[]{:S(2)}, u32[]{:S(2)}) %collective-permute-start.13) | collective-permute-done | bytes 131104 | tf_op jit(solution)/shard_map/ppermute | solution.py:327
  43.2 0.7 %shard_map.103 = (bf16[1024,256]{1,0:T(8,128)(2,1)S(1)}, bf16[1024,256]{1,0:T(8,128)(2,1)S(1)}, f32[1,128]{1,0:T(1,128)S(1)}, f32[1,128]{1,0:T(1,128)S(1)}) custom-call(f32[128,256]{1,0:T(8,128)S(1)} %add.40.own, f32[128,256]{1,0:T(8,128)S(1)} %collective-permute-done.11.near, f32[128,256]{1,0:T(8,128)S(1)} %collective-permute-done.12.far, ...), custom_call_target="tpu_custom_call" | custom-call | tf_op jit(solution)/shard_map/pallas_call | solution.py:407
  43.9 0.0 collective-permute-done.4.near
  43.9 0.6 %collective-permute-done.5.far = f32[128,256]{1,0:T(8,128)S(1)} collective-permute-done((f32[128,256]{1,0:T(8,128)S(1)}, f32[128,256]{1,0:T(8,128)S(1)}, u32[]{:S(2)}, u32[]{:S(2)}) %collective-permute-start.5) | collective-permute-done | bytes 131104 | tf_op jit(solution)/shard_map/ppermute | solution.py:327
  44.5 1.6 %collective-permute-done.6.across = f32[128,256]{1,0:T(8,128)S(1)} collective-permute-done((f32[128,256]{1,0:T(8,128)S(1)}, f32[128,256]{1,0:T(8,128)S(1)}, u32[]{:S(2)}, u32[]{:S(2)}) %collective-permute-start.6) | collective-permute-done | bytes 131104 | tf_op jit(solution)/shard_map/ppermute | solution.py:327
  46.1 0.7 %shard_map.104 = (bf16[1024,256]{1,0:T(8,128)(2,1)S(1)}, bf16[1024,256]{1,0:T(8,128)(2,1)S(1)}, f32[1,128]{1,0:T(1,128)S(1)}, f32[1,128]{1,0:T(1,128)S(1)}) custom-call(f32[128,256]{1,0:T(8,128)S(1)} %slice.28.own, f32[128,256]{1,0:T(8,128)S(1)} %collective-permute-done.4.near, f32[128,256]{1,0:T(8,128)S(1)} %collective-permute-done.5.far, ...), custom_call_target="tpu_custom_call" | custom-call | tf_op jit(solution)/shard_map/pallas_call | solution.py:407
  46.9 0.0 collective-permute-start.14
  46.9 1.4 %collective-permute-start.15 = (f32[1,128]{1,0:T(1,128)S(1)}, f32[1,128]{1,0:T(1,128)S(1)}, u32[]{:S(2)}, u32[]{:S(2)}) collective-permute-start(f32[1,128]{1,0:T(1,128)S(1)} %get-tuple-element.64), channel_id=1, source_target_pairs={{0,2},{1,3},{2,0},{3,1},{4,6},{5,7},{6,4},{7,5},{8,10},{9,11},{10,... | collective-permute-start | bytes 1544 | tf_op jit(solution)/shard_map/ppermute | solution.py:327
  48.3 0.5 collective-permute-start.16
  48.8 2.9 %shard_map.105.refs_1_ = f32[2,1024,256]{2,1,0:T(8,128)} custom-call(bf16[1024,256]{1,0:T(8,128)(2,1)S(1)} %get-tuple-element.60.rhs_hi, bf16[1024,256]{1,0:T(8,128)(2,1)S(1)} %get-tuple-element.61.rhs_lo, f32[2,1024,256]{2,1,0:T(8,128)S(1)} %copy-done, s32[3,1024]{1,0:T(4,128)S(1)} %copy-done.2, bf16[1024,1024]{1,0:T(8,128)(2,1)S(1)} %get-tuple-element.56.hi_ref, ...), custom_call_target="tpu_custom_call" | custom-call | tf_op jit(solution)/shard_map/pallas_call | solution.py:418
  51.6 2.9 %shard_map.106 = (f32[2,1024,256]{2,1,0:T(8,128)}, f32[2,128]{1,0:T(2,128)}) custom-call(bf16[1024,256]{1,0:T(8,128)(2,1)S(1)} %get-tuple-element.54.rhs_hi, bf16[1024,256]{1,0:T(8,128)(2,1)S(1)} %get-tuple-element.55.rhs_lo, f32[2,1024,256]{2,1,0:T(8,128)S(1)} %copy-done, s32[3,1024]{1,0:T(4,128)S(1)} %copy-done.2, ...), custom_call_target="tpu_custom_call", output_to_operand_aliasing={{0}: (8, {})} | custom-call | tf_op jit(solution)/shard_map/pallas_call | solution.py:418
  54.5 0.0 collective-permute-done.14
  54.5 0.0 collective-permute-done.15
  54.5 0.0 collective-permute-done.16
  54.5 0.5 add_add_fusion.2
  (7 shorter events, 0.1 us)
Async XLA Ops:
  0.6 3.8 %copy-start = (f32[2,1024,256]{2,1,0:T(8,128)S(1)}, f32[2,1024,256]{2,1,0:T(8,128)}, u32[]{:S(2)}) copy-start(f32[2,1024,256]{2,1,0:T(8,128)} %waves.5) | copy-start | bytes 6291460
  0.6 3.8 %copy-start.2 = (s32[3,1024]{1,0:T(4,128)S(1)}, s32[3,1024]{1,0:T(4,128)}, u32[]{:S(2)}) copy-start(s32[3,1024]{1,0:T(4,128)} %miller.7) | copy-start | bytes 36868
  4.4 27.1 %copy-start.1 = (f32[4,18,1024]{2,0,1:T(4,128)S(1)}, f32[4,18,1024]{2,0,1:T(4,128)}, u32[]{:S(2)}) copy-start(f32[4,18,1024]{2,0,1:T(4,128)} %param.11) | copy-start | bytes 884740
  4.4 27.1 %copy-start.3 = (f32[4,18,18]{2,0,1:T(4,128)S(1)}, f32[4,18,18]{2,0,1:T(4,128)}, u32[]{:S(2)}) copy-start(f32[4,18,18]{2,0,1:T(4,128)} %param.12) | copy-start | bytes 15556
  4.5 27.1 %copy-start.4 = (f32[64,3]{0,1:T(4,128)S(1)}, f32[64,3]{0,1:T(4,128)}, u32[]{:S(2)}) copy-start(f32[64,3]{0,1:T(4,128)} %param.10) | copy-start | bytes 2308
  4.5 27.1 %copy-start.5 = (s32[64]{0:T(128)S(1)}, s32[64]{0:T(128)}, u32[]{:S(2)}) copy-start(s32[64]{0:T(128)} %param.13) | copy-start | bytes 772
  4.5 27.1 %copy-start.6 = (s32[64]{0:T(128)S(1)}, s32[64]{0:T(128)}, u32[]{:S(2)}) copy-start(s32[64]{0:T(128)} %param.14) | copy-start | bytes 772
  7.8 33.9 %copy-start.7 = (f32[256]{0:T(256)S(1)}, f32[256]{0:T(256)}, u32[]{:S(2)}) copy-start(f32[256]{0:T(256)} %param.15) | copy-start | bytes 3076
  7.8 8.2 %collective-permute-start.7 = (f32[128,256]{1,0:T(8,128)S(1)}, f32[128,256]{1,0:T(8,128)S(1)}, u32[]{:S(2)}, u32[]{:S(2)}) collective-permute-start(f32[128,256]{1,0:T(8,128)S(1)} %get-tuple-element.50), channel_id=1, source_target_pairs={{0,8},{4,12},{8,0},{12,4},{16,24},{20,28},{24,16},{28,20},{1,9},{5... | collective-permute-start | bytes 393224 | tf_op jit(solution)/shard_map/ppermute | solution.py:327
  11.0 8.8 %collective-permute-start.8 = (f32[128,256]{1,0:T(8,128)S(1)}, f32[128,256]{1,0:T(8,128)S(1)}, u32[]{:S(2)}, u32[]{:S(2)}) collective-permute-start(f32[128,256]{1,0:T(8,128)S(1)} %get-tuple-element.51), channel_id=1, source_target_pairs={{0,4},{4,0},{8,12},{12,8},{16,20},{20,16},{24,28},{28,24},{1,5},{5... | collective-permute-start | bytes 393224 | tf_op jit(solution)/shard_map/ppermute | solution.py:327
  12.5 7.3 %collective-permute-start.9 = (f32[128,256]{1,0:T(8,128)S(1)}, f32[128,256]{1,0:T(8,128)S(1)}, u32[]{:S(2)}, u32[]{:S(2)}) collective-permute-start(f32[128,256]{1,0:T(8,128)S(1)} %get-tuple-element.52), channel_id=1, source_target_pairs={{0,12},{4,8},{8,4},{12,0},{16,28},{20,24},{24,20},{28,16},{1,13},{... | collective-permute-start | bytes 393224 | tf_op jit(solution)/shard_map/ppermute | solution.py:327
  12.5 10.7 %collective-permute-start = (f32[136,256]{1,0:T(8,128)S(1)}, f32[136,256]{1,0:T(8,128)S(1)}, u32[]{:S(2)}, u32[]{:S(2)}) collective-permute-start(f32[136,256]{1,0:T(8,128)S(1)} %get-tuple-element.44), channel_id=1, source_target_pairs={{0,8},{4,12},{8,0},{12,4},{16,24},{20,28},{24,16},{28,20},{1,9},{5... | collective-permute-start | bytes 417800 | tf_op jit(solution)/shard_map/ppermute | solution.py:327
  14.5 8.7 %collective-permute-start.1 = (f32[136,256]{1,0:T(8,128)S(1)}, f32[136,256]{1,0:T(8,128)S(1)}, u32[]{:S(2)}, u32[]{:S(2)}) collective-permute-start(f32[136,256]{1,0:T(8,128)S(1)} %get-tuple-element.45), channel_id=1, source_target_pairs={{0,4},{4,0},{8,12},{12,8},{16,20},{20,16},{24,28},{28,24},{1,5},{5... | collective-permute-start | bytes 417800 | tf_op jit(solution)/shard_map/ppermute | solution.py:327
  16.0 9.8 %collective-permute-start.2 = (f32[136,256]{1,0:T(8,128)S(1)}, f32[136,256]{1,0:T(8,128)S(1)}, u32[]{:S(2)}, u32[]{:S(2)}) collective-permute-start(f32[136,256]{1,0:T(8,128)S(1)} %get-tuple-element.46), channel_id=1, source_target_pairs={{0,12},{4,8},{8,4},{12,0},{16,28},{20,24},{24,20},{28,16},{1,13},{... | collective-permute-start | bytes 417800 | tf_op jit(solution)/shard_map/ppermute | solution.py:327
  19.8 8.7 %collective-permute-start.10 = (f32[128,256]{1,0:T(8,128)S(1)}, f32[128,256]{1,0:T(8,128)S(1)}, u32[]{:S(2)}, u32[]{:S(2)}) collective-permute-start(f32[128,256]{1,0:T(8,128)S(1)} %add_add_fusion.1), channel_id=1, source_target_pairs={{0,16},{4,20},{8,24},{12,28},{16,0},{20,4},{24,8},{28,12},{1,17},{... | collective-permute-start | bytes 393224 | tf_op jit(solution)/shard_map/ppermute | solution.py:327
  25.8 12.4 %collective-permute-start.3 = (f32[136,256]{1,0:T(8,128)S(1)}, f32[136,256]{1,0:T(8,128)S(1)}, u32[]{:S(2)}, u32[]{:S(2)}) collective-permute-start(f32[136,256]{1,0:T(8,128)S(1)} %add_add_fusion), channel_id=1, source_target_pairs={{0,16},{4,20},{8,24},{12,28},{16,0},{20,4},{24,8},{28,12},{1,17},{... | collective-permute-start | bytes 417800 | tf_op jit(solution)/shard_map/ppermute | solution.py:327
  28.5 11.8 %collective-permute-start.11 = (f32[128,256]{1,0:T(8,128)S(1)}, f32[128,256]{1,0:T(8,128)S(1)}, u32[]{:S(2)}, u32[]{:S(2)}) collective-permute-start(f32[128,256]{1,0:T(8,128)S(1)} %add.40.own), channel_id=1, source_target_pairs={{0,8},{4,12},{8,0},{12,4},{16,24},{20,28},{24,16},{28,20},{1,9},{5... | collective-permute-start | bytes 393224 | tf_op jit(solution)/shard_map/ppermute | solution.py:327
  33.6 8.2 %collective-permute-start.12 = (f32[128,256]{1,0:T(8,128)S(1)}, f32[128,256]{1,0:T(8,128)S(1)}, u32[]{:S(2)}, u32[]{:S(2)}) collective-permute-start(f32[128,256]{1,0:T(8,128)S(1)} %add.40.own), channel_id=1, source_target_pairs={{0,4},{4,0},{8,12},{12,8},{16,20},{20,16},{24,28},{28,24},{1,5},{5... | collective-permute-start | bytes 393224 | tf_op jit(solution)/shard_map/ppermute | solution.py:327
  36.6 6.5 %collective-permute-start.13 = (f32[128,256]{1,0:T(8,128)S(1)}, f32[128,256]{1,0:T(8,128)S(1)}, u32[]{:S(2)}, u32[]{:S(2)}) collective-permute-start(f32[128,256]{1,0:T(8,128)S(1)} %add.40.own), channel_id=1, source_target_pairs={{0,12},{4,8},{8,4},{12,0},{16,28},{20,24},{24,20},{28,16},{1,13},{... | collective-permute-start | bytes 393224 | tf_op jit(solution)/shard_map/ppermute | solution.py:327
  38.2 5.7 %collective-permute-start.4 = (f32[128,256]{1,0:T(8,128)S(1)}, f32[128,256]{1,0:T(8,128)S(1)}, u32[]{:S(2)}, u32[]{:S(2)}) collective-permute-start(f32[128,256]{1,0:T(8,128)S(1)} %slice.28.own), channel_id=1, source_target_pairs={{0,8},{4,12},{8,0},{12,4},{16,24},{20,28},{24,16},{28,20},{1,9},{5... | collective-permute-start | bytes 393224 | tf_op jit(solution)/shard_map/ppermute | solution.py:327
  38.7 5.8 %collective-permute-start.5 = (f32[128,256]{1,0:T(8,128)S(1)}, f32[128,256]{1,0:T(8,128)S(1)}, u32[]{:S(2)}, u32[]{:S(2)}) collective-permute-start(f32[128,256]{1,0:T(8,128)S(1)} %slice.28.own), channel_id=1, source_target_pairs={{0,4},{4,0},{8,12},{12,8},{16,20},{20,16},{24,28},{28,24},{1,5},{5... | collective-permute-start | bytes 393224 | tf_op jit(solution)/shard_map/ppermute | solution.py:327
  40.3 5.9 %collective-permute-start.6 = (f32[128,256]{1,0:T(8,128)S(1)}, f32[128,256]{1,0:T(8,128)S(1)}, u32[]{:S(2)}, u32[]{:S(2)}) collective-permute-start(f32[128,256]{1,0:T(8,128)S(1)} %slice.28.own), channel_id=1, source_target_pairs={{0,12},{4,8},{8,4},{12,0},{16,28},{20,24},{24,20},{28,16},{1,13},{... | collective-permute-start | bytes 393224 | tf_op jit(solution)/shard_map/ppermute | solution.py:327
  46.9 7.6 %collective-permute-start.14 = (f32[1,128]{1,0:T(1,128)S(1)}, f32[1,128]{1,0:T(1,128)S(1)}, u32[]{:S(2)}, u32[]{:S(2)}) collective-permute-start(f32[1,128]{1,0:T(1,128)S(1)} %get-tuple-element.64), channel_id=1, source_target_pairs={{0,1},{1,0},{2,3},{3,2},{4,5},{5,4},{6,7},{7,6},{8,9},{9,8},{10,11... | collective-permute-start | bytes 1544 | tf_op jit(solution)/shard_map/ppermute | solution.py:327
  46.9 7.6 %collective-permute-start.15 = (f32[1,128]{1,0:T(1,128)S(1)}, f32[1,128]{1,0:T(1,128)S(1)}, u32[]{:S(2)}, u32[]{:S(2)}) collective-permute-start(f32[1,128]{1,0:T(1,128)S(1)} %get-tuple-element.64), channel_id=1, source_target_pairs={{0,2},{1,3},{2,0},{3,1},{4,6},{5,7},{6,4},{7,5},{8,10},{9,11},{10,... | collective-permute-start | bytes 1544 | tf_op jit(solution)/shard_map/ppermute | solution.py:327
  48.3 6.3 %collective-permute-start.16 = (f32[1,128]{1,0:T(1,128)S(1)}, f32[1,128]{1,0:T(1,128)S(1)}, u32[]{:S(2)}, u32[]{:S(2)}) collective-permute-start(f32[1,128]{1,0:T(1,128)S(1)} %get-tuple-element.64), channel_id=1, source_target_pairs={{0,3},{1,2},{2,1},{3,0},{4,7},{5,6},{6,5},{7,4},{8,11},{9,10},{10,... | collective-permute-start | bytes 1544 | tf_op jit(solution)/shard_map/ppermute | solution.py:327

commit v3 on v2

--- a/solution.py
+++ b/solution.py
@@ -12,6 +12,7 @@
 KINETIC_SCALE = 0.005
 EPSILON = 1e-06
 LANES = 128
+CHUNKS = 4
 F32 = jnp.float32
 BF16 = jnp.bfloat16
 
@@ -199,16 +200,17 @@
     for copy in copies:
         copy.start()
     device = lax.axis_index("ga")
-    for copy in copies[:5]:
+    for copy in copies[:4]:
         copy.wait()
-    fill_rows(table, form)
     cos, sin = trig(positions[...], miller[...].astype(F32))
     cosine[...] = stacked(cos)
     sine[...] = stacked(sin)
-    radial[...] = stacked(table[...])
     row, owner, _ = rows_by_projector(sizes[...].astype(F32), species[...].astype(F32), form.shape[1])
     picks[...] = hot_rows(row, table.shape[0])
     owners[...] = owner
+    copies[4].wait()
+    fill_rows(table, form)
+    radial[...] = stacked(table[...])
     rows = PROJ // 4
     beta_rows(half_row(device, order, 1, rows), 2 * rows, picks, owners, cosine, sine, radial, hi_ref, lo_ref)
     copies[5].wait()
@@ -217,21 +219,26 @@
     ordered(device, order, full, outs)
 
 
-def project_rest(order, waves, miller, hi_ref, lo_ref, rhs_hi, rhs_lo, cosine, sine, radial, picks, owners, *refs):
-    first, second_send, second_keep = refs[:2], refs[2:4], refs[4:6]
-    hi_keep, lo_keep, rhs_hi2, rhs_lo2, full = refs[6:]
-    half = waves.shape[2] // 2
+def project_keep(order, rhs_hi, rhs_lo, cosine, sine, radial, picks, owners, *refs):
+    first, (hi_keep, lo_keep, full) = refs[:2], refs[2:]
     rows = PROJ // 4
     device = lax.axis_index("ga")
     beta_rows(half_row(device, order, 0, rows), 2 * rows, picks, owners, cosine, sine, radial, hi_keep, lo_keep)
     full[...] = project(hi_keep, lo_keep, rhs_hi, rhs_lo)
     ordered(device, order, full, first)
-    load_bands(waves[0, :, half:], waves[1, :, half:], rhs_hi2, rhs_lo2)
+
+
+def project_second(order, waves, miller, hi_ref, lo_ref, hi_keep, lo_keep, *refs):
+    second_send, second_keep, (rhs_hi, rhs_lo, full) = refs[:2], refs[2:4], refs[4:]
+    half = waves.shape[2] // 2
+    rows = PROJ // 4
+    device = lax.axis_index("ga")
+    load_bands(waves[0, :, half:], waves[1, :, half:], rhs_hi, rhs_lo)
     m = miller[...].astype(F32)
     sums = [band_sums(waves[0, :, part], waves[1, :, part], m) for part in (slice(0, half), slice(half, 2 * half))]
     tail = jnp.concatenate(sums, axis=1)
     for hi, lo, outs in ((hi_ref, lo_ref, second_send), (hi_keep, lo_keep, second_keep)):
-        full[...] = project(hi, lo, rhs_hi2, rhs_lo2)
+        full[...] = project(hi, lo, rhs_hi, rhs_lo)
         ordered(device, order, full, outs)
         for out in outs:
             out[rows:] = tail
@@ -303,22 +310,26 @@
     half = level.shape[1]
     bands = slice(q * half, (q + 1) * half)
     unit = jnp.where(iota((8, half), 0) == 0, 1.0, 0.0).astype(BF16)
-    applied = dot(hi_ref[...], rhs_hi[...]) + dot(hi_ref[...], rhs_lo[...]) + dot(lo_ref[...], rhs_hi[...])
     line = jnp.broadcast_to(squares(miller[...].astype(F32)), (8, planes)).astype(BF16)
     shifted = (0.5 * KINETIC_SCALE) * dot(line, unit, ((0,), (0,))) - level[...]
+    copies = []
     if q == 0:
         residual, staged, sems = refs
     else:
         before, _, residual, estimate, staged, levels, sems = refs
         levels[0:1] = before[...]
         levels[1:2] = level[...]
-    staged[0] = shifted * waves[0, :, bands] + applied[:, 0:half]
-    staged[1] = shifted * waves[1, :, bands] + applied[:, half:]
-    copies = [pltpu.make_async_copy(staged, residual.at[:, :, pl.ds(q * half, half)], sems.at[0])]
-    if q == 1:
-        copies.append(pltpu.make_async_copy(levels, estimate, sems.at[1]))
-    for copy in copies:
-        copy.start()
+        copies.append(pltpu.make_async_copy(levels, estimate, sems.at[2 * CHUNKS]))
+        copies[-1].start()
+    step = planes // CHUNKS
+    for r in range(CHUNKS):
+        part = slice(r * step, (r + 1) * step)
+        applied = dot(hi_ref[part], rhs_hi[...]) + dot(hi_ref[part], rhs_lo[...]) + dot(lo_ref[part], rhs_hi[...])
+        for n in range(2):
+            staged[n, r] = shifted[part] * waves[n, part, bands] + applied[:, n * half : (n + 1) * half]
+            target = residual.at[n, pl.ds(r * step, step), pl.ds(q * half, half)]
+            copies.append(pltpu.make_async_copy(staged.at[n, r], target, sems.at[2 * r + n]))
+            copies[-1].start()
     for copy in copies:
         copy.wait()
 
@@ -373,13 +384,21 @@
         ],
         compiler_params=params,
     )(*(pltpu.with_memory_space_constraint(x, pltpu.HBM) for x in (waves, miller, positions, form, species, sizes)))
-    keep_first, near_first, far_second, across_second, keep_second, near_second = pl.pallas_call(
-        functools.partial(project_rest, order),
-        name="project_rest",
-        out_shape=[plain] * 2 + [summed] * 4,
-        scratch_shapes=[pltpu.VMEM(*x) for x in beta + rhs] + [pltpu.VMEM((2 * rows, bands), F32)],
+    hi_send, lo_send, *halves = passed
+    keep_first, near_first, hi_keep, lo_keep = pl.pallas_call(
+        functools.partial(project_keep, order),
+        name="project_keep",
+        out_shape=[plain] * 2 + [shape(*x) for x in beta],
+        scratch_shapes=[pltpu.VMEM((2 * rows, bands), F32)],
         compiler_params=params,
-    )(waves, miller, *passed)
+    )(*halves)
+    far_second, across_second, keep_second, near_second = pl.pallas_call(
+        functools.partial(project_second, order),
+        name="project_second",
+        out_shape=[summed] * 4,
+        scratch_shapes=[pltpu.VMEM(*x) for x in rhs] + [pltpu.VMEM((2 * rows, bands), F32)],
+        compiler_params=params,
+    )(waves, miller, hi_send, lo_send, hi_keep, lo_keep)
     tables = pl.pallas_call(
         apply_tables_kernel,
         name="apply_tables",
@@ -420,9 +439,9 @@
             in_specs=[vmem] * (7 + q) + [hbm] * q,
             out_specs=[hbm] * (1 + q),
             out_shape=[shape(waves.shape, F32)] + [shape((2, half), F32)] * q,
-            scratch_shapes=[pltpu.VMEM((2, planes, half), F32)]
+            scratch_shapes=[pltpu.VMEM((2, CHUNKS, planes // CHUNKS, half), F32)]
             + [pltpu.VMEM((2, half), F32)] * q
-            + [pltpu.SemaphoreType.DMA((2,))],
+            + [pltpu.SemaphoreType.DMA((2 * CHUNKS + 1,))],
             input_output_aliases={8: 0} if q else {},
             compiler_params=params,
         )(*operands)

time: 55.2 us -> 52.1 us (0.944)
  starting transfers between devices: 28.7 us -> 21.9 us
  waiting for transfers between devices: 8.52 us -> 12.2 us
    ppermute x17, starting transfers between devices: 28.7 us -> 21.9 us  [swap(): return lax.ppermute(x, axis, [(i, i ^ mask) for i in range(size)])]
    ppermute x17, waiting for transfers between devices: 8.52 us -> 12.2 us  [swap(): return lax.ppermute(x, axis, [(i, i ^ mask) for i in range(size)])]
    pallas_call x1 -> x2, Pallas kernels: 3.3 us -> 3.73 us  [the longest x1 2.17 us: on_device(): pl.pallas_call(functools.partial(project_second, order), name='project_se...]
  transfers between devices with their start and end apart: 17 -> 17, of which waited for: 7 -> 6; matrix products, arithmetic and copies ran while one was open for 0% -> 0% of each run, Pallas kernels for 15% -> 20%
where the time goes in v3:
time: 52.1 us; the launch traced here: 51.9 us
  starting transfers between devices  21.9 us (42%)
  Pallas kernels  16.3 us (31%)
  waiting for transfers between devices  12.2 us (23%)
  between operations  0.81 us (2%)
  other arithmetic  0.63 us (1%)
    ppermute x17, starting transfers between devices, swap(): return lax.ppermute(x, axis, [(i, i ^ mask) for i in range(size)])  21.9 us
    ppermute x17, waiting for transfers between devices, swap(): return lax.ppermute(x, axis, [(i, i ^ mask) for i in range(size)])  12.2 us
    pallas_call x2, Pallas kernels, on_device(): pl.pallas_call(functools.partial(apply_kernel, q), in_specs=[vmem] * (7 +...  5.67 us
    pallas_call x1, Pallas kernels, on_device(): pl.pallas_call(functools.partial(project_send, order), name='project_send...  3.42 us
    pallas_call x1, Pallas kernels, on_device(): pl.pallas_call(functools.partial(project_second, order), name='project_se...  2.17 us
    pallas_call x1, Pallas kernels, on_device(): pl.pallas_call(apply_tables_kernel, name='apply_tables', out_shape=[shape...  2.03 us
    pallas_call x1, Pallas kernels, on_device(): pl.pallas_call(functools.partial(project_keep, order), name='project_keep...  1.56 us
    pallas_call x2, Pallas kernels, on_device(): pl.pallas_call(functools.partial(stats_kernel, order, q), out_shape=[shap...  1.48 us
  transfers between devices with their start and end apart: 17, of which 6 were waited for; matrix products, arithmetic and copies ran while one was open for 0% of the time, Pallas kernels for 20%

profile of v3, /device:TPU:0, one launch (start us, length us, event | category | flops | bytes accessed | tf_op | source)
XLA Modules:
  0.0 51.9 jit_solution(16013536398012711625)
XLA Ops:
  0.6 3.4 %project_send.1 = (f32[128,256]{1,0:T(8,128)S(1)}, f32[128,256]{1,0:T(8,128)S(1)}, bf16[256,2048]{1,0:T(8,128)(2,1)S(1)}, bf16[256,2048]{1,0:T(8,128)(2,1)S(1)},...) custom-call(f32[2,1024,256]{2,1,0:T(8,128)} %waves.5, ...), custom_call_target="tpu_custom_call" | custom-call | tf_op jit(solution)/shard_map/project_send/pallas_call | solution.py:369
  4.1 0.0 copy-start
  4.1 0.0 copy-start.2
  4.1 1.6 %project_keep.1 = (f32[128,256]{1,0:T(8,128)S(1)}, f32[128,256]{1,0:T(8,128)S(1)}, bf16[256,2048]{1,0:T(8,128)(2,1)S(1)}, bf16[256,2048]{1,0:T(8,128)(2,1)S(1)}) custom-call(bf16[2048,256]{1,0:T(8,128)(2,1)S(1)} %get-tuple-element.38.rhs_hi, bf16[2048,256]{1,0:T(8,128)(2,1)S(1)} %get-tuple-element.39.rhs_lo, bf16[128,1024]{1,0:T(8,128)(2,1)S(1)} %get-tuple-element.40.cosine, ...), custom_call_target="tpu_custom_call" | custom-call | tf_op jit(solution)/shard_map/project_keep/pallas_call | solution.py:388
  5.6 3.1 %collective-permute-start.7 = (f32[128,256]{1,0:T(8,128)S(1)}, f32[128,256]{1,0:T(8,128)S(1)}, u32[]{:S(2)}, u32[]{:S(2)}) collective-permute-start(f32[128,256]{1,0:T(8,128)S(1)} %get-tuple-element.54), channel_id=1, source_target_pairs={{0,8},{4,12},{8,0},{12,4},{16,24},{20,28},{24,16},{28,20},{1,9},{5... | collective-permute-start | bytes 393224 | tf_op jit(solution)/shard_map/ppermute | solution.py:338
  8.8 1.5 %collective-permute-start.8 = (f32[128,256]{1,0:T(8,128)S(1)}, f32[128,256]{1,0:T(8,128)S(1)}, u32[]{:S(2)}, u32[]{:S(2)}) collective-permute-start(f32[128,256]{1,0:T(8,128)S(1)} %get-tuple-element.55), channel_id=1, source_target_pairs={{0,4},{4,0},{8,12},{12,8},{16,20},{20,16},{24,28},{28,24},{1,5},{5... | collective-permute-start | bytes 393224 | tf_op jit(solution)/shard_map/ppermute | solution.py:338
  10.3 0.0 collective-permute-start.9
  10.3 0.0 copy-done
  10.3 0.0 copy-done.2
  10.3 0.0 copy-start.1
  10.3 0.0 copy-start.3
  10.3 0.0 copy-start.4
  10.4 0.0 copy-start.5
  10.4 0.0 copy-start.6
  10.4 2.2 %project_second.1 = (f32[136,256]{1,0:T(8,128)S(1)}, f32[136,256]{1,0:T(8,128)S(1)}, f32[136,256]{1,0:T(8,128)S(1)}, f32[136,256]{1,0:T(8,128)S(1)}) custom-call(f32[2,1024,256]{2,1,0:T(8,128)S(1)} %copy-done, s32[3,1024]{1,0:T(4,128)S(1)} %copy-done.2, bf16[256,2048]{1,0:T(8,128)(2,1)S(1)} %get-tuple-element.36.hi_ref, ...), custom_call_target="tpu_custom_call" | custom-call | tf_op jit(solution)/shard_map/project_second/pallas_call | solution.py:395
  12.6 0.0 copy-start.7
  12.6 2.0 %collective-permute-start = (f32[136,256]{1,0:T(8,128)S(1)}, f32[136,256]{1,0:T(8,128)S(1)}, u32[]{:S(2)}, u32[]{:S(2)}) collective-permute-start(f32[136,256]{1,0:T(8,128)S(1)} %get-tuple-element.48), channel_id=1, source_target_pairs={{0,8},{4,12},{8,0},{12,4},{16,24},{20,28},{24,16},{28,20},{1,9},{5... | collective-permute-start | bytes 417800 | tf_op jit(solution)/shard_map/ppermute | solution.py:338
  14.6 1.5 %collective-permute-start.1 = (f32[136,256]{1,0:T(8,128)S(1)}, f32[136,256]{1,0:T(8,128)S(1)}, u32[]{:S(2)}, u32[]{:S(2)}) collective-permute-start(f32[136,256]{1,0:T(8,128)S(1)} %get-tuple-element.49), channel_id=1, source_target_pairs={{0,4},{4,0},{8,12},{12,8},{16,20},{20,16},{24,28},{28,24},{1,5},{5... | collective-permute-start | bytes 417800 | tf_op jit(solution)/shard_map/ppermute | solution.py:338
  16.1 0.0 collective-permute-done.7
  16.1 0.0 collective-permute-start.2
  16.2 0.4 collective-permute-done.8
  16.5 0.4 collective-permute-done.9
  16.9 2.7 %collective-permute-start.10 = (f32[128,256]{1,0:T(8,128)S(1)}, f32[128,256]{1,0:T(8,128)S(1)}, u32[]{:S(2)}, u32[]{:S(2)}) collective-permute-start(f32[128,256]{1,0:T(8,128)S(1)} %add_add_fusion.1), channel_id=1, source_target_pairs={{0,16},{4,20},{8,24},{12,28},{16,0},{20,4},{24,8},{28,12},{1,17},{... | collective-permute-start | bytes 393224 | tf_op jit(solution)/shard_map/ppermute | solution.py:338
  19.6 1.0 %collective-permute-done = f32[136,256]{1,0:T(8,128)S(1)} collective-permute-done((f32[136,256]{1,0:T(8,128)S(1)}, f32[136,256]{1,0:T(8,128)S(1)}, u32[]{:S(2)}, u32[]{:S(2)}) %collective-permute-start) | collective-permute-done | bytes 139296 | tf_op jit(solution)/shard_map/ppermute | solution.py:338
  20.6 0.0 collective-permute-done.1
  20.6 4.0 %collective-permute-done.2 = f32[136,256]{1,0:T(8,128)S(1)} collective-permute-done((f32[136,256]{1,0:T(8,128)S(1)}, f32[136,256]{1,0:T(8,128)S(1)}, u32[]{:S(2)}, u32[]{:S(2)}) %collective-permute-start.2) | collective-permute-done | bytes 139296 | tf_op jit(solution)/shard_map/ppermute | solution.py:338
  24.6 1.6 %collective-permute-start.3 = (f32[136,256]{1,0:T(8,128)S(1)}, f32[136,256]{1,0:T(8,128)S(1)}, u32[]{:S(2)}, u32[]{:S(2)}) collective-permute-start(f32[136,256]{1,0:T(8,128)S(1)} %add_add_fusion), channel_id=1, source_target_pairs={{0,16},{4,20},{8,24},{12,28},{16,0},{20,4},{24,8},{28,12},{1,17},{... | collective-permute-start | bytes 417800 | tf_op jit(solution)/shard_map/ppermute | solution.py:338
  26.2 0.0 collective-permute-done.10
  26.3 2.4 %collective-permute-start.11 = (f32[128,256]{1,0:T(8,128)S(1)}, f32[128,256]{1,0:T(8,128)S(1)}, u32[]{:S(2)}, u32[]{:S(2)}) collective-permute-start(f32[128,256]{1,0:T(8,128)S(1)} %add.40.own), channel_id=1, source_target_pairs={{0,8},{4,12},{8,0},{12,4},{16,24},{20,28},{24,16},{28,20},{1,9},{5... | collective-permute-start | bytes 393224 | tf_op jit(solution)/shard_map/ppermute | solution.py:338
  28.6 0.0 copy-done.1
  28.7 0.0 copy-done.3
  28.7 0.0 copy-done.4
  28.7 0.0 copy-done.5
  28.7 0.0 copy-done.6
  28.7 2.0 %apply_tables.1 = (bf16[1024,1024]{1,0:T(8,128)(2,1)S(1)}, bf16[1024,1024]{1,0:T(8,128)(2,1)S(1)}, bf16[512,512]{1,0:T(8,128)(2,1)S(1)}, bf16[512,512]{1,0:T(8,128)(2,1)S(1)}) custom-call(s32[3,1024]{1,0:T(4,128)S(1)} %copy-done.2, f32[3,64]{1,0:T(4,128)S(1)} %bitcast.16, f32[18,4,1024]{2,1,0:T(4,128)S(1)} %bitcast.13, f32[18,4,18]{2,1,0:T(4,128)S(1)} %bitcast.14, ...), custom_call_target="tpu_custom_call" | custom-call | tf_op jit(solution)/shard_map/apply_tables/pallas_call | solution.py:402
  30.7 0.5 collective-permute-start.12
  31.2 1.1 %collective-permute-start.13 = (f32[128,256]{1,0:T(8,128)S(1)}, f32[128,256]{1,0:T(8,128)S(1)}, u32[]{:S(2)}, u32[]{:S(2)}) collective-permute-start(f32[128,256]{1,0:T(8,128)S(1)} %add.40.own), channel_id=1, source_target_pairs={{0,12},{4,8},{8,4},{12,0},{16,28},{20,24},{24,20},{28,16},{1,13},{... | collective-permute-start | bytes 393224 | tf_op jit(solution)/shard_map/ppermute | solution.py:338
  32.3 0.0 collective-permute-done.3
  32.3 2.0 %collective-permute-start.4 = (f32[128,256]{1,0:T(8,128)S(1)}, f32[128,256]{1,0:T(8,128)S(1)}, u32[]{:S(2)}, u32[]{:S(2)}) collective-permute-start(f32[128,256]{1,0:T(8,128)S(1)} %slice.28.own), channel_id=1, source_target_pairs={{0,8},{4,12},{8,0},{12,4},{16,24},{20,28},{24,16},{28,20},{1,9},{5... | collective-permute-start | bytes 393224 | tf_op jit(solution)/shard_map/ppermute | solution.py:338
  34.4 0.4 collective-permute-start.5
  34.8 0.0 collective-permute-done.11.near
  34.8 1.1 %collective-permute-start.6 = (f32[128,256]{1,0:T(8,128)S(1)}, f32[128,256]{1,0:T(8,128)S(1)}, u32[]{:S(2)}, u32[]{:S(2)}) collective-permute-start(f32[128,256]{1,0:T(8,128)S(1)} %slice.28.own), channel_id=1, source_target_pairs={{0,12},{4,8},{8,4},{12,0},{16,28},{20,24},{24,20},{28,16},{1,13},{... | collective-permute-start | bytes 393224 | tf_op jit(solution)/shard_map/ppermute | solution.py:338
  35.9 0.0 copy-done.7
  35.9 4.4 %collective-permute-done.12.far = f32[128,256]{1,0:T(8,128)S(1)} collective-permute-done((f32[128,256]{1,0:T(8,128)S(1)}, f32[128,256]{1,0:T(8,128)S(1)}, u32[]{:S(2)}, u32[]{:S(2)}) %collective-permute-start.12) | collective-permute-done | bytes 131104 | tf_op jit(solution)/shard_map/ppermute | solution.py:338
  40.3 0.0 collective-permute-done.13.across
  40.3 0.7 %shard_map.103 = (bf16[1024,256]{1,0:T(8,128)(2,1)S(1)}, bf16[1024,256]{1,0:T(8,128)(2,1)S(1)}, f32[1,128]{1,0:T(1,128)S(1)}, f32[1,128]{1,0:T(1,128)S(1)}) custom-call(f32[128,256]{1,0:T(8,128)S(1)} %add.40.own, f32[128,256]{1,0:T(8,128)S(1)} %collective-permute-done.11.near, f32[128,256]{1,0:T(8,128)S(1)} %collective-permute-done.12.far, ...), custom_call_target="tpu_custom_call" | custom-call | tf_op jit(solution)/shard_map/pallas_call | solution.py:426
  41.0 0.0 collective-permute-done.4.near
  41.0 2.1 %collective-permute-done.5.far = f32[128,256]{1,0:T(8,128)S(1)} collective-permute-done((f32[128,256]{1,0:T(8,128)S(1)}, f32[128,256]{1,0:T(8,128)S(1)}, u32[]{:S(2)}, u32[]{:S(2)}) %collective-permute-start.5) | collective-permute-done | bytes 131104 | tf_op jit(solution)/shard_map/ppermute | solution.py:338
  43.1 0.0 collective-permute-done.6.across
  43.1 0.7 %shard_map.104 = (bf16[1024,256]{1,0:T(8,128)(2,1)S(1)}, bf16[1024,256]{1,0:T(8,128)(2,1)S(1)}, f32[1,128]{1,0:T(1,128)S(1)}, f32[1,128]{1,0:T(1,128)S(1)}) custom-call(f32[128,256]{1,0:T(8,128)S(1)} %slice.28.own, f32[128,256]{1,0:T(8,128)S(1)} %collective-permute-done.4.near, f32[128,256]{1,0:T(8,128)S(1)} %collective-permute-done.5.far, ...), custom_call_target="tpu_custom_call" | custom-call | tf_op jit(solution)/shard_map/pallas_call | solution.py:426
  43.8 0.0 collective-permute-start.14
  43.9 1.6 %collective-permute-start.15 = (f32[1,128]{1,0:T(1,128)S(1)}, f32[1,128]{1,0:T(1,128)S(1)}, u32[]{:S(2)}, u32[]{:S(2)}) collective-permute-start(f32[1,128]{1,0:T(1,128)S(1)} %get-tuple-element.68), channel_id=1, source_target_pairs={{0,2},{1,3},{2,0},{3,1},{4,6},{5,7},{6,4},{7,5},{8,10},{9,11},{10,... | collective-permute-start | bytes 1544 | tf_op jit(solution)/shard_map/ppermute | solution.py:338
  45.5 0.3 collective-permute-start.16
  45.7 2.8 %shard_map.105.refs_1_ = f32[2,1024,256]{2,1,0:T(8,128)} custom-call(bf16[1024,256]{1,0:T(8,128)(2,1)S(1)} %get-tuple-element.64.rhs_hi, bf16[1024,256]{1,0:T(8,128)(2,1)S(1)} %get-tuple-element.65.rhs_lo, f32[2,1024,256]{2,1,0:T(8,128)S(1)} %copy-done, s32[3,1024]{1,0:T(4,128)S(1)} %copy-done.2, bf16[1024,1024]{1,0:T(8,128)(2,1)S(1)} %get-tuple-element.60.hi_ref, ...), custom_call_target="tpu_custom_call" | custom-call | tf_op jit(solution)/shard_map/pallas_call | solution.py:437
  48.5 2.8 %shard_map.106 = (f32[2,1024,256]{2,1,0:T(8,128)}, f32[2,128]{1,0:T(2,128)}) custom-call(bf16[1024,256]{1,0:T(8,128)(2,1)S(1)} %get-tuple-element.58.rhs_hi, bf16[1024,256]{1,0:T(8,128)(2,1)S(1)} %get-tuple-element.59.rhs_lo, f32[2,1024,256]{2,1,0:T(8,128)S(1)} %copy-done, s32[3,1024]{1,0:T(4,128)S(1)} %copy-done.2, ...), custom_call_target="tpu_custom_call", output_to_operand_aliasing={{0}: (8, {})} | custom-call | tf_op jit(solution)/shard_map/pallas_call | solution.py:437
  51.4 0.0 collective-permute-done.14
  51.4 0.0 collective-permute-done.15
  51.4 0.0 collective-permute-done.16
  51.4 0.5 add_add_fusion.2
  (7 shorter events, 0.1 us)
Async XLA Ops:
  4.1 6.3 %copy-start = (f32[2,1024,256]{2,1,0:T(8,128)S(1)}, f32[2,1024,256]{2,1,0:T(8,128)}, u32[]{:S(2)}) copy-start(f32[2,1024,256]{2,1,0:T(8,128)} %waves.5) | copy-start | bytes 6291460
  4.1 6.3 %copy-start.2 = (s32[3,1024]{1,0:T(4,128)S(1)}, s32[3,1024]{1,0:T(4,128)}, u32[]{:S(2)}) copy-start(s32[3,1024]{1,0:T(4,128)} %miller.7) | copy-start | bytes 36868
  5.6 10.5 %collective-permute-start.7 = (f32[128,256]{1,0:T(8,128)S(1)}, f32[128,256]{1,0:T(8,128)S(1)}, u32[]{:S(2)}, u32[]{:S(2)}) collective-permute-start(f32[128,256]{1,0:T(8,128)S(1)} %get-tuple-element.54), channel_id=1, source_target_pairs={{0,8},{4,12},{8,0},{12,4},{16,24},{20,28},{24,16},{28,20},{1,9},{5... | collective-permute-start | bytes 393224 | tf_op jit(solution)/shard_map/ppermute | solution.py:338
  8.8 7.7 %collective-permute-start.8 = (f32[128,256]{1,0:T(8,128)S(1)}, f32[128,256]{1,0:T(8,128)S(1)}, u32[]{:S(2)}, u32[]{:S(2)}) collective-permute-start(f32[128,256]{1,0:T(8,128)S(1)} %get-tuple-element.55), channel_id=1, source_target_pairs={{0,4},{4,0},{8,12},{12,8},{16,20},{20,16},{24,28},{28,24},{1,5},{5... | collective-permute-start | bytes 393224 | tf_op jit(solution)/shard_map/ppermute | solution.py:338
  10.3 6.6 %collective-permute-start.9 = (f32[128,256]{1,0:T(8,128)S(1)}, f32[128,256]{1,0:T(8,128)S(1)}, u32[]{:S(2)}, u32[]{:S(2)}) collective-permute-start(f32[128,256]{1,0:T(8,128)S(1)} %get-tuple-element.56), channel_id=1, source_target_pairs={{0,12},{4,8},{8,4},{12,0},{16,28},{20,24},{24,20},{28,16},{1,13},{... | collective-permute-start | bytes 393224 | tf_op jit(solution)/shard_map/ppermute | solution.py:338
  10.3 18.3 %copy-start.1 = (f32[4,18,1024]{2,0,1:T(4,128)S(1)}, f32[4,18,1024]{2,0,1:T(4,128)}, u32[]{:S(2)}) copy-start(f32[4,18,1024]{2,0,1:T(4,128)} %param.11) | copy-start | bytes 884740
  10.3 18.3 %copy-start.3 = (f32[4,18,18]{2,0,1:T(4,128)S(1)}, f32[4,18,18]{2,0,1:T(4,128)}, u32[]{:S(2)}) copy-start(f32[4,18,18]{2,0,1:T(4,128)} %param.12) | copy-start | bytes 15556
  10.3 18.3 %copy-start.4 = (f32[64,3]{0,1:T(4,128)S(1)}, f32[64,3]{0,1:T(4,128)}, u32[]{:S(2)}) copy-start(f32[64,3]{0,1:T(4,128)} %param.10) | copy-start | bytes 2308
  10.4 18.3 %copy-start.5 = (s32[64]{0:T(128)S(1)}, s32[64]{0:T(128)}, u32[]{:S(2)}) copy-start(s32[64]{0:T(128)} %param.13) | copy-start | bytes 772
  10.4 18.3 %copy-start.6 = (s32[64]{0:T(128)S(1)}, s32[64]{0:T(128)}, u32[]{:S(2)}) copy-start(s32[64]{0:T(128)} %param.14) | copy-start | bytes 772
  12.6 23.4 %copy-start.7 = (f32[256]{0:T(256)S(1)}, f32[256]{0:T(256)}, u32[]{:S(2)}) copy-start(f32[256]{0:T(256)} %param.15) | copy-start | bytes 3076
  12.6 8.0 %collective-permute-start = (f32[136,256]{1,0:T(8,128)S(1)}, f32[136,256]{1,0:T(8,128)S(1)}, u32[]{:S(2)}, u32[]{:S(2)}) collective-permute-start(f32[136,256]{1,0:T(8,128)S(1)} %get-tuple-element.48), channel_id=1, source_target_pairs={{0,8},{4,12},{8,0},{12,4},{16,24},{20,28},{24,16},{28,20},{1,9},{5... | collective-permute-start | bytes 417800 | tf_op jit(solution)/shard_map/ppermute | solution.py:338
  14.6 6.0 %collective-permute-start.1 = (f32[136,256]{1,0:T(8,128)S(1)}, f32[136,256]{1,0:T(8,128)S(1)}, u32[]{:S(2)}, u32[]{:S(2)}) collective-permute-start(f32[136,256]{1,0:T(8,128)S(1)} %get-tuple-element.49), channel_id=1, source_target_pairs={{0,4},{4,0},{8,12},{12,8},{16,20},{20,16},{24,28},{28,24},{1,5},{5... | collective-permute-start | bytes 417800 | tf_op jit(solution)/shard_map/ppermute | solution.py:338
  16.1 8.5 %collective-permute-start.2 = (f32[136,256]{1,0:T(8,128)S(1)}, f32[136,256]{1,0:T(8,128)S(1)}, u32[]{:S(2)}, u32[]{:S(2)}) collective-permute-start(f32[136,256]{1,0:T(8,128)S(1)} %get-tuple-element.50), channel_id=1, source_target_pairs={{0,12},{4,8},{8,4},{12,0},{16,28},{20,24},{24,20},{28,16},{1,13},{... | collective-permute-start | bytes 417800 | tf_op jit(solution)/shard_map/ppermute | solution.py:338
  16.9 9.3 %collective-permute-start.10 = (f32[128,256]{1,0:T(8,128)S(1)}, f32[128,256]{1,0:T(8,128)S(1)}, u32[]{:S(2)}, u32[]{:S(2)}) collective-permute-start(f32[128,256]{1,0:T(8,128)S(1)} %add_add_fusion.1), channel_id=1, source_target_pairs={{0,16},{4,20},{8,24},{12,28},{16,0},{20,4},{24,8},{28,12},{1,17},{... | collective-permute-start | bytes 393224 | tf_op jit(solution)/shard_map/ppermute | solution.py:338
  24.6 7.7 %collective-permute-start.3 = (f32[136,256]{1,0:T(8,128)S(1)}, f32[136,256]{1,0:T(8,128)S(1)}, u32[]{:S(2)}, u32[]{:S(2)}) collective-permute-start(f32[136,256]{1,0:T(8,128)S(1)} %add_add_fusion), channel_id=1, source_target_pairs={{0,16},{4,20},{8,24},{12,28},{16,0},{20,4},{24,8},{28,12},{1,17},{... | collective-permute-start | bytes 417800 | tf_op jit(solution)/shard_map/ppermute | solution.py:338
  26.3 8.5 %collective-permute-start.11 = (f32[128,256]{1,0:T(8,128)S(1)}, f32[128,256]{1,0:T(8,128)S(1)}, u32[]{:S(2)}, u32[]{:S(2)}) collective-permute-start(f32[128,256]{1,0:T(8,128)S(1)} %add.40.own), channel_id=1, source_target_pairs={{0,8},{4,12},{8,0},{12,4},{16,24},{20,28},{24,16},{28,20},{1,9},{5... | collective-permute-start | bytes 393224 | tf_op jit(solution)/shard_map/ppermute | solution.py:338
  30.7 9.6 %collective-permute-start.12 = (f32[128,256]{1,0:T(8,128)S(1)}, f32[128,256]{1,0:T(8,128)S(1)}, u32[]{:S(2)}, u32[]{:S(2)}) collective-permute-start(f32[128,256]{1,0:T(8,128)S(1)} %add.40.own), channel_id=1, source_target_pairs={{0,4},{4,0},{8,12},{12,8},{16,20},{20,16},{24,28},{28,24},{1,5},{5... | collective-permute-start | bytes 393224 | tf_op jit(solution)/shard_map/ppermute | solution.py:338
  31.2 9.1 %collective-permute-start.13 = (f32[128,256]{1,0:T(8,128)S(1)}, f32[128,256]{1,0:T(8,128)S(1)}, u32[]{:S(2)}, u32[]{:S(2)}) collective-permute-start(f32[128,256]{1,0:T(8,128)S(1)} %add.40.own), channel_id=1, source_target_pairs={{0,12},{4,8},{8,4},{12,0},{16,28},{20,24},{24,20},{28,16},{1,13},{... | collective-permute-start | bytes 393224 | tf_op jit(solution)/shard_map/ppermute | solution.py:338
  32.3 8.7 %collective-permute-start.4 = (f32[128,256]{1,0:T(8,128)S(1)}, f32[128,256]{1,0:T(8,128)S(1)}, u32[]{:S(2)}, u32[]{:S(2)}) collective-permute-start(f32[128,256]{1,0:T(8,128)S(1)} %slice.28.own), channel_id=1, source_target_pairs={{0,8},{4,12},{8,0},{12,4},{16,24},{20,28},{24,16},{28,20},{1,9},{5... | collective-permute-start | bytes 393224 | tf_op jit(solution)/shard_map/ppermute | solution.py:338
  34.4 8.7 %collective-permute-start.5 = (f32[128,256]{1,0:T(8,128)S(1)}, f32[128,256]{1,0:T(8,128)S(1)}, u32[]{:S(2)}, u32[]{:S(2)}) collective-permute-start(f32[128,256]{1,0:T(8,128)S(1)} %slice.28.own), channel_id=1, source_target_pairs={{0,4},{4,0},{8,12},{12,8},{16,20},{20,16},{24,28},{28,24},{1,5},{5... | collective-permute-start | bytes 393224 | tf_op jit(solution)/shard_map/ppermute | solution.py:338
  34.8 8.3 %collective-permute-start.6 = (f32[128,256]{1,0:T(8,128)S(1)}, f32[128,256]{1,0:T(8,128)S(1)}, u32[]{:S(2)}, u32[]{:S(2)}) collective-permute-start(f32[128,256]{1,0:T(8,128)S(1)} %slice.28.own), channel_id=1, source_target_pairs={{0,12},{4,8},{8,4},{12,0},{16,28},{20,24},{24,20},{28,16},{1,13},{... | collective-permute-start | bytes 393224 | tf_op jit(solution)/shard_map/ppermute | solution.py:338
  43.8 7.6 %collective-permute-start.14 = (f32[1,128]{1,0:T(1,128)S(1)}, f32[1,128]{1,0:T(1,128)S(1)}, u32[]{:S(2)}, u32[]{:S(2)}) collective-permute-start(f32[1,128]{1,0:T(1,128)S(1)} %get-tuple-element.68), channel_id=1, source_target_pairs={{0,1},{1,0},{2,3},{3,2},{4,5},{5,4},{6,7},{7,6},{8,9},{9,8},{10,11... | collective-permute-start | bytes 1544 | tf_op jit(solution)/shard_map/ppermute | solution.py:338
  43.9 7.6 %collective-permute-start.15 = (f32[1,128]{1,0:T(1,128)S(1)}, f32[1,128]{1,0:T(1,128)S(1)}, u32[]{:S(2)}, u32[]{:S(2)}) collective-permute-start(f32[1,128]{1,0:T(1,128)S(1)} %get-tuple-element.68), channel_id=1, source_target_pairs={{0,2},{1,3},{2,0},{3,1},{4,6},{5,7},{6,4},{7,5},{8,10},{9,11},{10,... | collective-permute-start | bytes 1544 | tf_op jit(solution)/shard_map/ppermute | solution.py:338
  45.5 6.0 %collective-permute-start.16 = (f32[1,128]{1,0:T(1,128)S(1)}, f32[1,128]{1,0:T(1,128)S(1)}, u32[]{:S(2)}, u32[]{:S(2)}) collective-permute-start(f32[1,128]{1,0:T(1,128)S(1)} %get-tuple-element.68), channel_id=1, source_target_pairs={{0,3},{1,2},{2,1},{3,0},{4,7},{5,6},{6,5},{7,4},{8,11},{9,10},{10,... | collective-permute-start | bytes 1544 | tf_op jit(solution)/shard_map/ppermute | solution.py:338

commit v4 on v3

--- a/solution.py
+++ b/solution.py
@@ -244,7 +244,7 @@
             out[rows:] = tail
 
 
-def apply_tables_kernel(miller, positions, form, coupling, species, sizes, hi_ref, lo_ref, dense_hi, dense_lo, table, ctable):
+def apply_tables_kernel(miller, positions, form, coupling, species, sizes, hi_ref, lo_ref, dense_hi, dense_lo, kinetic, table, ctable):
     planes = miller.shape[1]
     nspec = form.shape[1]
     fill_rows(table, form)
@@ -276,6 +276,9 @@
     hi, lo = split(jnp.where(owner_col == owner_row, dense, 0.0))
     dense_hi[...] = hi
     dense_lo[...] = lo
+    unit = jnp.where(iota((8, kinetic.shape[1]), 0) == 0, 1.0, 0.0).astype(BF16)
+    line = jnp.broadcast_to(squares(m), (8, planes)).astype(BF16)
+    kinetic[...] = (0.5 * KINETIC_SCALE) * dot(line, unit, over)
 
 
 def stats_kernel(order, q, own, near, far, across, sums, occupation, dense_hi, dense_lo, *refs):
@@ -305,13 +308,9 @@
         ref[PROJ:, half:] = m[:, 0:half]
 
 
-def apply_kernel(q, rhs_hi, rhs_lo, waves, miller, hi_ref, lo_ref, level, *refs):
-    planes = miller.shape[1]
-    half = level.shape[1]
+def apply_kernel(q, rhs_hi, rhs_lo, waves, kinetic, hi_ref, lo_ref, level, *refs):
+    planes, half = kinetic.shape
     bands = slice(q * half, (q + 1) * half)
-    unit = jnp.where(iota((8, half), 0) == 0, 1.0, 0.0).astype(BF16)
-    line = jnp.broadcast_to(squares(miller[...].astype(F32)), (8, planes)).astype(BF16)
-    shifted = (0.5 * KINETIC_SCALE) * dot(line, unit, ((0,), (0,))) - level[...]
     copies = []
     if q == 0:
         residual, staged, sems = refs
@@ -326,7 +325,7 @@
         part = slice(r * step, (r + 1) * step)
         applied = dot(hi_ref[part], rhs_hi[...]) + dot(hi_ref[part], rhs_lo[...]) + dot(lo_ref[part], rhs_hi[...])
         for n in range(2):
-            staged[n, r] = shifted[part] * waves[n, part, bands] + applied[:, n * half : (n + 1) * half]
+            staged[n, r] = (kinetic[part] - level[...]) * waves[n, part, bands] + applied[:, n * half : (n + 1) * half]
             target = residual.at[n, pl.ds(r * step, step), pl.ds(q * half, half)]
             copies.append(pltpu.make_async_copy(staged.at[n, r], target, sems.at[2 * r + n]))
             copies[-1].start()
@@ -402,7 +401,7 @@
     tables = pl.pallas_call(
         apply_tables_kernel,
         name="apply_tables",
-        out_shape=[shape((planes, 2 * PROJ), BF16)] * 2 + [shape((PROJ, PROJ), BF16)] * 2,
+        out_shape=[shape((planes, 2 * PROJ), BF16)] * 2 + [shape((PROJ, PROJ), BF16)] * 2 + [shape((planes, half), F32)],
         scratch_shapes=[pltpu.VMEM((depth, planes), F32), pltpu.VMEM((depth, LANES), F32)],
         compiler_params=params,
     )(miller, positions, form, coupling, species, sizes)
@@ -432,7 +431,7 @@
         share = [total]
         if q == 1:
             energy = tree([total] + [swap(total, "band", band, d) for d in range(1, band)])[0, 0]
-        operands = [rhs_hi, rhs_lo, waves, miller, tables[0], tables[1], level, *levels, *residual]
+        operands = [rhs_hi, rhs_lo, waves, tables[4], tables[0], tables[1], level, *levels, *residual]
         levels.append(level)
         residual = pl.pallas_call(
             functools.partial(apply_kernel, q),

time: 52.1 us -> 50.9 us (0.977)
  waiting for transfers between devices: 12.2 us -> 11.2 us
    ppermute x17, waiting for transfers between devices: 12.2 us -> 11.2 us  [swap(): return lax.ppermute(x, axis, [(i, i ^ mask) for i in range(size)])]
  transfers between devices with their start and end apart: 17 -> 17, of which waited for: 6 -> 7; matrix products, arithmetic and copies ran while one was open for 0% -> 0% of each run, Pallas kernels for 20% -> 24%
where the time goes in v4:
time: 50.9 us; the launch traced here: 50.7 us
  starting transfers between devices  21.6 us (42%)
  Pallas kernels  16.4 us (32%)
  waiting for transfers between devices  11.2 us (22%)
  between operations  0.82 us (2%)
  other arithmetic  0.63 us (1%)
    ppermute x17, starting transfers between devices, swap(): return lax.ppermute(x, axis, [(i, i ^ mask) for i in range(size)])  21.6 us
    ppermute x17, waiting for transfers between devices, swap(): return lax.ppermute(x, axis, [(i, i ^ mask) for i in range(size)])  11.2 us
    pallas_call x2, Pallas kernels, on_device(): pl.pallas_call(functools.partial(apply_kernel, q), in_specs=[vmem] * (7 +...  5.58 us
    pallas_call x1, Pallas kernels, on_device(): pl.pallas_call(functools.partial(project_send, order), name='project_send...  3.4 us
    pallas_call x1, Pallas kernels, on_device(): pl.pallas_call(apply_tables_kernel, name='apply_tables', out_shape=[shape...  2.28 us
    pallas_call x1, Pallas kernels, on_device(): pl.pallas_call(functools.partial(project_second, order), name='project_se...  2.17 us
    pallas_call x1, Pallas kernels, on_device(): pl.pallas_call(functools.partial(project_keep, order), name='project_keep...  1.51 us
    pallas_call x2, Pallas kernels, on_device(): pl.pallas_call(functools.partial(stats_kernel, order, q), out_shape=[shap...  1.48 us
  transfers between devices with their start and end apart: 17, of which 7 were waited for; matrix products, arithmetic and copies ran while one was open for 0% of the time, Pallas kernels for 24%

profile of v4, /device:TPU:0, one launch (start us, length us, event | category | flops | bytes accessed | tf_op | source)
XLA Modules:
  0.0 50.7 jit_solution(9734039146127209899)
XLA Ops:
  0.6 3.4 %project_send.1 = (f32[128,256]{1,0:T(8,128)S(1)}, f32[128,256]{1,0:T(8,128)S(1)}, bf16[256,2048]{1,0:T(8,128)(2,1)S(1)}, bf16[256,2048]{1,0:T(8,128)(2,1)S(1)},...) custom-call(f32[2,1024,256]{2,1,0:T(8,128)} %waves.5, ...), custom_call_target="tpu_custom_call" | custom-call | tf_op jit(solution)/shard_map/project_send/pallas_call | solution.py:368
  4.0 0.0 copy-start
  4.1 0.0 copy-start.2
  4.1 3.0 %collective-permute-start.8 = (f32[128,256]{1,0:T(8,128)S(1)}, f32[128,256]{1,0:T(8,128)S(1)}, u32[]{:S(2)}, u32[]{:S(2)}) collective-permute-start(f32[128,256]{1,0:T(8,128)S(1)} %get-tuple-element.56), channel_id=1, source_target_pairs={{0,4},{4,0},{8,12},{12,8},{16,20},{20,16},{24,28},{28,24},{1,5},{5... | collective-permute-start | bytes 393224 | tf_op jit(solution)/shard_map/ppermute | solution.py:337
  7.1 1.6 %collective-permute-start.9 = (f32[128,256]{1,0:T(8,128)S(1)}, f32[128,256]{1,0:T(8,128)S(1)}, u32[]{:S(2)}, u32[]{:S(2)}) collective-permute-start(f32[128,256]{1,0:T(8,128)S(1)} %get-tuple-element.57), channel_id=1, source_target_pairs={{0,12},{4,8},{8,4},{12,0},{16,28},{20,24},{24,20},{28,16},{1,13},{... | collective-permute-start | bytes 393224 | tf_op jit(solution)/shard_map/ppermute | solution.py:337
  8.7 1.5 %project_keep.1 = (f32[128,256]{1,0:T(8,128)S(1)}, f32[128,256]{1,0:T(8,128)S(1)}, bf16[256,2048]{1,0:T(8,128)(2,1)S(1)}, bf16[256,2048]{1,0:T(8,128)(2,1)S(1)}) custom-call(bf16[2048,256]{1,0:T(8,128)(2,1)S(1)} %get-tuple-element.39.rhs_hi, bf16[2048,256]{1,0:T(8,128)(2,1)S(1)} %get-tuple-element.40.rhs_lo, bf16[128,1024]{1,0:T(8,128)(2,1)S(1)} %get-tuple-element.41.cosine, ...), custom_call_target="tpu_custom_call" | custom-call | tf_op jit(solution)/shard_map/project_keep/pallas_call | solution.py:387
  10.2 0.1 collective-permute-start.7
  10.3 0.0 copy-done
  10.3 0.0 copy-done.2
  10.3 0.0 copy-start.1
  10.3 0.0 copy-start.3
  10.3 0.0 copy-start.4
  10.3 0.0 copy-start.5
  10.3 0.0 copy-start.6
  10.3 2.2 %project_second.1 = (f32[136,256]{1,0:T(8,128)S(1)}, f32[136,256]{1,0:T(8,128)S(1)}, f32[136,256]{1,0:T(8,128)S(1)}, f32[136,256]{1,0:T(8,128)S(1)}) custom-call(f32[2,1024,256]{2,1,0:T(8,128)S(1)} %copy-done, s32[3,1024]{1,0:T(4,128)S(1)} %copy-done.2, bf16[256,2048]{1,0:T(8,128)(2,1)S(1)} %get-tuple-element.37.hi_ref, ...), custom_call_target="tpu_custom_call" | custom-call | tf_op jit(solution)/shard_map/project_second/pallas_call | solution.py:394
  12.5 0.0 copy-start.7
  12.5 2.1 %collective-permute-start = (f32[136,256]{1,0:T(8,128)S(1)}, f32[136,256]{1,0:T(8,128)S(1)}, u32[]{:S(2)}, u32[]{:S(2)}) collective-permute-start(f32[136,256]{1,0:T(8,128)S(1)} %get-tuple-element.49), channel_id=1, source_target_pairs={{0,8},{4,12},{8,0},{12,4},{16,24},{20,28},{24,16},{28,20},{1,9},{5... | collective-permute-start | bytes 417800 | tf_op jit(solution)/shard_map/ppermute | solution.py:337
  14.6 1.5 %collective-permute-start.1 = (f32[136,256]{1,0:T(8,128)S(1)}, f32[136,256]{1,0:T(8,128)S(1)}, u32[]{:S(2)}, u32[]{:S(2)}) collective-permute-start(f32[136,256]{1,0:T(8,128)S(1)} %get-tuple-element.50), channel_id=1, source_target_pairs={{0,4},{4,0},{8,12},{12,8},{16,20},{20,16},{24,28},{28,24},{1,5},{5... | collective-permute-start | bytes 417800 | tf_op jit(solution)/shard_map/ppermute | solution.py:337
  16.1 0.0 collective-permute-done.8
  16.1 0.1 collective-permute-start.2
  16.2 0.0 collective-permute-done.9
  16.2 0.0 collective-permute-done.7
  16.2 3.0 %collective-permute-start.10 = (f32[128,256]{1,0:T(8,128)S(1)}, f32[128,256]{1,0:T(8,128)S(1)}, u32[]{:S(2)}, u32[]{:S(2)}) collective-permute-start(f32[128,256]{1,0:T(8,128)S(1)} %add_add_fusion.1), channel_id=1, source_target_pairs={{0,16},{4,20},{8,24},{12,28},{16,0},{20,4},{24,8},{28,12},{1,17},{... | collective-permute-start | bytes 393224 | tf_op jit(solution)/shard_map/ppermute | solution.py:337
  19.2 1.4 %collective-permute-done = f32[136,256]{1,0:T(8,128)S(1)} collective-permute-done((f32[136,256]{1,0:T(8,128)S(1)}, f32[136,256]{1,0:T(8,128)S(1)}, u32[]{:S(2)}, u32[]{:S(2)}) %collective-permute-start) | collective-permute-done | bytes 139296 | tf_op jit(solution)/shard_map/ppermute | solution.py:337
  20.6 0.0 collective-permute-done.1
  20.6 4.4 %collective-permute-done.2 = f32[136,256]{1,0:T(8,128)S(1)} collective-permute-done((f32[136,256]{1,0:T(8,128)S(1)}, f32[136,256]{1,0:T(8,128)S(1)}, u32[]{:S(2)}, u32[]{:S(2)}) %collective-permute-start.2) | collective-permute-done | bytes 139296 | tf_op jit(solution)/shard_map/ppermute | solution.py:337
  24.9 1.3 %collective-permute-start.3 = (f32[136,256]{1,0:T(8,128)S(1)}, f32[136,256]{1,0:T(8,128)S(1)}, u32[]{:S(2)}, u32[]{:S(2)}) collective-permute-start(f32[136,256]{1,0:T(8,128)S(1)} %add_add_fusion), channel_id=1, source_target_pairs={{0,16},{4,20},{8,24},{12,28},{16,0},{20,4},{24,8},{28,12},{1,17},{... | collective-permute-start | bytes 417800 | tf_op jit(solution)/shard_map/ppermute | solution.py:337
  26.2 0.0 collective-permute-done.10
  26.2 2.5 %collective-permute-start.13 = (f32[128,256]{1,0:T(8,128)S(1)}, f32[128,256]{1,0:T(8,128)S(1)}, u32[]{:S(2)}, u32[]{:S(2)}) collective-permute-start(f32[128,256]{1,0:T(8,128)S(1)} %add.40.own), channel_id=1, source_target_pairs={{0,12},{4,8},{8,4},{12,0},{16,28},{20,24},{24,20},{28,16},{1,13},{... | collective-permute-start | bytes 393224 | tf_op jit(solution)/shard_map/ppermute | solution.py:337
  28.7 0.0 copy-done.1
  28.7 0.0 copy-done.3
  28.7 0.0 copy-done.4
  28.7 0.0 copy-done.5
  28.7 0.0 copy-done.6
  28.7 2.3 %apply_tables.1 = (bf16[1024,1024]{1,0:T(8,128)(2,1)S(1)}, bf16[1024,1024]{1,0:T(8,128)(2,1)S(1)}, bf16[512,512]{1,0:T(8,128)(2,1)S(1)}, bf16[512,512]{1,0:T(8,128)(2,1)S(1)}, f32[1024,128]{1,0:T(8,128)S(1)}) custom-call(s32[3,1024]{1,0:T(4,128)S(1)} %copy-done.2, f32[3,64]{1,0:T(4,128)S(1)} %bitcast.16, f32[18,4,1024]{2,1,0:T(4,128)S(1)} %bitcast.13, ...), custom_call_target="tpu_custom_call" | custom-call | tf_op jit(solution)/shard_map/apply_tables/pallas_call | solution.py:401
  31.0 1.1 %collective-permute-start.12 = (f32[128,256]{1,0:T(8,128)S(1)}, f32[128,256]{1,0:T(8,128)S(1)}, u32[]{:S(2)}, u32[]{:S(2)}) collective-permute-start(f32[128,256]{1,0:T(8,128)S(1)} %add.40.own), channel_id=1, source_target_pairs={{0,4},{4,0},{8,12},{12,8},{16,20},{20,16},{24,28},{28,24},{1,5},{5... | collective-permute-start | bytes 393224 | tf_op jit(solution)/shard_map/ppermute | solution.py:337
  32.1 0.1 collective-permute-start.11
  32.2 0.1 collective-permute-done.3
  32.3 2.3 %collective-permute-start.6 = (f32[128,256]{1,0:T(8,128)S(1)}, f32[128,256]{1,0:T(8,128)S(1)}, u32[]{:S(2)}, u32[]{:S(2)}) collective-permute-start(f32[128,256]{1,0:T(8,128)S(1)} %slice.28.own), channel_id=1, source_target_pairs={{0,12},{4,8},{8,4},{12,0},{16,28},{20,24},{24,20},{28,16},{1,13},{... | collective-permute-start | bytes 393224 | tf_op jit(solution)/shard_map/ppermute | solution.py:337
  34.7 1.0 %collective-permute-start.5 = (f32[128,256]{1,0:T(8,128)S(1)}, f32[128,256]{1,0:T(8,128)S(1)}, u32[]{:S(2)}, u32[]{:S(2)}) collective-permute-start(f32[128,256]{1,0:T(8,128)S(1)} %slice.28.own), channel_id=1, source_target_pairs={{0,4},{4,0},{8,12},{12,8},{16,20},{20,16},{24,28},{28,24},{1,5},{5... | collective-permute-start | bytes 393224 | tf_op jit(solution)/shard_map/ppermute | solution.py:337
  35.7 0.0 collective-permute-done.13.across
  35.7 0.2 collective-permute-start.4
  35.9 0.0 copy-done.7
  35.9 2.5 %collective-permute-done.12.far = f32[128,256]{1,0:T(8,128)S(1)} collective-permute-done((f32[128,256]{1,0:T(8,128)S(1)}, f32[128,256]{1,0:T(8,128)S(1)}, u32[]{:S(2)}, u32[]{:S(2)}) %collective-permute-start.12) | collective-permute-done | bytes 131104 | tf_op jit(solution)/shard_map/ppermute | solution.py:337
  38.4 0.0 collective-permute-done.11.near
  38.5 0.7 %shard_map.103 = (bf16[1024,256]{1,0:T(8,128)(2,1)S(1)}, bf16[1024,256]{1,0:T(8,128)(2,1)S(1)}, f32[1,128]{1,0:T(1,128)S(1)}, f32[1,128]{1,0:T(1,128)S(1)}) custom-call(f32[128,256]{1,0:T(8,128)S(1)} %add.40.own, f32[128,256]{1,0:T(8,128)S(1)} %collective-permute-done.11.near, f32[128,256]{1,0:T(8,128)S(1)} %collective-permute-done.12.far, ...), custom_call_target="tpu_custom_call" | custom-call | tf_op jit(solution)/shard_map/pallas_call | solution.py:425
  39.2 1.7 %collective-permute-done.6.across = f32[128,256]{1,0:T(8,128)S(1)} collective-permute-done((f32[128,256]{1,0:T(8,128)S(1)}, f32[128,256]{1,0:T(8,128)S(1)}, u32[]{:S(2)}, u32[]{:S(2)}) %collective-permute-start.6) | collective-permute-done | bytes 131104 | tf_op jit(solution)/shard_map/ppermute | solution.py:337
  40.9 0.4 collective-permute-done.5.far
  41.3 0.7 %collective-permute-done.4.near = f32[128,256]{1,0:T(8,128)S(1)} collective-permute-done((f32[128,256]{1,0:T(8,128)S(1)}, f32[128,256]{1,0:T(8,128)S(1)}, u32[]{:S(2)}, u32[]{:S(2)}) %collective-permute-start.4) | collective-permute-done | bytes 131104 | tf_op jit(solution)/shard_map/ppermute | solution.py:337
  42.0 0.7 %shard_map.104 = (bf16[1024,256]{1,0:T(8,128)(2,1)S(1)}, bf16[1024,256]{1,0:T(8,128)(2,1)S(1)}, f32[1,128]{1,0:T(1,128)S(1)}, f32[1,128]{1,0:T(1,128)S(1)}) custom-call(f32[128,256]{1,0:T(8,128)S(1)} %slice.28.own, f32[128,256]{1,0:T(8,128)S(1)} %collective-permute-done.4.near, f32[128,256]{1,0:T(8,128)S(1)} %collective-permute-done.5.far, ...), custom_call_target="tpu_custom_call" | custom-call | tf_op jit(solution)/shard_map/pallas_call | solution.py:425
  42.7 0.0 collective-permute-start.16
  42.7 1.6 %collective-permute-start.15 = (f32[1,128]{1,0:T(1,128)S(1)}, f32[1,128]{1,0:T(1,128)S(1)}, u32[]{:S(2)}, u32[]{:S(2)}) collective-permute-start(f32[1,128]{1,0:T(1,128)S(1)} %get-tuple-element.70), channel_id=1, source_target_pairs={{0,2},{1,3},{2,0},{3,1},{4,6},{5,7},{6,4},{7,5},{8,10},{9,11},{10,... | collective-permute-start | bytes 1544 | tf_op jit(solution)/shard_map/ppermute | solution.py:337
  44.3 0.3 collective-permute-start.14
  44.6 2.8 %shard_map.105.refs_1_ = f32[2,1024,256]{2,1,0:T(8,128)} custom-call(bf16[1024,256]{1,0:T(8,128)(2,1)S(1)} %get-tuple-element.66.rhs_hi, bf16[1024,256]{1,0:T(8,128)(2,1)S(1)} %get-tuple-element.67.rhs_lo, f32[2,1024,256]{2,1,0:T(8,128)S(1)} %copy-done, f32[1024,128]{1,0:T(8,128)S(1)} %get-tuple-element.61.kinetic, ...), custom_call_target="tpu_custom_call" | custom-call | tf_op jit(solution)/shard_map/pallas_call | solution.py:436
  47.3 2.8 %shard_map.106 = (f32[2,1024,256]{2,1,0:T(8,128)}, f32[2,128]{1,0:T(2,128)}) custom-call(bf16[1024,256]{1,0:T(8,128)(2,1)S(1)} %get-tuple-element.59.rhs_hi, bf16[1024,256]{1,0:T(8,128)(2,1)S(1)} %get-tuple-element.60.rhs_lo, f32[2,1024,256]{2,1,0:T(8,128)S(1)} %copy-done, ...), custom_call_target="tpu_custom_call", output_to_operand_aliasing={{0}: (8, {})} | custom-call | tf_op jit(solution)/shard_map/pallas_call | solution.py:436
  50.2 0.0 collective-permute-done.16
  50.2 0.0 collective-permute-done.15
  50.2 0.0 collective-permute-done.14
  50.2 0.5 %add_add_fusion.2 = f32[1,128]{1,0:T(1,128)} fusion(f32[1,128]{1,0:T(1,128)S(1)} %collective-permute-done.15, f32[1,128]{1,0:T(1,128)S(1)} %collective-permute-done.16, f32[1,128]{1,0:T(1,128)S(1)} %get-tuple-element.70, f32[1,128]{1,0:T(1,128)S(1)} %collective-permute-done.14), kind=kLoop, calls=%fused_computation.2 | loop fusion | flops 384 | bytes 2560 | tf_op jit(solution)/shard_map/add | solution.py:342
  (7 shorter events, 0.1 us)
Async XLA Ops:
  4.0 6.2 %copy-start = (f32[2,1024,256]{2,1,0:T(8,128)S(1)}, f32[2,1024,256]{2,1,0:T(8,128)}, u32[]{:S(2)}) copy-start(f32[2,1024,256]{2,1,0:T(8,128)} %waves.5) | copy-start | bytes 6291460
  4.1 6.2 %copy-start.2 = (s32[3,1024]{1,0:T(4,128)S(1)}, s32[3,1024]{1,0:T(4,128)}, u32[]{:S(2)}) copy-start(s32[3,1024]{1,0:T(4,128)} %miller.3) | copy-start | bytes 36868
  4.1 12.0 %collective-permute-start.8 = (f32[128,256]{1,0:T(8,128)S(1)}, f32[128,256]{1,0:T(8,128)S(1)}, u32[]{:S(2)}, u32[]{:S(2)}) collective-permute-start(f32[128,256]{1,0:T(8,128)S(1)} %get-tuple-element.56), channel_id=1, source_target_pairs={{0,4},{4,0},{8,12},{12,8},{16,20},{20,16},{24,28},{28,24},{1,5},{5... | collective-permute-start | bytes 393224 | tf_op jit(solution)/shard_map/ppermute | solution.py:337
  7.1 9.1 %collective-permute-start.9 = (f32[128,256]{1,0:T(8,128)S(1)}, f32[128,256]{1,0:T(8,128)S(1)}, u32[]{:S(2)}, u32[]{:S(2)}) collective-permute-start(f32[128,256]{1,0:T(8,128)S(1)} %get-tuple-element.57), channel_id=1, source_target_pairs={{0,12},{4,8},{8,4},{12,0},{16,28},{20,24},{24,20},{28,16},{1,13},{... | collective-permute-start | bytes 393224 | tf_op jit(solution)/shard_map/ppermute | solution.py:337
  10.2 6.0 %collective-permute-start.7 = (f32[128,256]{1,0:T(8,128)S(1)}, f32[128,256]{1,0:T(8,128)S(1)}, u32[]{:S(2)}, u32[]{:S(2)}) collective-permute-start(f32[128,256]{1,0:T(8,128)S(1)} %get-tuple-element.55), channel_id=1, source_target_pairs={{0,8},{4,12},{8,0},{12,4},{16,24},{20,28},{24,16},{28,20},{1,9},{5... | collective-permute-start | bytes 393224 | tf_op jit(solution)/shard_map/ppermute | solution.py:337
  10.3 18.4 %copy-start.1 = (f32[4,18,1024]{2,0,1:T(4,128)S(1)}, f32[4,18,1024]{2,0,1:T(4,128)}, u32[]{:S(2)}) copy-start(f32[4,18,1024]{2,0,1:T(4,128)} %param.11) | copy-start | bytes 884740
  10.3 18.4 %copy-start.3 = (f32[4,18,18]{2,0,1:T(4,128)S(1)}, f32[4,18,18]{2,0,1:T(4,128)}, u32[]{:S(2)}) copy-start(f32[4,18,18]{2,0,1:T(4,128)} %param.12) | copy-start | bytes 15556
  10.3 18.4 %copy-start.4 = (f32[64,3]{0,1:T(4,128)S(1)}, f32[64,3]{0,1:T(4,128)}, u32[]{:S(2)}) copy-start(f32[64,3]{0,1:T(4,128)} %param.10) | copy-start | bytes 2308
  10.3 18.4 %copy-start.5 = (s32[64]{0:T(128)S(1)}, s32[64]{0:T(128)}, u32[]{:S(2)}) copy-start(s32[64]{0:T(128)} %param.13) | copy-start | bytes 772
  10.3 18.4 %copy-start.6 = (s32[64]{0:T(128)S(1)}, s32[64]{0:T(128)}, u32[]{:S(2)}) copy-start(s32[64]{0:T(128)} %param.14) | copy-start | bytes 772
  12.5 23.4 %copy-start.7 = (f32[256]{0:T(256)S(1)}, f32[256]{0:T(256)}, u32[]{:S(2)}) copy-start(f32[256]{0:T(256)} %param.15) | copy-start | bytes 3076
  12.5 8.0 %collective-permute-start = (f32[136,256]{1,0:T(8,128)S(1)}, f32[136,256]{1,0:T(8,128)S(1)}, u32[]{:S(2)}, u32[]{:S(2)}) collective-permute-start(f32[136,256]{1,0:T(8,128)S(1)} %get-tuple-element.49), channel_id=1, source_target_pairs={{0,8},{4,12},{8,0},{12,4},{16,24},{20,28},{24,16},{28,20},{1,9},{5... | collective-permute-start | bytes 417800 | tf_op jit(solution)/shard_map/ppermute | solution.py:337
  14.6 5.9 %collective-permute-start.1 = (f32[136,256]{1,0:T(8,128)S(1)}, f32[136,256]{1,0:T(8,128)S(1)}, u32[]{:S(2)}, u32[]{:S(2)}) collective-permute-start(f32[136,256]{1,0:T(8,128)S(1)} %get-tuple-element.50), channel_id=1, source_target_pairs={{0,4},{4,0},{8,12},{12,8},{16,20},{20,16},{24,28},{28,24},{1,5},{5... | collective-permute-start | bytes 417800 | tf_op jit(solution)/shard_map/ppermute | solution.py:337
  16.1 8.8 %collective-permute-start.2 = (f32[136,256]{1,0:T(8,128)S(1)}, f32[136,256]{1,0:T(8,128)S(1)}, u32[]{:S(2)}, u32[]{:S(2)}) collective-permute-start(f32[136,256]{1,0:T(8,128)S(1)} %get-tuple-element.51), channel_id=1, source_target_pairs={{0,12},{4,8},{8,4},{12,0},{16,28},{20,24},{24,20},{28,16},{1,13},{... | collective-permute-start | bytes 417800 | tf_op jit(solution)/shard_map/ppermute | solution.py:337
  16.2 10.0 %collective-permute-start.10 = (f32[128,256]{1,0:T(8,128)S(1)}, f32[128,256]{1,0:T(8,128)S(1)}, u32[]{:S(2)}, u32[]{:S(2)}) collective-permute-start(f32[128,256]{1,0:T(8,128)S(1)} %add_add_fusion.1), channel_id=1, source_target_pairs={{0,16},{4,20},{8,24},{12,28},{16,0},{20,4},{24,8},{28,12},{1,17},{... | collective-permute-start | bytes 393224 | tf_op jit(solution)/shard_map/ppermute | solution.py:337
  24.9 7.4 %collective-permute-start.3 = (f32[136,256]{1,0:T(8,128)S(1)}, f32[136,256]{1,0:T(8,128)S(1)}, u32[]{:S(2)}, u32[]{:S(2)}) collective-permute-start(f32[136,256]{1,0:T(8,128)S(1)} %add_add_fusion), channel_id=1, source_target_pairs={{0,16},{4,20},{8,24},{12,28},{16,0},{20,4},{24,8},{28,12},{1,17},{... | collective-permute-start | bytes 417800 | tf_op jit(solution)/shard_map/ppermute | solution.py:337
  26.2 9.5 %collective-permute-start.13 = (f32[128,256]{1,0:T(8,128)S(1)}, f32[128,256]{1,0:T(8,128)S(1)}, u32[]{:S(2)}, u32[]{:S(2)}) collective-permute-start(f32[128,256]{1,0:T(8,128)S(1)} %add.40.own), channel_id=1, source_target_pairs={{0,12},{4,8},{8,4},{12,0},{16,28},{20,24},{24,20},{28,16},{1,13},{... | collective-permute-start | bytes 393224 | tf_op jit(solution)/shard_map/ppermute | solution.py:337
  31.0 7.4 %collective-permute-start.12 = (f32[128,256]{1,0:T(8,128)S(1)}, f32[128,256]{1,0:T(8,128)S(1)}, u32[]{:S(2)}, u32[]{:S(2)}) collective-permute-start(f32[128,256]{1,0:T(8,128)S(1)} %add.40.own), channel_id=1, source_target_pairs={{0,4},{4,0},{8,12},{12,8},{16,20},{20,16},{24,28},{28,24},{1,5},{5... | collective-permute-start | bytes 393224 | tf_op jit(solution)/shard_map/ppermute | solution.py:337
  32.1 6.4 %collective-permute-start.11 = (f32[128,256]{1,0:T(8,128)S(1)}, f32[128,256]{1,0:T(8,128)S(1)}, u32[]{:S(2)}, u32[]{:S(2)}) collective-permute-start(f32[128,256]{1,0:T(8,128)S(1)} %add.40.own), channel_id=1, source_target_pairs={{0,8},{4,12},{8,0},{12,4},{16,24},{20,28},{24,16},{28,20},{1,9},{5... | collective-permute-start | bytes 393224 | tf_op jit(solution)/shard_map/ppermute | solution.py:337
  32.3 8.6 %collective-permute-start.6 = (f32[128,256]{1,0:T(8,128)S(1)}, f32[128,256]{1,0:T(8,128)S(1)}, u32[]{:S(2)}, u32[]{:S(2)}) collective-permute-start(f32[128,256]{1,0:T(8,128)S(1)} %slice.28.own), channel_id=1, source_target_pairs={{0,12},{4,8},{8,4},{12,0},{16,28},{20,24},{24,20},{28,16},{1,13},{... | collective-permute-start | bytes 393224 | tf_op jit(solution)/shard_map/ppermute | solution.py:337
  34.7 6.6 %collective-permute-start.5 = (f32[128,256]{1,0:T(8,128)S(1)}, f32[128,256]{1,0:T(8,128)S(1)}, u32[]{:S(2)}, u32[]{:S(2)}) collective-permute-start(f32[128,256]{1,0:T(8,128)S(1)} %slice.28.own), channel_id=1, source_target_pairs={{0,4},{4,0},{8,12},{12,8},{16,20},{20,16},{24,28},{28,24},{1,5},{5... | collective-permute-start | bytes 393224 | tf_op jit(solution)/shard_map/ppermute | solution.py:337
  35.7 6.2 %collective-permute-start.4 = (f32[128,256]{1,0:T(8,128)S(1)}, f32[128,256]{1,0:T(8,128)S(1)}, u32[]{:S(2)}, u32[]{:S(2)}) collective-permute-start(f32[128,256]{1,0:T(8,128)S(1)} %slice.28.own), channel_id=1, source_target_pairs={{0,8},{4,12},{8,0},{12,4},{16,24},{20,28},{24,16},{28,20},{1,9},{5... | collective-permute-start | bytes 393224 | tf_op jit(solution)/shard_map/ppermute | solution.py:337
  42.7 7.5 %collective-permute-start.16 = (f32[1,128]{1,0:T(1,128)S(1)}, f32[1,128]{1,0:T(1,128)S(1)}, u32[]{:S(2)}, u32[]{:S(2)}) collective-permute-start(f32[1,128]{1,0:T(1,128)S(1)} %get-tuple-element.70), channel_id=1, source_target_pairs={{0,3},{1,2},{2,1},{3,0},{4,7},{5,6},{6,5},{7,4},{8,11},{9,10},{10,... | collective-permute-start | bytes 1544 | tf_op jit(solution)/shard_map/ppermute | solution.py:337
  42.7 7.5 %collective-permute-start.15 = (f32[1,128]{1,0:T(1,128)S(1)}, f32[1,128]{1,0:T(1,128)S(1)}, u32[]{:S(2)}, u32[]{:S(2)}) collective-permute-start(f32[1,128]{1,0:T(1,128)S(1)} %get-tuple-element.70), channel_id=1, source_target_pairs={{0,2},{1,3},{2,0},{3,1},{4,6},{5,7},{6,4},{7,5},{8,10},{9,11},{10,... | collective-permute-start | bytes 1544 | tf_op jit(solution)/shard_map/ppermute | solution.py:337
  44.3 5.9 %collective-permute-start.14 = (f32[1,128]{1,0:T(1,128)S(1)}, f32[1,128]{1,0:T(1,128)S(1)}, u32[]{:S(2)}, u32[]{:S(2)}) collective-permute-start(f32[1,128]{1,0:T(1,128)S(1)} %get-tuple-element.70), channel_id=1, source_target_pairs={{0,1},{1,0},{2,3},{3,2},{4,5},{5,4},{6,7},{7,6},{8,9},{9,8},{10,11... | collective-permute-start | bytes 1544 | tf_op jit(solution)/shard_map/ppermute | solution.py:337
